TPU v7x, 32 devices: a whole 2x2x4 slice. The times are simulated.
32 devices in a mesh: gx: 2 (over y), gy: 4 (over z), gz: 4 (over x, core).
Axes of the slice: x: 2, y: 2, z: 4, core: 2. Of those that a mesh axis runs over, the one named last changes fastest.
Arguments:
- fields: bfloat16 [384, 4, 16, 512], P(None, 'gx', 'gy', 'gz'), may hold values from -6 to 6
- trace_old: float32 [3, 32, 4, 16, 512], P(None, None, 'gx', 'gy', 'gz'), may hold values from -4 to 4
- face_load: float32 [3, 32, 4, 16, 512], P(None, None, 'gx', 'gy', 'gz'), may hold values from -6 to 6
- face_diag: float32 [3, 4, 16, 512], P(None, 'gx', 'gy', 'gz'), may hold values from 0.5 to 4
- fine_flag: int32 [4, 16, 512], P('gx', 'gy', 'gz'), may hold values from 0 to 1
- coeff: float32 [4, 16, 512], P('gx', 'gy', 'gz'), may hold values from 0.5 to 8
- volume_op: bfloat16 [384, 384], replicated, may hold values from -0.3125 to 0.3125
- lift_op: bfloat16 [384, 192], replicated, may hold values from -0.4375 to 0.4375
- schur_op: float32 [192, 192], replicated, may hold values from -8 to 8.5, as said below
Outputs:
- fields_new: bfloat16 [384, 4, 16, 512], P(None, 'gx', 'gy', 'gz')
- trace_new: float32 [3, 32, 4, 16, 512], P(None, None, 'gx', 'gy', 'gz')
Inputs may be any that keep to these rules, and one draw needn't show every extreme that they name: schur_op is symmetric and positive definite.
All inputs are finite; a program needn't handle non-finite values.
Results may differ from a plain program's by a relative error of at most 0.0013.
Values sent between devices are 32-bit elements; how exact they have to be, the bound alone decides.
No kernel may reach another device: no remote copies, remote signals or barrier semaphores. Data moves between devices by JAX's collectives and lax.ppermute only.
A program may use at most 64 MiB of HBM per device.

v0:
```python
import jax
import jax.numpy as jnp
from jax import lax
from jax.sharding import PartitionSpec as P

ITERS = 2


time_step = 0.25
highest = lax.Precision.HIGHEST


def from_behind(block, axis, distance):
    devices = range(lax.axis_size(axis))
    route = [(i - distance, i) for i in devices if i - distance in devices]
    return lax.ppermute(block, axis, route)


def padded(value, sides, width):
    for axis, dim in sides:
        size, length = (lax.axis_size(axis), value.shape[dim])
        up = [(i, (i + 1) % size) for i in range(size - 1)]
        down = [(j, i) for i, j in up]
        last = lax.slice_in_dim(value, length - width, length, axis=dim)
        first = lax.slice_in_dim(value, 0, width, axis=dim)
        before = lax.ppermute(last, axis, up)
        after = lax.ppermute(first, axis, down)
        value = jnp.concatenate([before, value, after], axis=dim)
    return value


def upper_extend(values):
    from_x = from_behind(values[0, :, 0:1], "gx", -1)
    from_y = from_behind(values[1, :, :, 0:1], "gy", -1)
    from_z = from_behind(values[2, :, :, :, 0:1], "gz", -1)
    wide = jnp.pad(values, ((0, 0), (0, 0), (1, 1), (1, 1), (1, 1)))
    wide = wide.at[0, :, -1:, 1:-1, 1:-1].set(from_x)
    wide = wide.at[1, :, 1:-1, -1:, 1:-1].set(from_y)
    wide = wide.at[2, :, 1:-1, 1:-1, -1:].set(from_z)
    return wide


def extend(values):
    return upper_extend(values)


def owned_coupled(extended, weight, schur_op):
    span_x = extended.shape[2] - 2
    span_y = extended.shape[3] - 2
    span_z = extended.shape[4] - 2
    face_values = own_faces(extended)
    applied = jnp.dot(schur_op, face_values, precision=highest, preferred_element_type=jnp.float32)
    applied = (applied * weight.reshape(1, span_x * span_y * span_z)).reshape(
        6, extended.shape[1], span_x, span_y, span_z
    )
    below_x = from_behind(applied[1][:, -1:], "gx", 1)
    below_y = from_behind(applied[3][:, :, -1:], "gy", 1)
    below_z = from_behind(applied[5][:, :, :, -1:], "gz", 1)
    along_x = applied[0] + jnp.concatenate([below_x, applied[1][:, :-1]], 1)
    along_y = applied[2] + jnp.concatenate([below_y, applied[3][:, :, :-1]], 2)
    along_z = applied[4] + jnp.concatenate([below_z, applied[5][:, :, :, :-1]], 3)
    return jnp.stack([along_x, along_y, along_z], 0)


def own_faces(extended):
    span_x = extended.shape[2] - 2
    span_y = extended.shape[3] - 2
    span_z = extended.shape[4] - 2
    pieces = [
        extended[0, :, 1 : span_x + 1, 1 : span_y + 1, 1 : span_z + 1],
        extended[0, :, 2 : span_x + 2, 1 : span_y + 1, 1 : span_z + 1],
        extended[1, :, 1 : span_x + 1, 1 : span_y + 1, 1 : span_z + 1],
        extended[1, :, 1 : span_x + 1, 2 : span_y + 2, 1 : span_z + 1],
        extended[2, :, 1 : span_x + 1, 1 : span_y + 1, 1 : span_z + 1],
        extended[2, :, 1 : span_x + 1, 1 : span_y + 1, 2 : span_z + 2],
    ]
    face_values = jnp.concatenate(pieces, 0)
    return face_values.reshape(face_values.shape[0], span_x * span_y * span_z)


def squares(residual):
    return lax.psum(jnp.sum(residual * residual), ("gx", "gy", "gz"))


def body(fields, trace_old, face_load, face_diag, fine_flag, coeff, volume_op, lift_op, schur_op):
    fine_mask = fine_flag.astype(jnp.float32)
    weight = fine_mask * coeff
    wide_old, weight_wide = (
        padded(trace_old, (("gx", 2), ("gy", 3), ("gz", 4)), 1),
        padded(weight[None, None], (("gx", 2), ("gy", 3), ("gz", 4)), 1),
    )

    def operate(extended, traces):
        return face_diag[:, None] * traces + owned_coupled(extended, weight, schur_op)

    solution = trace_old
    residual = face_load - operate(wide_old, trace_old)
    direction = residual
    norm_now = squares(residual)
    for iteration in range(ITERS):
        wide_direction = extend(direction)
        applied = operate(wide_direction, direction)
        step_length = norm_now / lax.psum(jnp.sum(direction * applied), ("gx", "gy", "gz"))
        solution = solution + step_length * direction
        if iteration + 1 < ITERS:
            residual = residual - step_length * applied
            norm_next = squares(residual)
            direction = residual + norm_next / norm_now * direction
            norm_now = norm_next
    wide_new = extend(solution)
    cells = fine_mask.size
    fine_row = fine_mask.reshape(1, cells)
    traced = fine_row * own_faces(wide_new) + (1.0 - fine_row) * own_faces(wide_old)
    nodal = fields.reshape(fields.shape[0], cells)
    volume = jnp.dot(volume_op, nodal, preferred_element_type=jnp.float32)
    lifted = jnp.dot(lift_op, traced.astype(jnp.bfloat16), preferred_element_type=jnp.float32)
    result = nodal.astype(jnp.float32) + time_step * ((1.0 - fine_row) * volume + lifted)
    return (result.astype(jnp.bfloat16).reshape(fields.shape), solution)


def solution(mesh):
    placed = (
        P(None, "gx", "gy", "gz"),
        P(None, None, "gx", "gy", "gz"),
        P(None, None, "gx", "gy", "gz"),
        P(None, "gx", "gy", "gz"),
        P("gx", "gy", "gz"),
        P("gx", "gy", "gz"),
        P(),
        P(),
        P(),
    )
    return jax.shard_map(
        body,
        mesh=mesh,
        in_specs=placed,
        out_specs=(P(None, "gx", "gy", "gz"), P(None, None, "gx", "gy", "gz")),
        check_vma=False,
    )
```

profile of v0, /device:TPU:0, one launch (start us, length us, event | category | flops | bytes accessed | tf_op | source)
XLA Modules:
  0.0 393.7 jit_solution(17369945597653385307)
XLA Ops:
  3.1 4.9 %collective-permute-start.1 = (f32[3,32,1,4,128]{4,1,3,2,0:T(8,128)S(1)}, f32[3,32,1,4,128]{4,1,3,2,0:T(8,128)S(1)}, u32[]{:S(2)}, u32[]{:S(2)}) collective-permute-start(f32[3,32,1,4,128]{4,1,3,2,0:T(8,128)S(1)} %copy.140), channel_id=1, source_target_pairs={{0,16},{1,17},{2,18},{3,19},{4,20},{5,21},{6,22},{7,23},{8,24},{9,... | collective-permute-start | bytes 589832 | tf_op jit(solution)/shard_map/ppermute | solution.py:26
  8.1 4.1 %collective-permute-done.1 = f32[3,32,1,4,128]{4,1,3,2,0:T(8,128)S(1)} collective-permute-done((f32[3,32,1,4,128]{4,1,3,2,0:T(8,128)S(1)}, f32[3,32,1,4,128]{4,1,3,2,0:T(8,128)S(1)}, u32[]{:S(2)}, u32[]{:S(2)}) %collective-permute-start.1) | collective-permute-done | bytes 196640 | tf_op jit(solution)/shard_map/ppermute | solution.py:26
  13.7 5.6 %collective-permute-start.3 = (f32[3,32,4,1,128]{4,1,3,2,0:T(8,128)S(1)}, f32[3,32,4,1,128]{4,1,3,2,0:T(8,128)}, u32[]{:S(2)}, u32[]{:S(2)}) collective-permute-start(f32[3,32,4,1,128]{4,1,3,2,0:T(8,128)S(1)} %get-tuple-element.152), channel_id=1, source_target_pairs={{0,4},{4,8},{8,12},{1,5},{5,9},{9,13},{2,6},{6,10},{10,14},{3,7},{... | collective-permute-start | bytes 589832 | tf_op jit(solution)/shard_map/ppermute | solution.py:26
  32.9 3.8 collective-permute-start.7
  36.8 4.4 %collective-permute-start.5 = (f32[32,1,4,128]{3,2,0,1:T(4,128)S(1)}, f32[32,1,4,128]{3,2,0,1:T(4,128)S(1)}, u32[]{:S(2)}, u32[]{:S(2)}) collective-permute-start(f32[32,1,4,128]{3,2,0,1:T(4,128)S(1)} %get-tuple-element.164), channel_id=1, source_target_pairs={{0,16},{1,17},{2,18},{3,19},{4,20},{5,21},{6,22},{7,23},{8,24},{9,... | collective-permute-start | bytes 196616 | tf_op jit(solution)/shard_map/ppermute | solution.py:16
  41.2 4.5 %collective-permute-start.6 = (f32[32,2,1,128]{3,2,1,0:T(1,128)S(1)}, f32[32,2,1,128]{3,2,1,0:T(1,128)S(1)}, u32[]{:S(2)}, u32[]{:S(2)}) collective-permute-start(f32[32,2,1,128]{3,2,1,0:T(1,128)S(1)} %slice.709), channel_id=1, source_target_pairs={{0,4},{4,8},{8,12},{1,5},{5,9},{9,13},{2,6},{6,10},{10,14},{3,7},{... | collective-permute-start | bytes 98312 | tf_op jit(solution)/shard_map/ppermute | solution.py:16
  54.2 10.5 %scatter.30 = f32[3,32,4,6,130]{4,3,2,1,0:T(8,128)} dynamic-update-slice(f32[3,32,4,6,130]{4,3,2,1,0:T(8,128)} %pad.46, f32[1,32,1,4,128]{4,3,2,1,0:T(4,128)S(1)} %bitcast.110, s32[]{:T(128)} %constant.241.clone.1, s32[]{:T(128)} %constant.241.clone.1, s32[]{:T(128)} %constant.242.clone.1, s32[]{:T(128)} %constant.243.clone.1, s32[]{:T(128)} %constant.243.clone.1) | dynamic-update-slice | bytes 131076 | tf_op jit(solution)/shard_map/scatter | solution.py:37
  64.7 11.1 %scatter.31 = f32[3,32,4,6,130]{4,3,2,1,0:T(8,128)} dynamic-update-slice(f32[3,32,4,6,130]{4,3,2,1,0:T(8,128)} %scatter.30, f32[1,32,2,1,128]{4,3,2,1,0:T(1,128)S(1)} %bitcast.118, s32[]{:T(128)} %constant.243.clone.1, s32[]{:T(128)} %constant.241.clone.1, s32[]{:T(128)} %constant.243.clone.1, s32[]{:T(128)} %constant.244.clone.1, s32[]{:T(128)} %constant.243.clone.1) | dynamic-update-slice | bytes 65540 | tf_op jit(solution)/shard_map/scatter | solution.py:38
  75.9 10.4 %scatter.34 = f32[3,32,4,6,130]{4,3,2,1,0:T(8,128)} dynamic-update-slice(f32[3,32,4,6,130]{4,3,2,1,0:T(8,128)} %scatter.31, f32[1,32,2,4,1]{4,3,2,1,0:T(4,128)S(1)} %copy.111, s32[]{:T(128)} %constant.245.clone.1, s32[]{:T(128)} %constant.241.clone.1, s32[]{:T(128)} %constant.243.clone.1, s32[]{:T(128)} %constant.243.clone.1, s32[]{:T(128)} %constant.246.clone.1) | dynamic-update-slice | bytes 2052 | tf_op jit(solution)/shard_map/scatter | solution.py:39
  93.6 4.5 %collective-permute-start.11 = (f32[32,1,4,128]{3,2,0,1:T(4,128)S(1)}, f32[32,1,4,128]{3,2,0,1:T(4,128)S(1)}, u32[]{:S(2)}, u32[]{:S(2)}) collective-permute-start(f32[32,1,4,128]{3,2,0,1:T(4,128)S(1)} %get-tuple-element.162), channel_id=1, source_target_pairs={{0,16},{1,17},{2,18},{3,19},{4,20},{5,21},{6,22},{7,23},{8,24},{9,... | collective-permute-start | bytes 196616 | tf_op jit(solution)/shard_map/ppermute | solution.py:16
  98.3 4.8 %collective-permute-start.12 = (f32[32,2,1,128]{3,2,1,0:T(1,128)S(1)}, f32[32,2,1,128]{3,2,1,0:T(1,128)S(1)}, u32[]{:S(2)}, u32[]{:S(2)}) collective-permute-start(f32[32,2,1,128]{3,2,1,0:T(1,128)S(1)} %slice.730), channel_id=1, source_target_pairs={{0,4},{4,8},{8,12},{1,5},{5,9},{9,13},{2,6},{6,10},{10,14},{3,7},{... | collective-permute-start | bytes 98312 | tf_op jit(solution)/shard_map/ppermute | solution.py:16
  105.8 41.1 %all-reduce.3 = (f32[]{:T(128)}, f32[]{:T(128)}) all-reduce(f32[]{:T(128)} %get-tuple-element.111, f32[]{:T(128)} %get-tuple-element.110), channel_id=1, replica_groups=mesh['gx'=2,'gy'=4,'gz'=4] {'gx','gy','gz'}, use_global_device_ids=true, to_apply=%region_1.0 | all-reduce | flops 2 | bytes 16 | tf_op jit(solution)/shard_map/psum | solution.py:82
  149.6 41.2 %psum.30 = f32[]{:T(128)} all-reduce(f32[]{:T(128)} %multiply_reduce_fusion), channel_id=1, replica_groups=mesh['gx'=2,'gy'=4,'gz'=4] {'gx','gy','gz'}, use_global_device_ids=true, to_apply=%region_5.6 | all-reduce | flops 1 | bytes 8 | tf_op jit(solution)/shard_map/psum | solution.py:82
  202.2 10.5 %scatter.35 = f32[3,32,4,6,130]{4,3,2,1,0:T(8,128)} dynamic-update-slice(f32[3,32,4,6,130]{4,3,2,1,0:T(8,128)} %pad.47, f32[1,32,1,4,128]{4,3,2,1,0:T(4,128)} %bitcast.28, s32[]{:T(128)} %constant.241.clone.1, s32[]{:T(128)} %constant.241.clone.1, s32[]{:T(128)} %constant.242.clone.1, s32[]{:T(128)} %constant.243.clone.1, s32[]{:T(128)} %constant.243.clone.1) | dynamic-update-slice | bytes 131076 | tf_op jit(solution)/shard_map/scatter | solution.py:37
  212.7 11.1 %scatter.36 = f32[3,32,4,6,130]{4,3,2,1,0:T(8,128)} dynamic-update-slice(f32[3,32,4,6,130]{4,3,2,1,0:T(8,128)} %scatter.35, f32[1,32,2,1,128]{4,3,2,1,0:T(1,128)} %bitcast.31, s32[]{:T(128)} %constant.243.clone.1, s32[]{:T(128)} %constant.241.clone.1, s32[]{:T(128)} %constant.243.clone.1, s32[]{:T(128)} %constant.244.clone.1, s32[]{:T(128)} %constant.243.clone.1) | dynamic-update-slice | bytes 65540 | tf_op jit(solution)/shard_map/scatter | solution.py:38
  223.8 10.5 %scatter.39 = f32[3,32,4,6,130]{4,3,2,1,0:T(8,128)} dynamic-update-slice(f32[3,32,4,6,130]{4,3,2,1,0:T(8,128)} %scatter.36, f32[1,32,2,4,1]{4,3,2,1,0:T(4,128)} %copy.120, s32[]{:T(128)} %constant.245.clone.1, s32[]{:T(128)} %constant.241.clone.1, s32[]{:T(128)} %constant.243.clone.1, s32[]{:T(128)} %constant.243.clone.1, s32[]{:T(128)} %constant.246.clone.1) | dynamic-update-slice | bytes 2052 | tf_op jit(solution)/shard_map/scatter | solution.py:39
  269.1 4.3 %collective-permute-start.19 = (f32[32,2,4,1]{3,2,1,0:T(4,128)}, f32[32,2,4,1]{3,2,1,0:T(4,128)}, u32[]{:S(2)}, u32[]{:S(2)}) collective-permute-start(f32[32,2,4,1]{3,2,1,0:T(4,128)} %slice.755), channel_id=1, source_target_pairs={{0,1},{1,2},{2,3},{4,5},{5,6},{6,7},{8,9},{9,10},{10,11},{12,13},{... | collective-permute-start | bytes 3080 | tf_op jit(solution)/shard_map/ppermute | solution.py:16
  275.8 5.8 %collective-permute-start.17 = (f32[32,1,4,128]{3,2,0,1:T(4,128)}, f32[32,1,4,128]{3,2,0,1:T(4,128)}, u32[]{:S(2)}, u32[]{:S(2)}) collective-permute-start(f32[32,1,4,128]{3,2,0,1:T(4,128)} %get-tuple-element.160), channel_id=1, source_target_pairs={{0,16},{1,17},{2,18},{3,19},{4,20},{5,21},{6,22},{7,23},{8,24},{9,... | collective-permute-start | bytes 196616 | tf_op jit(solution)/shard_map/ppermute | solution.py:16
  283.2 5.2 %collective-permute-start.18 = (f32[32,2,1,128]{3,2,1,0:T(1,128)S(1)}, f32[32,2,1,128]{3,2,1,0:T(1,128)}, u32[]{:S(2)}, u32[]{:S(2)}) collective-permute-start(f32[32,2,1,128]{3,2,1,0:T(1,128)S(1)} %slice.751), channel_id=1, source_target_pairs={{0,4},{4,8},{8,12},{1,5},{5,9},{9,13},{2,6},{6,10},{10,14},{3,7},{... | collective-permute-start | bytes 98312 | tf_op jit(solution)/shard_map/ppermute | solution.py:16
  298.6 38.2 %psum.31 = f32[]{:T(128)} all-reduce(f32[]{:T(128)} %fusion.8), channel_id=1, replica_groups=mesh['gx'=2,'gy'=4,'gz'=4] {'gx','gy','gz'}, use_global_device_ids=true, to_apply=%region_7.8 | all-reduce | flops 1 | bytes 8 | tf_op jit(solution)/shard_map/psum | solution.py:103
  344.4 3.3 pad.48
  347.9 10.5 %scatter.40 = f32[3,32,4,6,130]{4,3,2,1,0:T(8,128)} dynamic-update-slice(f32[3,32,4,6,130]{4,3,2,1,0:T(8,128)} %pad.48, f32[1,32,1,4,128]{4,3,2,1,0:T(4,128)S(1)} %bitcast.109, s32[]{:T(128)} %constant.241.clone.1, s32[]{:T(128)} %constant.241.clone.1, s32[]{:T(128)} %constant.242.clone.1, s32[]{:T(128)} %constant.243.clone.1, s32[]{:T(128)} %constant.243.clone.1) | dynamic-update-slice | bytes 131076 | tf_op jit(solution)/shard_map/scatter | solution.py:37
  358.4 11.1 %scatter.41 = f32[3,32,4,6,130]{4,3,2,1,0:T(8,128)} dynamic-update-slice(f32[3,32,4,6,130]{4,3,2,1,0:T(8,128)} %scatter.40, f32[1,32,2,1,128]{4,3,2,1,0:T(1,128)S(1)} %bitcast.117, s32[]{:T(128)} %constant.243.clone.1, s32[]{:T(128)} %constant.241.clone.1, s32[]{:T(128)} %constant.243.clone.1, s32[]{:T(128)} %constant.244.clone.1, s32[]{:T(128)} %constant.243.clone.1) | dynamic-update-slice | bytes 65540 | tf_op jit(solution)/shard_map/scatter | solution.py:38
  369.6 10.4 %scatter.44 = f32[3,32,4,6,130]{4,3,2,1,0:T(8,128)} dynamic-update-slice(f32[3,32,4,6,130]{4,3,2,1,0:T(8,128)} %scatter.41, f32[1,32,2,4,1]{4,3,2,1,0:T(4,128)S(1)} %copy.129, s32[]{:T(128)} %constant.245.clone.1, s32[]{:T(128)} %constant.241.clone.1, s32[]{:T(128)} %constant.243.clone.1, s32[]{:T(128)} %constant.243.clone.1, s32[]{:T(128)} %constant.246.clone.1) | dynamic-update-slice | bytes 2052 | tf_op jit(solution)/shard_map/scatter | solution.py:39
  (219 shorter events, 116.1 us)
Async XLA Ops:
  0.6 197.2 %copy-start = (bf16[384,384]{1,0:T(8,128)(2,1)S(1)}, bf16[384,384]{1,0:T(8,128)(2,1)}, u32[]{:S(2)}) copy-start(bf16[384,384]{1,0:T(8,128)(2,1)} %param.33) | copy-start | bytes 884740
  1.8 10.5 %collective-permute-start = (f32[3,32,1,4,128]{4,1,3,2,0:T(8,128)S(1)}, f32[3,32,1,4,128]{4,1,3,2,0:T(8,128)S(1)}, u32[]{:S(2)}, u32[]{:S(2)}) collective-permute-start(f32[3,32,1,4,128]{4,1,3,2,0:T(8,128)S(1)} %copy.139), channel_id=1, source_target_pairs={{16,0},{17,1},{18,2},{19,3},{20,4},{21,5},{22,6},{23,7},{24,8},{25... | collective-permute-start | bytes 589832 | tf_op jit(solution)/shard_map/ppermute | solution.py:27
  3.1 9.1 %collective-permute-start.1 = (f32[3,32,1,4,128]{4,1,3,2,0:T(8,128)S(1)}, f32[3,32,1,4,128]{4,1,3,2,0:T(8,128)S(1)}, u32[]{:S(2)}, u32[]{:S(2)}) collective-permute-start(f32[3,32,1,4,128]{4,1,3,2,0:T(8,128)S(1)} %copy.140), channel_id=1, source_target_pairs={{0,16},{1,17},{2,18},{3,19},{4,20},{5,21},{6,22},{7,23},{8,24},{9,... | collective-permute-start | bytes 589832 | tf_op jit(solution)/shard_map/ppermute | solution.py:26
  12.4 8.6 %collective-permute-start.2 = (f32[3,32,4,1,128]{4,1,3,2,0:T(8,128)S(1)}, f32[3,32,4,1,128]{4,1,3,2,0:T(8,128)S(1)}, u32[]{:S(2)}, u32[]{:S(2)}) collective-permute-start(f32[3,32,4,1,128]{4,1,3,2,0:T(8,128)S(1)} %get-tuple-element.153), channel_id=1, source_target_pairs={{4,0},{8,4},{12,8},{5,1},{9,5},{13,9},{6,2},{10,6},{14,10},{7,3},{... | collective-permute-start | bytes 589832 | tf_op jit(solution)/shard_map/ppermute | solution.py:27
  13.7 8.1 %collective-permute-start.3 = (f32[3,32,4,1,128]{4,1,3,2,0:T(8,128)S(1)}, f32[3,32,4,1,128]{4,1,3,2,0:T(8,128)}, u32[]{:S(2)}, u32[]{:S(2)}) collective-permute-start(f32[3,32,4,1,128]{4,1,3,2,0:T(8,128)S(1)} %get-tuple-element.152), channel_id=1, source_target_pairs={{0,4},{4,8},{8,12},{1,5},{5,9},{9,13},{2,6},{6,10},{10,14},{3,7},{... | collective-permute-start | bytes 589832 | tf_op jit(solution)/shard_map/ppermute | solution.py:26
  23.4 3.8 collective-permute-start.4
  32.9 13.0 %collective-permute-start.7 = (f32[32,2,4,1]{3,2,1,0:T(4,128)S(1)}, f32[32,2,4,1]{3,2,1,0:T(4,128)S(1)}, u32[]{:S(2)}, u32[]{:S(2)}) collective-permute-start(f32[32,2,4,1]{3,2,1,0:T(4,128)S(1)} %slice.713), channel_id=1, source_target_pairs={{0,1},{1,2},{2,3},{4,5},{5,6},{6,7},{8,9},{9,10},{10,11},{12,13},{... | collective-permute-start | bytes 3080 | tf_op jit(solution)/shard_map/ppermute | solution.py:16
  36.8 10.6 %collective-permute-start.5 = (f32[32,1,4,128]{3,2,0,1:T(4,128)S(1)}, f32[32,1,4,128]{3,2,0,1:T(4,128)S(1)}, u32[]{:S(2)}, u32[]{:S(2)}) collective-permute-start(f32[32,1,4,128]{3,2,0,1:T(4,128)S(1)} %get-tuple-element.164), channel_id=1, source_target_pairs={{0,16},{1,17},{2,18},{3,19},{4,20},{5,21},{6,22},{7,23},{8,24},{9,... | collective-permute-start | bytes 196616 | tf_op jit(solution)/shard_map/ppermute | solution.py:16
  41.2 6.1 %collective-permute-start.6 = (f32[32,2,1,128]{3,2,1,0:T(1,128)S(1)}, f32[32,2,1,128]{3,2,1,0:T(1,128)S(1)}, u32[]{:S(2)}, u32[]{:S(2)}) collective-permute-start(f32[32,2,1,128]{3,2,1,0:T(1,128)S(1)} %slice.709), channel_id=1, source_target_pairs={{0,4},{4,8},{8,12},{1,5},{5,9},{9,13},{2,6},{6,10},{10,14},{3,7},{... | collective-permute-start | bytes 98312 | tf_op jit(solution)/shard_map/ppermute | solution.py:16
  47.7 6.5 %collective-permute-start.8 = (f32[32,1,4,128]{3,2,0,1:T(4,128)S(1)}, f32[32,1,4,128]{3,2,0,1:T(4,128)S(1)}, u32[]{:S(2)}, u32[]{:S(2)}) collective-permute-start(f32[32,1,4,128]{3,2,0,1:T(4,128)S(1)} %slice_bitcast_fusion.12), channel_id=1, source_target_pairs={{16,0},{17,1},{18,2},{19,3},{20,4},{21,5},{22,6},{23,7},{24,8},{25... | collective-permute-start | bytes 196616 | tf_op jit(solution)/shard_map/ppermute | solution.py:16
  49.0 15.7 %collective-permute-start.9 = (f32[32,2,1,128]{3,1,0,2:T(2,128)S(1)}, f32[32,2,1,128]{3,1,0,2:T(2,128)S(1)}, u32[]{:S(2)}, u32[]{:S(2)}) collective-permute-start(f32[32,2,1,128]{3,1,0,2:T(2,128)S(1)} %bitcast.119), channel_id=1, source_target_pairs={{4,0},{8,4},{12,8},{5,1},{9,5},{13,9},{6,2},{10,6},{14,10},{7,3},{... | collective-permute-start | bytes 98312 | tf_op jit(solution)/shard_map/ppermute | solution.py:16
  50.4 3.6 collective-permute-start.10
  90.4 12.8 %collective-permute-start.13 = (f32[32,2,4,1]{3,2,1,0:T(4,128)S(1)}, f32[32,2,4,1]{3,2,1,0:T(4,128)S(1)}, u32[]{:S(2)}, u32[]{:S(2)}) collective-permute-start(f32[32,2,4,1]{3,2,1,0:T(4,128)S(1)} %slice.734), channel_id=1, source_target_pairs={{0,1},{1,2},{2,3},{4,5},{5,6},{6,7},{8,9},{9,10},{10,11},{12,13},{... | collective-permute-start | bytes 3080 | tf_op jit(solution)/shard_map/ppermute | solution.py:16
  93.6 11.1 %collective-permute-start.11 = (f32[32,1,4,128]{3,2,0,1:T(4,128)S(1)}, f32[32,1,4,128]{3,2,0,1:T(4,128)S(1)}, u32[]{:S(2)}, u32[]{:S(2)}) collective-permute-start(f32[32,1,4,128]{3,2,0,1:T(4,128)S(1)} %get-tuple-element.162), channel_id=1, source_target_pairs={{0,16},{1,17},{2,18},{3,19},{4,20},{5,21},{6,22},{7,23},{8,24},{9,... | collective-permute-start | bytes 196616 | tf_op jit(solution)/shard_map/ppermute | solution.py:16
  98.3 6.4 %collective-permute-start.12 = (f32[32,2,1,128]{3,2,1,0:T(1,128)S(1)}, f32[32,2,1,128]{3,2,1,0:T(1,128)S(1)}, u32[]{:S(2)}, u32[]{:S(2)}) collective-permute-start(f32[32,2,1,128]{3,2,1,0:T(1,128)S(1)} %slice.730), channel_id=1, source_target_pairs={{0,4},{4,8},{8,12},{1,5},{5,9},{9,13},{2,6},{6,10},{10,14},{3,7},{... | collective-permute-start | bytes 98312 | tf_op jit(solution)/shard_map/ppermute | solution.py:16
  193.1 9.1 %collective-permute-start.14 = (f32[32,1,4,128]{3,2,0,1:T(4,128)S(1)}, f32[32,1,4,128]{3,2,0,1:T(4,128)}, u32[]{:S(2)}, u32[]{:S(2)}) collective-permute-start(f32[32,1,4,128]{3,2,0,1:T(4,128)S(1)} %slice_bitcast_fusion.9), channel_id=1, source_target_pairs={{16,0},{17,1},{18,2},{19,3},{20,4},{21,5},{22,6},{23,7},{24,8},{25... | collective-permute-start | bytes 196616 | tf_op jit(solution)/shard_map/ppermute | solution.py:16
  194.4 18.2 %collective-permute-start.15 = (f32[32,2,1,128]{3,1,0,2:T(2,128)S(1)}, f32[32,2,1,128]{3,1,0,2:T(2,128)}, u32[]{:S(2)}, u32[]{:S(2)}) collective-permute-start(f32[32,2,1,128]{3,1,0,2:T(2,128)S(1)} %bitcast.116), channel_id=1, source_target_pairs={{4,0},{8,4},{12,8},{5,1},{9,5},{13,9},{6,2},{10,6},{14,10},{7,3},{... | collective-permute-start | bytes 98312 | tf_op jit(solution)/shard_map/ppermute | solution.py:16
  196.4 4.3 %collective-permute-start.16 = (f32[32,2,4,1]{0,2,3,1:T(4,128)}, f32[32,2,4,1]{0,2,3,1:T(4,128)}, u32[]{:S(2)}, u32[]{:S(2)}) collective-permute-start(f32[32,2,4,1]{0,2,3,1:T(4,128)} %bitcast.32), channel_id=1, source_target_pairs={{1,0},{2,1},{3,2},{5,4},{6,5},{7,6},{9,8},{10,9},{11,10},{13,12},{... | collective-permute-start | bytes 3080 | tf_op jit(solution)/shard_map/ppermute | solution.py:16
  269.1 22.5 %collective-permute-start.19 = (f32[32,2,4,1]{3,2,1,0:T(4,128)}, f32[32,2,4,1]{3,2,1,0:T(4,128)}, u32[]{:S(2)}, u32[]{:S(2)}) collective-permute-start(f32[32,2,4,1]{3,2,1,0:T(4,128)} %slice.755), channel_id=1, source_target_pairs={{0,1},{1,2},{2,3},{4,5},{5,6},{6,7},{8,9},{9,10},{10,11},{12,13},{... | collective-permute-start | bytes 3080 | tf_op jit(solution)/shard_map/ppermute | solution.py:16
  275.8 19.9 %collective-permute-start.17 = (f32[32,1,4,128]{3,2,0,1:T(4,128)}, f32[32,1,4,128]{3,2,0,1:T(4,128)}, u32[]{:S(2)}, u32[]{:S(2)}) collective-permute-start(f32[32,1,4,128]{3,2,0,1:T(4,128)} %get-tuple-element.160), channel_id=1, source_target_pairs={{0,16},{1,17},{2,18},{3,19},{4,20},{5,21},{6,22},{7,23},{8,24},{9,... | collective-permute-start | bytes 196616 | tf_op jit(solution)/shard_map/ppermute | solution.py:16
  283.2 11.4 %collective-permute-start.18 = (f32[32,2,1,128]{3,2,1,0:T(1,128)S(1)}, f32[32,2,1,128]{3,2,1,0:T(1,128)}, u32[]{:S(2)}, u32[]{:S(2)}) collective-permute-start(f32[32,2,1,128]{3,2,1,0:T(1,128)S(1)} %slice.751), channel_id=1, source_target_pairs={{0,4},{4,8},{8,12},{1,5},{5,9},{9,13},{2,6},{6,10},{10,14},{3,7},{... | collective-permute-start | bytes 98312 | tf_op jit(solution)/shard_map/ppermute | solution.py:16
  340.2 7.7 %collective-permute-start.20 = (f32[32,1,4,128]{3,2,0,1:T(4,128)S(1)}, f32[32,1,4,128]{3,2,0,1:T(4,128)S(1)}, u32[]{:S(2)}, u32[]{:S(2)}) collective-permute-start(f32[32,1,4,128]{3,2,0,1:T(4,128)S(1)} %slice_bitcast_fusion.6), channel_id=1, source_target_pairs={{16,0},{17,1},{18,2},{19,3},{20,4},{21,5},{22,6},{23,7},{24,8},{25... | collective-permute-start | bytes 196616 | tf_op jit(solution)/shard_map/ppermute | solution.py:16
  341.5 16.9 %collective-permute-start.21 = (f32[32,2,1,128]{3,1,0,2:T(2,128)S(1)}, f32[32,2,1,128]{3,1,0,2:T(2,128)S(1)}, u32[]{:S(2)}, u32[]{:S(2)}) collective-permute-start(f32[32,2,1,128]{3,1,0,2:T(2,128)S(1)} %bitcast.115), channel_id=1, source_target_pairs={{4,0},{8,4},{12,8},{5,1},{9,5},{13,9},{6,2},{10,6},{14,10},{7,3},{... | collective-permute-start | bytes 98312 | tf_op jit(solution)/shard_map/ppermute | solution.py:16
  342.9 4.8 %collective-permute-start.22 = (f32[32,2,4,1]{0,2,3,1:T(4,128)S(1)}, f32[32,2,4,1]{0,2,3,1:T(4,128)S(1)}, u32[]{:S(2)}, u32[]{:S(2)}) collective-permute-start(f32[32,2,4,1]{0,2,3,1:T(4,128)S(1)} %bitcast.127), channel_id=1, source_target_pairs={{1,0},{2,1},{3,2},{5,4},{6,5},{7,6},{9,8},{10,9},{11,10},{13,12},{... | collective-permute-start | bytes 3080 | tf_op jit(solution)/shard_map/ppermute | solution.py:16
  (16 other events, 377.2 us)
where the time goes:
time: 399 us; the launch traced here: 394 us
  local copies, waits for them, and re-layouts  175 us (44%)
  blocking collectives  121 us (30%)
  starting transfers between devices  66.7 us (17%)
  other arithmetic  12.6 us (3%)
  matrix products  7.08 us (2%)
  waiting for transfers between devices  6.24 us (2%)
  between operations  5.72 us (1%)
    psum x2, blocking collectives, squares(): return lax.psum(jnp.sum(residual * residual), ('gx', 'gy', 'gz'))  82.3 us
    ppermute x18, starting transfers between devices, from_behind(): return lax.ppermute(block, axis, route)  52.3 us
    psum x1, blocking collectives, body(): lax.psum(jnp.sum(direction * applied), ('gx', 'gy', 'gz'))  38.2 us
    scatter x3, local copies, waits for them, and re-layouts, upper_extend(): wide = wide.at[1, :, 1:-1, -1:, 1:-1].set(from_y)  33.4 us
    scatter x3, local copies, waits for them, and re-layouts, upper_extend(): wide = wide.at[0, :, -1:, 1:-1, 1:-1].set(from_x)  31.5 us
    scatter x3, local copies, waits for them, and re-layouts, upper_extend(): wide = wide.at[2, :, 1:-1, 1:-1, -1:].set(from_z)  31.3 us
    unnamed x61, local copies, waits for them, and re-layouts  17.7 us
    concatenate x28, local copies, waits for them, and re-layouts, own_faces(): face_values = jnp.concatenate(pieces, 0)  15.8 us
  transfers between devices with their start and end apart: 23, of which 4 were waited for; matrix products, arithmetic and copies ran while one was open for 15% of the time, Pallas kernels for 0%

commit v1 on v0

v1 whole, which is shorter than its diff:
```python
import functools

import jax
import jax.numpy as jnp
from jax import lax
from jax.experimental import pallas as pl
from jax.experimental.pallas import tpu as pltpu
from jax.sharding import PartitionSpec as P

AXES = ("gx", "gy", "gz")
TIME_STEP = 0.25
SHIFT_LIMIT = 1e4
VMEM_GRANT = 12 * 1024 * 1024
f32, bf16 = jnp.float32, jnp.bfloat16


def pairs(axis, odd):
    size = lax.axis_size(axis)
    route = []
    for i in range(odd, size - 1, 2):
        route += [(i, i + 1), (i + 1, i)]
    return route


def exchange(sends):
    got = []
    for axis, per_axis in zip(AXES, sends):
        got.append([lax.ppermute(v, axis, pairs(axis, odd)) if pairs(axis, odd) else None for odd, v in enumerate(per_axis)])
    return got


def counts():
    return [sum(bool(pairs(axis, odd)) for odd in (0, 1)) for axis in AXES]


def lane_iota(shape):
    return lax.broadcasted_iota(jnp.int32, shape, len(shape) - 1)


def moved(value, source, target):
    width = value.shape[-1]
    shift = (target - source) % width
    return pltpu.roll(value, shift, value.ndim - 1) if shift else value


def place():
    index = [lax.axis_index(a) for a in AXES]
    parity = [lax.rem(i, 2) for i in index]
    below_top = [(i < lax.axis_size(a) - 1).astype(f32) for i, a in zip(index, AXES)]
    return parity, below_top


def split(value):
    high = value.astype(bf16)
    return high, (value - high.astype(f32)).astype(bf16)


class Geometry:
    def __init__(self, F, EX, EY, EZ):
        self.F, self.EX, self.EY, self.EZ = F, EX, EY, EZ
        self.M = EX * EY


def gather_and_apply(geo, own, halo, schur, ghi, glo):
    F, EX, EY, EZ, M = geo.F, geo.EX, geo.EY, geo.EZ, geo.M
    hx, hy, hz = halo
    lanes = lane_iota((F, EZ))
    for m in range(M):
        i, j = divmod(m, EY)
        z_own = own(2, m)
        z_up = jnp.where(lanes == EZ - 1, moved(hz, m, EZ - 1), moved(z_own, 1, 0))
        blocks = [
            own(0, m), own(0, m + EY) if i + 1 < EX else hx(j),
            own(1, m), own(1, m + 1) if j + 1 < EY else hy(i),
            z_own, z_up,
        ]
        for s, block in enumerate(blocks):
            high, low = split(block)
            ghi[s * F:(s + 1) * F, m * EZ:(m + 1) * EZ] = high
            glo[s * F:(s + 1) * F, m * EZ:(m + 1) * EZ] = low
    n = 6 * F
    both = jnp.dot(schur[...], ghi[...], preferred_element_type=f32)
    return both[:n] + (both[n:] + jnp.dot(schur[:n], glo[...], preferred_element_type=f32))


def spread(geo, y, weight, own_term, sign, out, sends, parity):
    F, EX, EY, EZ, M = geo.F, geo.EX, geo.EY, geo.EZ, geo.M
    lanes = lane_iota((F, EZ))
    wrow = [weight[m:m + 1] * sign for m in range(M)]

    def block(s, m):
        return y[s * F:(s + 1) * F, m * EZ:(m + 1) * EZ] * wrow[m]

    low = {}
    bottom_z = jnp.zeros((F, EZ), f32)
    top_z = jnp.zeros((F, EZ), f32)
    for m in range(M):
        i, j = divmod(m, EY)
        vx = own_term(0, m) + block(0, m)
        if i > 0:
            vx = vx + block(1, m - EY)
        else:
            low[0, j] = vx
        out[0, m] = vx
        vy = own_term(1, m) + block(2, m)
        if j > 0:
            vy = vy + block(3, m - 1)
        else:
            low[1, i] = vy
        out[1, m] = vy
        up = block(5, m)
        vz = own_term(2, m) + block(4, m) + jnp.where(lanes == 0, 0.0, moved(up, 0, 1))
        out[2, m] = vz
        bottom_z = jnp.where(lanes == m, moved(vz, 0, m), bottom_z)
        top_z = jnp.where(lanes == m, moved(up, EZ - 1, m), top_z)
    high_x = [block(1, (EX - 1) * EY + j) for j in range(EY)]
    high_y = [block(3, i * EY + EY - 1) for i in range(EX)]
    for odd, ref in enumerate(sends[0]):
        for j in range(EY):
            ref[j] = jnp.where(parity[0] == odd, high_x[j], low[0, j])
    for odd, ref in enumerate(sends[1]):
        for i in range(EX):
            ref[i] = jnp.where(parity[1] == odd, high_y[i], low[1, i])
    for odd, ref in enumerate(sends[2]):
        ref[...] = jnp.where(parity[2] == odd, top_z, bottom_z)


def chosen(refs, parity, read, flip=False):
    values = [read(r) for r in refs]
    if not values:
        return None
    if len(values) == 1:
        values.append(jnp.zeros_like(values[0]))
    first, second = (values[1], values[0]) if flip else values
    return jnp.where(parity == 0, first, second)


def completed(geo, partial, sent, got, parity, below_top, full, halos):
    F, EX, EY, EZ, M = geo.F, geo.EX, geo.EY, geo.EZ, geo.M
    lanes = lane_iota((F, EZ))
    for f in range(3):
        for m in range(M):
            i, j = divmod(m, EY)
            v = partial[f, m]
            if f == 0 and i == 0 and got[0]:
                v = v + chosen(got[0], parity[0], lambda r: r[j], True)
            if f == 1 and j == 0 and got[1]:
                v = v + chosen(got[1], parity[1], lambda r: r[i], True)
            if f == 2 and got[2]:
                below = chosen(got[2], parity[2], lambda r: r[...], True)
                v = v + jnp.where(lanes == 0, moved(below, m, 0), 0.0)
            full[f, m] = v
    for a, n in ((0, EY), (1, EX)):
        for k in range(n):
            if got[a]:
                both = chosen(sent[a], parity[a], lambda r: r[k]) + chosen(got[a], parity[a], lambda r: r[k])
                halos[a][k] = both * below_top[a]
            else:
                halos[a][k] = jnp.zeros((F, EZ), f32)
    if got[2]:
        both = chosen(sent[2], parity[2], lambda r: r[...]) + chosen(got[2], parity[2], lambda r: r[...])
        halos[2][...] = both * below_top[2]
    else:
        halos[2][...] = jnp.zeros((F, EZ), f32)


def folded(total, value):
    v = value.reshape(value.shape[0] // 8, 8, value.shape[1]).sum(0)
    return v if total is None else total + v


def rows(ref, geo, f, m):
    return ref[pl.ds(f * geo.F * geo.M + m, geo.F, stride=geo.M), :]


def first_slabs(geo, trace, sx, sy, sz):
    F, EX, EY, EZ, M = geo.F, geo.EX, geo.EY, geo.EZ, geo.M
    lanes = lane_iota((F, EZ))
    for j in range(EY):
        sx[j] = rows(trace, geo, 0, j)
    for i in range(EX):
        sy[i] = rows(trace, geo, 1, i * EY)
    z = jnp.zeros((F, EZ), f32)
    for m in range(M):
        z = jnp.where(lanes == m, moved(rows(trace, geo, 2, m), 0, m), z)
    sz[...] = z


def take(refs, *sizes):
    refs = list(refs)
    out = []
    for s in sizes:
        if isinstance(s, (list, tuple)):
            group = []
            for n in s:
                group.append([refs.pop(0) for _ in range(n)])
            out.append(group)
        else:
            out.append([refs.pop(0) for _ in range(s)])
    assert not refs
    return out


def fetch(pairs, sems):
    copies = [pltpu.make_async_copy(src, dst, sems.at[k]) for k, (src, dst) in enumerate(pairs)]
    for c in copies:
        c.start()
    return copies


def kernel_prepare(geo, trace, load, diag_in, fine, coeff, schur, own, diag, weight, matrix, vload, vfine, vcoeff, vschur, sems):
    copies = fetch([(load, vload), (diag_in, diag), (fine, vfine), (coeff, vcoeff), (schur, vschur)], sems)
    for c in copies:
        c.wait()
    weight[...] = vfine[...].astype(f32) * vcoeff[...]
    n = 6 * geo.F
    matrix[:n], matrix[n:] = split(vschur[...])
    for f in range(3):
        for m in range(geo.M):
            own[f, m] = rows(vload, geo, f, m) - diag[f * geo.M + m:f * geo.M + m + 1] * rows(trace, geo, f, m)


def kernel_start(geo, n, trace, own, weight, schur, *refs):
    got, halos, (partial,), sends, (ghi, glo) = take(refs, n, 3, 1, n, 2)
    parity, _ = place()
    for a, k in ((0, geo.EY), (1, geo.EX)):
        for t in range(k):
            halos[a][t] = chosen(got[a], parity[a], lambda r: r[t]) if got[a] else jnp.zeros((geo.F, geo.EZ), f32)
    halos[2][...] = chosen(got[2], parity[2], lambda r: r[...]) if got[2] else jnp.zeros((geo.F, geo.EZ), f32)
    halo = (lambda j: halos[0][j], lambda i: halos[1][i], halos[2][...])
    y = gather_and_apply(geo, lambda f, m: rows(trace, geo, f, m), halo, schur, ghi, glo)
    spread(geo, y, weight[...], lambda f, m: own[f, m], -1.0, partial, sends, parity)


def accumulate(total, value):
    return value if total is None else total + value


def kernel_middle(geo, n, partial, diag, weight, schur, *refs):
    sent, got, (full,), halos, (image,), sends, (dots,), (ghi, glo) = take(refs, n, n, 1, 3, 1, n, 1, 2)
    F, EZ, M = geo.F, geo.EZ, geo.M
    parity, below_top = place()
    completed(geo, partial, sent, got, parity, below_top, full, halos)
    halo = (lambda j: halos[0][j], lambda i: halos[1][i], halos[2][...])
    y = gather_and_apply(geo, lambda f, m: full[f, m], halo, schur, ghi, glo)
    squares = energy = None
    for f in range(3):
        for m in range(M):
            vv = folded(None, full[f, m] * full[f, m])
            squares = accumulate(squares, vv)
            energy = accumulate(energy, vv * diag[f * M + m:f * M + m + 1])
    for m in range(M):
        part = None
        for s in range(6):
            at = (slice(s * F, (s + 1) * F), slice(m * EZ, (m + 1) * EZ))
            part = folded(part, (ghi[at].astype(f32) + glo[at].astype(f32)) * y[at])
        energy = energy + part * weight[m:m + 1]
    dots[0], dots[1] = squares, energy
    spread(geo, y, weight[...], lambda f, m: diag[f * M + m:f * M + m + 1] * full[f, m], 1.0, image, sends, parity)


def kernel_last(geo, n, partial, diag, weight, schur, dots, r, hxr, hyr, hzr, *refs):
    sent, got, (full,), halos, (message,), (ghi, glo) = take(refs, n, n, 1, 3, 1, 2)
    F, EX, EY, EZ, M = geo.F, geo.EX, geo.EY, geo.EZ, geo.M
    parity, below_top = place()
    completed(geo, partial, sent, got, parity, below_top, full, halos)
    along = None
    for f in range(3):
        for m in range(M):
            along = folded(along, r[f, m] * full[f, m])
    squares = jnp.sum(dots[0], keepdims=True)
    along = jnp.sum(along, keepdims=True)
    shift = jnp.where(squares > 0, jnp.clip(along / squares, -SHIFT_LIMIT, SHIFT_LIMIT), 0.0)
    halo = (lambda j: halos[0][j] - shift * hxr[j], lambda i: halos[1][i] - shift * hyr[i], halos[2][...] - shift * hzr[...])
    y = gather_and_apply(geo, lambda f, m: full[f, m] - shift * r[f, m], halo, schur, ghi, glo)
    rp = pp = erp = epp = None
    for f in range(3):
        for m in range(M):
            v = r[f, m]
            p = full[f, m] - shift * v
            d = diag[f * M + m:f * M + m + 1]
            a, b = folded(None, v * p), folded(None, p * p)
            rp, pp = accumulate(rp, a), accumulate(pp, b)
            erp, epp = accumulate(erp, a * d), accumulate(epp, b * d)
    lanes = lane_iota((F, EZ))
    for m in range(M):
        i, j = divmod(m, EY)
        blocks = [
            r[0, m], r[0, m + EY] if i + 1 < EX else hxr[j],
            r[1, m], r[1, m + 1] if j + 1 < EY else hyr[i],
            r[2, m], jnp.where(lanes == EZ - 1, moved(hzr[...], m, EZ - 1), moved(r[2, m], 1, 0)),
        ]
        one = two = None
        for s, block in enumerate(blocks):
            at = (slice(s * F, (s + 1) * F), slice(m * EZ, (m + 1) * EZ))
            one = folded(one, block * y[at])
            two = folded(two, (ghi[at].astype(f32) + glo[at].astype(f32)) * y[at])
        erp = erp + one * weight[m:m + 1]
        epp = epp + two * weight[m:m + 1]
    lane = lane_iota((1, EZ))
    line = jnp.where(lane == 0, shift, jnp.where(lane == 1, squares, 0.0))
    for k, v in enumerate((rp, pp, dots[1], erp, epp)):
        line = jnp.where(lane == k + 2, jnp.sum(v, keepdims=True), line)
    message[...] = jnp.broadcast_to(line, message.shape)


def step_sizes(rows_of_devices):
    lanes = lane_iota(rows_of_devices.shape)
    theta, rr, rp, pp, err, erp, epp = [jnp.sum(jnp.where(lanes == k, rows_of_devices, 0.0), 1, keepdims=True) for k in range(7)]

    def total(v):
        return jnp.sum(v, 0, keepdims=True)

    old = total(rr)
    alpha = old / total(err)
    u = 1.0 - alpha * theta
    new = total(u * u * rr - 2.0 * u * alpha * rp + alpha * alpha * pp)
    beta = new / old
    c = u + beta
    energy = total(c * c * err - 2.0 * c * alpha * erp + alpha * alpha * epp)
    second = jnp.where(energy > 0, new / energy, 0.0)
    return alpha + second * (1.0 + beta), -alpha * second


def kernel_volume(geo, fields, fine, operator, base, plain, vfields, vfine, voperator, vbase, sems):
    M, EZ = geo.M, geo.EZ
    dofs = operator.shape[0]
    for c in fetch([(fields, vfields), (fine, vfine), (operator, voperator)], sems):
        c.wait()
    plain[...] = vfields[...].astype(f32)
    nodal = [plain[pl.ds(m, dofs, stride=M), :] for m in range(M)]
    volume = jnp.dot(voperator[...], jnp.concatenate([v.astype(bf16) for v in nodal], 1), preferred_element_type=f32)
    coarse = 1.0 - vfine[...].astype(f32)
    for m in range(M):
        vbase[m] = nodal[m] + (TIME_STEP * coarse[m:m + 1]) * volume[:, m * EZ:(m + 1) * EZ]
    copy = pltpu.make_async_copy(vbase, base, sems.at[0])
    copy.start()
    copy.wait()


def kernel_finish(geo, message, trace, base, fine, lift, r, q, *refs):
    (hx, hy, hz), (hxr, hyr, hzr), (hxq, hyq, hzq), (fields_new, trace_new), (g, plain, vbase, sems) = take(refs, 3, 3, 3, 2, 4)
    F, EX, EY, EZ, M = geo.F, geo.EX, geo.EY, geo.EZ, geo.M
    copy = pltpu.make_async_copy(base, vbase, sems.at[0])
    copy.start()
    lanes = lane_iota((F, EZ))
    cr, cq = step_sizes(message[...])
    flag = fine[...].astype(f32)
    z_step = cr * hzr[...] + cq * hzq[...]
    for m in range(M):
        i, j = divmod(m, EY)
        mark = flag[m:m + 1]

        def old_step(f, k):
            return rows(trace, geo, f, k), cr * r[f, k] + cq * q[f, k]

        ox, sx = old_step(0, m)
        oy, sy = old_step(1, m)
        oz, sz = old_step(2, m)
        for f, (o, s) in enumerate(((ox, sx), (oy, sy), (oz, sz))):
            trace_new[pl.ds(f * F * M + m, F, stride=M), :] = o + s
        up_x = old_step(0, m + EY) if i + 1 < EX else (hx[j], cr * hxr[j] + cq * hxq[j])
        up_y = old_step(1, m + 1) if j + 1 < EY else (hy[i], cr * hyr[i] + cq * hyq[i])
        up_z = tuple(jnp.where(lanes == EZ - 1, moved(h, m, EZ - 1), moved(v, 1, 0)) for h, v in ((hz[...], oz), (z_step, sz)))
        for s, (o, step) in enumerate(((ox, sx), up_x, (oy, sy), up_y, (oz, sz), up_z)):
            g[s * F:(s + 1) * F, m * EZ:(m + 1) * EZ] = (o + mark * step).astype(bf16)
    lifted = jnp.dot(lift[...], g[...], preferred_element_type=f32)
    dofs = lift.shape[0]
    copy.wait()
    for m in range(M):
        plain[pl.ds(m, dofs, stride=M), :] = vbase[m] + TIME_STEP * lifted[:, m * EZ:(m + 1) * EZ]
    fields_new[...] = plain[...].astype(bf16)


VMEM, HBM = pltpu.MemorySpace.VMEM, pltpu.MemorySpace.HBM


def call(kernel, outs, args, scratch, flops, hbm_args=(), hbm_outs=()):
    def specs(count, in_hbm):
        return [pl.BlockSpec(memory_space=HBM if k in in_hbm else VMEM) for k in range(count)]

    return pl.pallas_call(
        kernel,
        out_shape=[jax.ShapeDtypeStruct(s, d) for s, d in outs],
        in_specs=specs(len(args), hbm_args),
        out_specs=specs(len(outs), hbm_outs),
        scratch_shapes=scratch,
        cost_estimate=pl.CostEstimate(flops=flops, bytes_accessed=1 << 20, transcendentals=0),
        compiler_params=pltpu.CompilerParams(vmem_limit_bytes=VMEM_GRANT),
    )(*args)


def flat(groups):
    return [v for group in groups for v in group if v is not None]


def like(array):
    return pltpu.VMEM(array.shape, array.dtype)


def body(fields, trace_old, face_load, face_diag, fine_flag, coeff, volume_op, lift_op, schur_op):
    _, F, EX, EY, EZ = trace_old.shape
    geo = Geometry(F, EX, EY, EZ)
    M, dofs, N = geo.M, fields.shape[0], 6 * F
    devices = 1
    for a in AXES:
        devices *= lax.axis_size(a)
    n = counts()
    trace = trace_old.reshape(3 * F * M, EZ)
    load = face_load.reshape(3 * F * M, EZ)
    diag_in = face_diag.reshape(3 * M, EZ)
    fine = fine_flag.reshape(M, EZ)
    scale = coeff.reshape(M, EZ)
    nodal = fields.reshape(dofs * M, EZ)
    slab = [(EY, F, EZ), (EX, F, EZ), (F, EZ)]
    full = (3, M, F, EZ)
    halo_outs = [(s, f32) for s in slab]
    send_outs = [(s, f32) for s, k in zip(slab, n) for _ in range(k)]
    halves = [pltpu.VMEM((N, M * EZ), bf16)] * 2
    flops = 2 * 3 * N * N * M * EZ
    dma = pltpu.SemaphoreType.DMA

    def grouped(values):
        values = list(values)
        return [[values.pop(0) for _ in range(k)] for k in n]

    slabs = call(functools.partial(first_slabs, geo), halo_outs, [trace], [], 1 << 20)
    got = exchange([[s, s] for s in slabs])
    own, diag, weight, schur = call(
        functools.partial(kernel_prepare, geo), [(full, f32), ((3 * M, EZ), f32), ((M, EZ), f32), ((2 * N, N), bf16)],
        [trace, load, diag_in, fine, scale, schur_op], [like(load), like(fine), like(scale), like(schur_op), dma((5,))],
        flops, hbm_args=(1, 2, 3, 4, 5))
    out = call(functools.partial(kernel_start, geo, n), halo_outs + [(full, f32)] + send_outs,
               [trace, own, weight, schur] + flat(got), halves, flops)
    halo_old, partial, sent = out[:3], out[3], grouped(out[4:])
    got = exchange(sent)
    out = call(functools.partial(kernel_middle, geo, n), [(full, f32)] + halo_outs + [(full, f32)] + send_outs + [((2, 8, EZ), f32)],
               [partial, diag, weight, schur] + flat(sent) + flat(got), halves, flops)
    r, halo_r, partial, sent, dots = out[0], out[1:4], out[4], grouped(out[5:-1]), out[-1]
    got = exchange(sent)
    out = call(functools.partial(kernel_last, geo, n), [(full, f32)] + halo_outs + [((devices, EZ), f32)],
               [partial, diag, weight, schur, dots, r, *halo_r] + flat(sent) + flat(got), halves, flops)
    q, halo_q, message = out[0], out[1:4], out[4]
    message = lax.all_to_all(message, AXES, 0, 0, tiled=True)
    base = call(functools.partial(kernel_volume, geo), [((M, dofs, EZ), f32)], [nodal, fine, volume_op],
                [pltpu.VMEM((dofs * M, EZ), f32), like(nodal), like(fine), like(volume_op), pltpu.VMEM((M, dofs, EZ), f32), dma((3,))],
                2 * dofs * dofs * M * EZ, hbm_args=(0, 1, 2), hbm_outs=(0,))[0]
    fields_new, trace_new = call(
        functools.partial(kernel_finish, geo), [((dofs * M, EZ), bf16), ((3 * F * M, EZ), f32)],
        [message, trace, base, fine, lift_op, r, q, *halo_old, *halo_r, *halo_q],
        [pltpu.VMEM((N, M * EZ), bf16), pltpu.VMEM((dofs * M, EZ), f32), pltpu.VMEM((M, dofs, EZ), f32), dma((1,))],
        2 * dofs * N * M * EZ, hbm_args=(2,))
    return fields_new.reshape(fields.shape), trace_new.reshape(trace_old.shape)


def solution(mesh):
    placed = (
        P(None, *AXES), P(None, None, *AXES), P(None, None, *AXES), P(None, *AXES), P(*AXES), P(*AXES), P(), P(), P(),
    )
    return jax.shard_map(body, mesh=mesh, in_specs=placed, out_specs=(P(None, *AXES), P(None, None, *AXES)), check_vma=False)
```

time: 399 us -> 60.2 us (0.15); the launches traced: 394 us -> 59.4 us
  local copies, waits for them, and re-layouts: 175 us -> 14.1 us
  blocking collectives: 121 us -> 0 us
  starting transfers between devices: 66.7 us -> 29.5 us
  other arithmetic: 12.6 us -> 0 us
  Pallas kernels: 0 us -> 7.27 us
  matrix products: 7.08 us -> 0 us
  between operations: 5.72 us -> 0.87 us
    psum x3 -> x0, blocking collectives: 121 us -> none  [the longest x2 82.3 us: squares(): return lax.psum(jnp.sum(residual * residual), ('gx', 'gy', 'gz'))]
    scatter x9 -> x0, local copies, waits for them, and re-layouts: 96.2 us -> none  [the longest x3 33.4 us: upper_extend(): wide = wide.at[1, :, 1:-1, -1:, 1:-1].set(from_y)]
    ppermute x23 -> x15, starting transfers between devices: 66.7 us -> 22.2 us  [exchange(): lax.ppermute(v, axis, pairs(axis, odd))]
    concatenate x38 -> x0, local copies, waits for them, and re-layouts: 20 us -> none  [the longest x28 15.8 us: own_faces(): face_values = jnp.concatenate(pieces, 0)]
    slice x26 -> x0, local copies, waits for them, and re-layouts: 15.6 us -> none  [the longest x4 8.88 us: own_faces(): extended[2, :, 1:span_x + 1, 1:span_y + 1, 2:span_z + 2]]
    squeeze x21 -> x0, local copies, waits for them, and re-layouts: 10.6 us -> none  [the longest x3 1.76 us: owned_coupled(): below_x = from_behind(applied[1][:, -1:], 'gx', 1)]
    pad x3 -> x0, local copies, waits for them, and re-layouts: 7.86 us -> none  [upper_extend(): wide = jnp.pad(values, ((0, 0), (0, 0), (1, 1), (1, 1), (1, 1)))]
    all_to_all x0 -> x1, starting transfers between devices: none -> 7.32 us  [body(): message = lax.all_to_all(message, AXES, 0, 0, tiled=True)]
  transfers between devices with their start and end apart: 23 -> 16, of which waited for: 4 -> 4; matrix products, arithmetic and copies ran while one was open for 15% -> 0% of each run, Pallas kernels for 0% -> 3%
where the time goes in v1:
time: 60.2 us; the launch traced here: 59.4 us
  starting transfers between devices  29.5 us (49%)
  local copies, waits for them, and re-layouts  14.1 us (23%)
  waiting for transfers between devices  7.7 us (13%)
  Pallas kernels  7.27 us (12%)
  between operations  0.87 us (1%)
    ppermute x15, starting transfers between devices, exchange(): lax.ppermute(v, axis, pairs(axis, odd))  22.2 us
    unnamed x47, local copies, waits for them, and re-layouts  14.1 us
    all_to_all x1, starting transfers between devices, body(): message = lax.all_to_all(message, AXES, 0, 0, tiled=True)  7.32 us
    pallas_call x7, Pallas kernels, call(): pl.pallas_call(kernel, out_shape=[jax.ShapeDtypeStruct(s, d) for s, d in...  7.27 us
    all_to_all x1, waiting for transfers between devices, body(): message = lax.all_to_all(message, AXES, 0, 0, tiled=True)  5.01 us
    ppermute x15, waiting for transfers between devices, exchange(): lax.ppermute(v, axis, pairs(axis, odd))  2.69 us
  transfers between devices with their start and end apart: 16, of which 4 were waited for; matrix products, arithmetic and copies ran while one was open for 0% of the time, Pallas kernels for 3%

profile of v1, /device:TPU:0, one launch (start us, length us, event | category | flops | bytes accessed | tf_op | source)
XLA Modules:
  0.0 59.4 jit_solution(11256189146767206578)
XLA Ops:
  0.6 1.0 %copy-done = f32[3,32,2,4,128]{4,3,2,1,0:T(4,128)S(1)} copy-done((f32[3,32,2,4,128]{4,3,2,1,0:T(4,128)S(1)}, f32[3,32,2,4,128]{4,3,2,1,0:T(4,128)}, u32[]{:S(2)}) %copy-start) | copy-done | bytes 393240
  1.7 3.1 %collective-permute-start = (f32[4,32,128]{2,1,0:T(8,128)S(1)}, f32[4,32,128]{2,1,0:T(8,128)S(1)}, u32[]{:S(2)}, u32[]{:S(2)}) collective-permute-start(f32[4,32,128]{2,1,0:T(8,128)S(1)} %get-tuple-element.39), channel_id=1, source_target_pairs={{0,16},{16,0},{1,17},{17,1},{2,18},{18,2},{3,19},{19,3},{4,20},{20... | collective-permute-start | bytes 196616 | tf_op jit(solution)/shard_map/ppermute | solution.py:28
  5.5 4.5 %collective-permute-start.1 = (f32[2,32,128]{2,1,0:T(8,128)S(1)}, f32[2,32,128]{2,1,0:T(8,128)S(1)}, u32[]{:S(2)}, u32[]{:S(2)}) collective-permute-start(f32[2,32,128]{2,1,0:T(8,128)S(1)} %get-tuple-element.40), channel_id=1, source_target_pairs={{0,4},{4,0},{8,12},{12,8},{1,5},{5,1},{9,13},{13,9},{2,6},{6,2},{1... | collective-permute-start | bytes 98312 | tf_op jit(solution)/shard_map/ppermute | solution.py:28
  10.6 2.9 %collective-permute-start.3 = (f32[32,128]{1,0:T(8,128)S(1)}, f32[32,128]{1,0:T(8,128)S(1)}, u32[]{:S(2)}, u32[]{:S(2)}) collective-permute-start(f32[32,128]{1,0:T(8,128)S(1)} %get-tuple-element.41), channel_id=1, source_target_pairs={{0,1},{1,0},{2,3},{3,2},{4,5},{5,4},{6,7},{7,6},{8,9},{9,8},{10,11... | collective-permute-start | bytes 49160 | tf_op jit(solution)/shard_map/ppermute | solution.py:28
  13.5 1.0 %copy-done.5 = f32[3,32,2,4,128]{4,3,2,1,0:T(4,128)S(1)} copy-done((f32[3,32,2,4,128]{4,3,2,1,0:T(4,128)S(1)}, f32[3,32,2,4,128]{4,3,2,1,0:T(4,128)}, u32[]{:S(2)}) %copy-start.5) | copy-done | bytes 393240
  14.5 0.9 %copy-done.7 = f32[192,192]{1,0:T(8,128)S(1)} copy-done((f32[192,192]{1,0:T(8,128)S(1)}, f32[192,192]{1,0:T(8,128)}, u32[]{:S(2)}) %copy-start.7) | copy-done | bytes 147480
  18.2 0.8 %shard_map.106 = (f32[4,32,128]{2,1,0:T(8,128)S(1)}, f32[2,32,128]{2,1,0:T(8,128)S(1)}, f32[32,128]{1,0:T(8,128)S(1)}, f32[3,8,32,128]{3,2,1,0:T(8,128)S(1)}, f3...) custom-call(f32[768,128]{1,0:T(8,128)S(1)} %bitcast.14, ...), custom_call_target="tpu_custom_call" | custom-call | flops 226492416 | bytes 1048576 | tf_op jit(solution)/shard_map/pallas_call | solution.py:382
  22.1 2.0 %collective-permute-done.6.refs_6_ = f32[2,32,128]{2,1,0:T(8,128)S(1)} collective-permute-done((f32[2,32,128]{2,1,0:T(8,128)S(1)}, f32[2,32,128]{2,1,0:T(8,128)S(1)}, u32[]{:S(2)}, u32[]{:S(2)}) %collective-permute-start.6) | collective-permute-done | bytes 32800 | tf_op jit(solution)/shard_map/ppermute | solution.py:28
  24.0 0.8 %shard_map.107 = (f32[3,8,32,128]{3,2,1,0:T(8,128)S(1)}, f32[4,32,128]{2,1,0:T(8,128)S(1)}, f32[2,32,128]{2,1,0:T(8,128)S(1)}, f32[32,128]{1,0:T(8,128)S(1)}, f3...) custom-call(f32[3,8,32,128]{3,2,1,0:T(8,128)S(1)} %get-tuple-element, ...), custom_call_target="tpu_custom_call" | custom-call | flops 226492416 | bytes 1048576 | tf_op jit(solution)/shard_map/pallas_call | solution.py:382
  24.9 1.6 %collective-permute-start.10 = (f32[4,32,128]{2,1,0:T(8,128)S(1)}, f32[4,32,128]{2,1,0:T(8,128)S(1)}, u32[]{:S(2)}, u32[]{:S(2)}) collective-permute-start(f32[4,32,128]{2,1,0:T(8,128)S(1)} %get-tuple-element.55.refs_0_), channel_id=1, source_target_pairs={{0,16},{16,0},{1,17},{17,1},{2,18},{18,2},{3,19},{19,3},{4,20},{20... | collective-permute-start | bytes 196616 | tf_op jit(solution)/shard_map/ppermute | solution.py:28
  26.5 3.9 %collective-permute-start.11 = (f32[2,32,128]{2,1,0:T(8,128)S(1)}, f32[2,32,128]{2,1,0:T(8,128)S(1)}, u32[]{:S(2)}, u32[]{:S(2)}) collective-permute-start(f32[2,32,128]{2,1,0:T(8,128)S(1)} %get-tuple-element.56.refs_1_), channel_id=1, source_target_pairs={{0,4},{4,0},{8,12},{12,8},{1,5},{5,1},{9,13},{13,9},{2,6},{6,2},{1... | collective-permute-start | bytes 98312 | tf_op jit(solution)/shard_map/ppermute | solution.py:28
  31.0 1.7 %collective-permute-start.13 = (f32[32,128]{1,0:T(8,128)S(1)}, f32[32,128]{1,0:T(8,128)S(1)}, u32[]{:S(2)}, u32[]{:S(2)}) collective-permute-start(f32[32,128]{1,0:T(8,128)S(1)} %get-tuple-element.58.refs_3_), channel_id=1, source_target_pairs={{0,1},{1,0},{2,3},{3,2},{4,5},{5,4},{6,7},{7,6},{8,9},{9,8},{10,11... | collective-permute-start | bytes 49160 | tf_op jit(solution)/shard_map/ppermute | solution.py:28
  33.6 1.7 %shard_map.108 = (f32[3,8,32,128]{3,2,1,0:T(8,128)S(1)}, f32[4,32,128]{2,1,0:T(8,128)S(1)}, f32[2,32,128]{2,1,0:T(8,128)S(1)}, f32[32,128]{1,0:T(8,128)S(1)}, f32[32,128]{1,0:T(8,128)}) custom-call(f32[3,8,32,128]{3,2,1,0:T(8,128)S(1)} %get-tuple-element.49.partial, f32[24,128]{1,0:T(8,128)S(1)} %get-tuple-element.43.diag, ...), custom_call_target="tpu_custom_call" | custom-call | flops 226492416 | bytes 1048576 | tf_op jit(solution)/shard_map/pallas_call | solution.py:382
  35.3 0.7 %copy-done.3 = f32[3,8,32,128]{3,2,1,0:T(8,128)} copy-done((f32[3,8,32,128]{3,2,1,0:T(8,128)}, f32[3,8,32,128]{3,2,1,0:T(8,128)S(1)}, u32[]{:S(2)}) %copy-start.3) | copy-done | bytes 393240
  37.8 7.3 %all-to-all-start = ((f32[32,1,128]{2,1,0:T(1,128)}), f32[32,1,128]{2,1,0:T(1,128)S(1)}, u32[]{:S(2)}, u32[]{:S(2)}) async-start(f32[32,1,128]{2,1,0:T(1,128)} %bitcast.6), calls=%async_computation | async-start | bytes 32768 | tf_op jit(solution)/shard_map/all_to_all | solution.py:444
  45.4 1.0 %copy-done.6 = bf16[384,384]{1,0:T(8,128)(2,1)S(1)} copy-done((bf16[384,384]{1,0:T(8,128)(2,1)S(1)}, bf16[384,384]{1,0:T(8,128)(2,1)}, u32[]{:S(2)}) %copy-start.6) | copy-done | bytes 294936
  46.3 1.0 %shard_map.109.base = f32[8,384,128]{2,1,0:T(8,128)S(1)} custom-call(bf16[3072,128]{1,0:T(8,128)(2,1)S(1)} %bitcast.16, s32[8,128]{1,0:T(8,128)S(1)} %bitcast.20, bf16[384,384]{1,0:T(8,128)(2,1)S(1)} %copy-done.6), custom_call_target="tpu_custom_call" | custom-call | flops 301989888 | bytes 1048576 | tf_op jit(solution)/shard_map/pallas_call | solution.py:382
  47.3 5.0 %all-to-all-done = f32[32,1,128]{2,1,0:T(1,128)S(1)} async-done(((f32[32,1,128]{2,1,0:T(1,128)}), f32[32,1,128]{2,1,0:T(1,128)S(1)}, u32[]{:S(2)}, u32[]{:S(2)}) %all-to-all-start) | async-done | bytes 16416 | tf_op jit(solution)/shard_map/all_to_all | solution.py:444
  52.4 1.0 %copy-done.4 = f32[3,8,32,128]{3,2,1,0:T(8,128)S(1)} copy-done((f32[3,8,32,128]{3,2,1,0:T(8,128)S(1)}, f32[3,8,32,128]{3,2,1,0:T(8,128)}, u32[]{:S(2)}) %copy-start.4) | copy-done | bytes 393240
  53.3 0.8 %copy-done.9 = f32[4,32,128]{2,1,0:T(8,128)S(1)} copy-done((f32[4,32,128]{2,1,0:T(8,128)S(1)}, f32[4,32,128]{2,1,0:T(8,128)}, u32[]{:S(2)}) %copy-start.9) | copy-done | bytes 65560
  54.2 0.8 %copy-done.13 = f32[2,32,128]{2,1,0:T(8,128)S(1)} copy-done((f32[2,32,128]{2,1,0:T(8,128)S(1)}, f32[2,32,128]{2,1,0:T(8,128)}, u32[]{:S(2)}) %copy-start.13) | copy-done | bytes 32792
  54.9 0.8 %copy-done.15 = f32[2,32,128]{2,1,0:T(8,128)S(1)} copy-done((f32[2,32,128]{2,1,0:T(8,128)S(1)}, f32[2,32,128]{2,1,0:T(8,128)}, u32[]{:S(2)}) %copy-start.15) | copy-done | bytes 32792
  55.7 0.7 %copy-done.17 = f32[32,128]{1,0:T(8,128)S(1)} copy-done((f32[32,128]{1,0:T(8,128)S(1)}, f32[32,128]{1,0:T(8,128)}, u32[]{:S(2)}) %copy-start.17) | copy-done | bytes 16408
  57.1 2.2 %shard_map.110 = (bf16[3072,128]{1,0:T(8,128)(2,1)}, f32[768,128]{1,0:T(8,128)}) custom-call(f32[32,128]{1,0:T(8,128)S(1)} %bitcast.18, f32[768,128]{1,0:T(8,128)S(1)} %bitcast.15, f32[8,384,128]{2,1,0:T(8,128)S(1)} %shard_map.109.base, s32[8,128]{1,0:T(8,128)S(1)} %bitcast.21, bf16[384,192]{1,0:T(8,128)(2,1)S(1)} %copy.13.lift, ...), custom_call_target="tpu_custom_call" | custom-call | flops 150994944 | bytes 1048576 | tf_op jit(solution)/shard_map/pallas_call | solution.py:382
  (62 shorter events, 11.4 us)
Async XLA Ops:
  0.6 1.0 %copy-start = (f32[3,32,2,4,128]{4,3,2,1,0:T(4,128)S(1)}, f32[3,32,2,4,128]{4,3,2,1,0:T(4,128)}, u32[]{:S(2)}) copy-start(f32[3,32,2,4,128]{4,3,2,1,0:T(4,128)} %param.10) | copy-start | bytes 1179652
  1.7 16.5 %collective-permute-start = (f32[4,32,128]{2,1,0:T(8,128)S(1)}, f32[4,32,128]{2,1,0:T(8,128)S(1)}, u32[]{:S(2)}, u32[]{:S(2)}) collective-permute-start(f32[4,32,128]{2,1,0:T(8,128)S(1)} %get-tuple-element.39), channel_id=1, source_target_pairs={{0,16},{16,0},{1,17},{17,1},{2,18},{18,2},{3,19},{19,3},{4,20},{20... | collective-permute-start | bytes 196616 | tf_op jit(solution)/shard_map/ppermute | solution.py:28
  4.8 13.4 %collective-permute-start.2 = (f32[2,32,128]{2,1,0:T(8,128)S(1)}, f32[2,32,128]{2,1,0:T(8,128)S(1)}, u32[]{:S(2)}, u32[]{:S(2)}) collective-permute-start(f32[2,32,128]{2,1,0:T(8,128)S(1)} %get-tuple-element.40), channel_id=1, source_target_pairs={{4,8},{8,4},{5,9},{9,5},{6,10},{10,6},{7,11},{11,7},{20,24},{24,20... | collective-permute-start | bytes 98312 | tf_op jit(solution)/shard_map/ppermute | solution.py:28
  5.5 12.8 %collective-permute-start.1 = (f32[2,32,128]{2,1,0:T(8,128)S(1)}, f32[2,32,128]{2,1,0:T(8,128)S(1)}, u32[]{:S(2)}, u32[]{:S(2)}) collective-permute-start(f32[2,32,128]{2,1,0:T(8,128)S(1)} %get-tuple-element.40), channel_id=1, source_target_pairs={{0,4},{4,0},{8,12},{12,8},{1,5},{5,1},{9,13},{13,9},{2,6},{6,2},{1... | collective-permute-start | bytes 98312 | tf_op jit(solution)/shard_map/ppermute | solution.py:28
  9.9 8.3 %collective-permute-start.4 = (f32[32,128]{1,0:T(8,128)S(1)}, f32[32,128]{1,0:T(8,128)S(1)}, u32[]{:S(2)}, u32[]{:S(2)}) collective-permute-start(f32[32,128]{1,0:T(8,128)S(1)} %get-tuple-element.41), channel_id=1, source_target_pairs={{1,2},{2,1},{5,6},{6,5},{9,10},{10,9},{13,14},{14,13},{17,18},{18,... | collective-permute-start | bytes 49160 | tf_op jit(solution)/shard_map/ppermute | solution.py:28
  10.6 7.6 %collective-permute-start.3 = (f32[32,128]{1,0:T(8,128)S(1)}, f32[32,128]{1,0:T(8,128)S(1)}, u32[]{:S(2)}, u32[]{:S(2)}) collective-permute-start(f32[32,128]{1,0:T(8,128)S(1)} %get-tuple-element.41), channel_id=1, source_target_pairs={{0,1},{1,0},{2,3},{3,2},{4,5},{5,4},{6,7},{7,6},{8,9},{9,8},{10,11... | collective-permute-start | bytes 49160 | tf_op jit(solution)/shard_map/ppermute | solution.py:28
  13.5 1.0 %copy-start.5 = (f32[3,32,2,4,128]{4,3,2,1,0:T(4,128)S(1)}, f32[3,32,2,4,128]{4,3,2,1,0:T(4,128)}, u32[]{:S(2)}) copy-start(f32[3,32,2,4,128]{4,3,2,1,0:T(4,128)} %param.11) | copy-start | bytes 1179652
  18.2 27.0 %copy-start.22 = (bf16[384,192]{0,1:T(8,128)(2,1)S(1)}, bf16[384,192]{0,1:T(8,128)(2,1)}, u32[]{:S(2)}) copy-start(bf16[384,192]{0,1:T(8,128)(2,1)} %param.16) | copy-start | bytes 442372
  19.6 14.0 %copy-start.12 = (f32[2,32,128]{2,1,0:T(8,128)}, f32[2,32,128]{2,1,0:T(8,128)S(1)}, u32[]{:S(2)}) copy-start(f32[2,32,128]{2,1,0:T(8,128)S(1)} %get-tuple-element.63.refs_1_) | copy-start | bytes 98308
  19.6 25.7 %copy-start.2 = (bf16[384,2,4,128]{3,2,1,0:T(4,128)(2,1)S(1)}, bf16[384,2,4,128]{3,2,1,0:T(4,128)(2,1)}, u32[]{:S(2)}) copy-start(bf16[384,2,4,128]{3,2,1,0:T(4,128)(2,1)} %param.9) | copy-start | bytes 2359300
  19.6 25.7 %copy-start.11 = (s32[2,4,128]{2,1,0:T(4,128)S(1)}, s32[2,4,128]{2,1,0:T(4,128)}, u32[]{:S(2)}) copy-start(s32[2,4,128]{2,1,0:T(4,128)} %param.13) | copy-start | bytes 12292
  19.6 4.4 %collective-permute-start.5 = (f32[4,32,128]{2,1,0:T(8,128)S(1)}, f32[4,32,128]{2,1,0:T(8,128)S(1)}, u32[]{:S(2)}, u32[]{:S(2)}) collective-permute-start(f32[4,32,128]{2,1,0:T(8,128)S(1)} %get-tuple-element.44.refs_0_), channel_id=1, source_target_pairs={{0,16},{16,0},{1,17},{17,1},{2,18},{18,2},{3,19},{19,3},{4,20},{20... | collective-permute-start | bytes 196616 | tf_op jit(solution)/shard_map/ppermute | solution.py:28
  20.1 3.9 %collective-permute-start.6 = (f32[2,32,128]{2,1,0:T(8,128)S(1)}, f32[2,32,128]{2,1,0:T(8,128)S(1)}, u32[]{:S(2)}, u32[]{:S(2)}) collective-permute-start(f32[2,32,128]{2,1,0:T(8,128)S(1)} %get-tuple-element.45.refs_1_), channel_id=1, source_target_pairs={{0,4},{4,0},{8,12},{12,8},{1,5},{5,1},{9,13},{13,9},{2,6},{6,2},{1... | collective-permute-start | bytes 98312 | tf_op jit(solution)/shard_map/ppermute | solution.py:28
  20.2 3.9 %collective-permute-start.7 = (f32[2,32,128]{2,1,0:T(8,128)S(1)}, f32[2,32,128]{2,1,0:T(8,128)S(1)}, u32[]{:S(2)}, u32[]{:S(2)}) collective-permute-start(f32[2,32,128]{2,1,0:T(8,128)S(1)} %get-tuple-element.46.refs_2_), channel_id=1, source_target_pairs={{4,8},{8,4},{5,9},{9,5},{6,10},{10,6},{7,11},{11,7},{20,24},{24,20... | collective-permute-start | bytes 98312 | tf_op jit(solution)/shard_map/ppermute | solution.py:28
  20.8 1.2 %collective-permute-start.8 = (f32[32,128]{1,0:T(8,128)S(1)}, f32[32,128]{1,0:T(8,128)S(1)}, u32[]{:S(2)}, u32[]{:S(2)}) collective-permute-start(f32[32,128]{1,0:T(8,128)S(1)} %get-tuple-element.47.refs_3_), channel_id=1, source_target_pairs={{0,1},{1,0},{2,3},{3,2},{4,5},{5,4},{6,7},{7,6},{8,9},{9,8},{10,11... | collective-permute-start | bytes 49160 | tf_op jit(solution)/shard_map/ppermute | solution.py:28
  20.9 1.2 %collective-permute-start.9 = (f32[32,128]{1,0:T(8,128)S(1)}, f32[32,128]{1,0:T(8,128)S(1)}, u32[]{:S(2)}, u32[]{:S(2)}) collective-permute-start(f32[32,128]{1,0:T(8,128)S(1)} %get-tuple-element.48.refs_4_), channel_id=1, source_target_pairs={{1,2},{2,1},{5,6},{6,5},{9,10},{10,9},{13,14},{14,13},{17,18},{18,... | collective-permute-start | bytes 49160 | tf_op jit(solution)/shard_map/ppermute | solution.py:28
  24.9 8.7 %collective-permute-start.10 = (f32[4,32,128]{2,1,0:T(8,128)S(1)}, f32[4,32,128]{2,1,0:T(8,128)S(1)}, u32[]{:S(2)}, u32[]{:S(2)}) collective-permute-start(f32[4,32,128]{2,1,0:T(8,128)S(1)} %get-tuple-element.55.refs_0_), channel_id=1, source_target_pairs={{0,16},{16,0},{1,17},{17,1},{2,18},{18,2},{3,19},{19,3},{4,20},{20... | collective-permute-start | bytes 196616 | tf_op jit(solution)/shard_map/ppermute | solution.py:28
  26.5 7.1 %collective-permute-start.11 = (f32[2,32,128]{2,1,0:T(8,128)S(1)}, f32[2,32,128]{2,1,0:T(8,128)S(1)}, u32[]{:S(2)}, u32[]{:S(2)}) collective-permute-start(f32[2,32,128]{2,1,0:T(8,128)S(1)} %get-tuple-element.56.refs_1_), channel_id=1, source_target_pairs={{0,4},{4,0},{8,12},{12,8},{1,5},{5,1},{9,13},{13,9},{2,6},{6,2},{1... | collective-permute-start | bytes 98312 | tf_op jit(solution)/shard_map/ppermute | solution.py:28
  30.4 3.2 %collective-permute-start.12 = (f32[2,32,128]{2,1,0:T(8,128)S(1)}, f32[2,32,128]{2,1,0:T(8,128)S(1)}, u32[]{:S(2)}, u32[]{:S(2)}) collective-permute-start(f32[2,32,128]{2,1,0:T(8,128)S(1)} %get-tuple-element.57.refs_2_), channel_id=1, source_target_pairs={{4,8},{8,4},{5,9},{9,5},{6,10},{10,6},{7,11},{11,7},{20,24},{24,20... | collective-permute-start | bytes 98312 | tf_op jit(solution)/shard_map/ppermute | solution.py:28
  31.0 2.5 %collective-permute-start.13 = (f32[32,128]{1,0:T(8,128)S(1)}, f32[32,128]{1,0:T(8,128)S(1)}, u32[]{:S(2)}, u32[]{:S(2)}) collective-permute-start(f32[32,128]{1,0:T(8,128)S(1)} %get-tuple-element.58.refs_3_), channel_id=1, source_target_pairs={{0,1},{1,0},{2,3},{3,2},{4,5},{5,4},{6,7},{7,6},{8,9},{9,8},{10,11... | collective-permute-start | bytes 49160 | tf_op jit(solution)/shard_map/ppermute | solution.py:28
  32.7 0.8 %collective-permute-start.14 = (f32[32,128]{1,0:T(8,128)S(1)}, f32[32,128]{1,0:T(8,128)S(1)}, u32[]{:S(2)}, u32[]{:S(2)}) collective-permute-start(f32[32,128]{1,0:T(8,128)S(1)} %get-tuple-element.59.refs_4_), channel_id=1, source_target_pairs={{1,2},{2,1},{5,6},{6,5},{9,10},{10,9},{13,14},{14,13},{17,18},{18,... | collective-permute-start | bytes 49160 | tf_op jit(solution)/shard_map/ppermute | solution.py:28
  37.8 14.5 %copy-start.1 = (f32[3,32,2,4,128]{4,3,2,1,0:T(4,128)S(1)}, f32[3,32,2,4,128]{4,3,2,1,0:T(4,128)}, u32[]{:S(2)}) copy-start(f32[3,32,2,4,128]{4,3,2,1,0:T(4,128)} %param.10) | copy-start | bytes 1179652
  37.8 14.5 %all-to-all-start = ((f32[32,1,128]{2,1,0:T(1,128)}), f32[32,1,128]{2,1,0:T(1,128)S(1)}, u32[]{:S(2)}, u32[]{:S(2)}) async-start(f32[32,1,128]{2,1,0:T(1,128)} %bitcast.6), calls=%async_computation | async-start | bytes 32768 | tf_op jit(solution)/shard_map/all_to_all | solution.py:444
  52.3 1.0 %copy-start.4 = (f32[3,8,32,128]{3,2,1,0:T(8,128)S(1)}, f32[3,8,32,128]{3,2,1,0:T(8,128)}, u32[]{:S(2)}) copy-start(f32[3,8,32,128]{3,2,1,0:T(8,128)} %copy-done.3) | copy-start | bytes 1179652
  (15 other events, 10.9 us)

commit v2 on v1

v2 whole, which is shorter than its diff:
```python
import functools

import jax
import jax.numpy as jnp
from jax import lax
from jax.experimental import pallas as pl
from jax.experimental.pallas import tpu as pltpu
from jax.sharding import PartitionSpec as P

AXES = ("gx", "gy", "gz")
TIME_STEP = 0.25
SHIFT_LIMIT = 1e4
PARTS = 4
STRIDE = 8
VMEM_GRANT = 12 * 1024 * 1024
f32, bf16 = jnp.float32, jnp.bfloat16


def pairs(axis, odd):
    size = lax.axis_size(axis)
    route = []
    for i in range(odd, size - 1, 2):
        route += [(i, i + 1), (i + 1, i)]
    return route


def exchange(axes, sends):
    return [[lax.ppermute(v, axis, pairs(axis, odd)) for odd, v in enumerate(s) if pairs(axis, odd)] for axis, s in zip(axes, sends)]


def counts():
    return [sum(bool(pairs(axis, odd)) for odd in (0, 1)) for axis in AXES]


def lane_iota(shape):
    return lax.broadcasted_iota(jnp.int32, shape, len(shape) - 1)


def moved(value, source, target):
    width = value.shape[-1]
    shift = (target - source) % width
    return pltpu.roll(value, shift, value.ndim - 1) if shift else value


def place():
    index = [lax.axis_index(a) for a in AXES]
    parity = [lax.rem(i, 2) for i in index]
    below_top = [(i < lax.axis_size(a) - 1).astype(f32) for i, a in zip(index, AXES)]
    return parity, below_top


def split(value):
    high = value.astype(bf16)
    return high, (value - high.astype(f32)).astype(bf16)


class Geometry:
    def __init__(self, F, EX, EY, EZ):
        self.F, self.EX, self.EY, self.EZ = F, EX, EY, EZ
        self.M = EX * EY


def at_rows(geo, s, m):
    return slice(s * geo.F, (s + 1) * geo.F), slice(m * geo.EZ, (m + 1) * geo.EZ)


def lanes_of(geo):
    lane = lane_iota((geo.F, geo.EZ))
    return lane, lane % STRIDE, lane // (STRIDE * geo.EY), (lane // STRIDE) % geo.EY


def z_above(geo, z_own, z_pack, m):
    lane = lane_iota((geo.F, geo.EZ))
    return jnp.where(lane == geo.EZ - 1, moved(z_pack, m * STRIDE + 2, geo.EZ - 1), moved(z_own, 1, 0))


def gather_and_apply(geo, own, halo, schur, ghi, glo, wide=None):
    F, EX, EY, EZ, M = geo.F, geo.EX, geo.EY, geo.EZ, geo.M
    hx, hy, hz = halo

    def put(m, blocks):
        for s, block in enumerate(blocks):
            high, low = split(block)
            ghi[at_rows(geo, s, m)] = high
            glo[at_rows(geo, s, m)] = low

    bottom = jnp.zeros((F, EZ), f32)
    lane, column, at_i, at_j = lanes_of(geo)
    for m in range(M):
        i, j = divmod(m, EY)
        z_own = own(2, m)
        put(m, [
            own(0, m), own(0, m + EY) if i + 1 < EX else hx(j),
            own(1, m), own(1, m + 1) if j + 1 < EY else hy(i),
            z_own, z_above(geo, z_own, hz, m),
        ])
        if wide:
            bottom = jnp.where(lane == m * STRIDE + 1, moved(z_own, 0, m * STRIDE + 1), bottom)
    if wide:
        x, y, hx_pack, hy_pack = wide
        put(M, [
            x, jnp.where(at_i == EX - 1, moved(hx_pack, 0, (EX - 1) * EY * STRIDE), moved(x, EY * STRIDE, 0)),
            y, jnp.where(at_j == EY - 1, moved(hy_pack, 0, (EY - 1) * STRIDE), moved(y, STRIDE, 0)),
            hz, jnp.where(column == 1, bottom, moved(hz, 1, 0)),
        ])
    n = 6 * F
    both = jnp.dot(schur[...], ghi[...], preferred_element_type=f32)
    return both[:n] + (both[n:] + jnp.dot(schur[:n], glo[...], preferred_element_type=f32))


def spread(geo, y, weight, own_term, sign, out, sends, parity, weight_pack, own_pack, pack_out):
    F, EX, EY, EZ, M = geo.F, geo.EX, geo.EY, geo.EZ, geo.M
    lane, column, at_i, at_j = lanes_of(geo)
    wrow = [weight[m:m + 1] * sign for m in range(M)] + [weight_pack * sign]

    def block(s, m):
        return y[at_rows(geo, s, m)] * wrow[m]

    low = {}
    below = block(5, M)
    top = jnp.zeros((F, EZ), f32)
    for m in range(M):
        i, j = divmod(m, EY)
        vx = own_term(0, m) + block(0, m)
        if i > 0:
            vx = vx + block(1, m - EY)
        else:
            low[0, j] = vx
        out[0, m] = vx
        vy = own_term(1, m) + block(2, m)
        if j > 0:
            vy = vy + block(3, m - 1)
        else:
            low[1, i] = vy
        out[1, m] = vy
        up = block(5, m)
        out[2, m] = own_term(2, m) + block(4, m) + jnp.where(lane == 0, moved(below, m * STRIDE + 1, 0), moved(up, 0, 1))
        top = jnp.where(lane == m * STRIDE + 2, moved(up, EZ - 1, m * STRIDE + 2), top)
    shared = [
        [(low[0, j], block(1, (EX - 1) * EY + j)) for j in range(EY)],
        [(low[1, i], block(3, i * EY + EY - 1)) for i in range(EX)],
    ]
    pack_out[2][...] = own_pack(2) + block(4, M) + jnp.where(column == 2, top, moved(below, 0, 1))
    if 0 in pack_out:
        up = block(1, M)
        v = own_pack(0) + block(0, M)
        pack_out[0][...] = v + jnp.where(at_i > 0, moved(up, 0, EY * STRIDE), 0.0)
        shared[0].append((v, moved(up, (EX - 1) * EY * STRIDE, 0)))
        up = block(3, M)
        v = own_pack(1) + block(2, M)
        pack_out[1][...] = v + jnp.where(at_j > 0, moved(up, 0, STRIDE), 0.0)
        shared[1].append((v, moved(up, (EY - 1) * STRIDE, 0)))
    for a in (0, 1):
        for odd, ref in enumerate(sends[a]):
            for k, (bottom, high) in enumerate(shared[a]):
                ref[k] = jnp.where(parity[a] == odd, high, bottom)


def chosen(refs, parity, read, flip=False):
    values = [read(r) for r in refs]
    if not values:
        return None
    if len(values) == 1:
        values.append(jnp.zeros_like(values[0]))
    first, second = (values[1], values[0]) if flip else values
    return jnp.where(parity == 0, first, second)


def completed(geo, partial, sent, got, parity, below_top, full, halos):
    F, EX, EY, EZ, M = geo.F, geo.EX, geo.EY, geo.EZ, geo.M
    for f in range(3):
        for m in range(M):
            i, j = divmod(m, EY)
            v = partial[f, m]
            if f == 0 and i == 0 and got[0]:
                v = v + chosen(got[0], parity[0], lambda r: r[j], True)
            if f == 1 and j == 0 and got[1]:
                v = v + chosen(got[1], parity[1], lambda r: r[i], True)
            full[f, m] = v
    for a, n in ((0, EY), (1, EX)):
        for k in range(n):
            halos[a][k] = both_sides(geo, sent[a], got[a], parity[a], below_top[a], k)


def both_sides(geo, sent, got, parity, below_top, k):
    if not got:
        return jnp.zeros((geo.F, geo.EZ), f32)
    return (chosen(sent, parity, lambda r: r[k]) + chosen(got, parity, lambda r: r[k])) * below_top


def folded(total, value):
    v = value.reshape(value.shape[0] // 8, 8, value.shape[1]).sum(0)
    return v if total is None else total + v


def rows(ref, geo, f, m):
    return ref[pl.ds(f * geo.F * geo.M + m, geo.F, stride=geo.M), :]


def kernel_pack(geo, trace, load, diag, fine, coeff, pack, vtrace, vload, vdiag, vfine, vcoeff, sems):
    F, EZ, M = geo.F, geo.EZ, geo.M
    for c in fetch([(trace, vtrace), (load, vload), (diag, vdiag), (fine, vfine), (coeff, vcoeff)], sems):
        c.wait()
    half = EZ // 2

    def packed(parts):
        shape = parts[0].shape
        lane = lane_iota(shape)
        out = jnp.zeros(shape, f32)
        for m, part in enumerate(parts):
            start = (m // M) * half + (m % M) * STRIDE
            out = jnp.where((lane >= start) & (lane < start + 5), moved(part, 0, start + 2), out)
        return out

    for f in range(3):
        pack[f * F:(f + 1) * F] = packed([rows(v, geo, f, m) for v in (vtrace, vload) for m in range(M)])
    weight = vfine[...].astype(f32) * vcoeff[...]
    lines = [packed([vdiag[f * M + m:f * M + m + 1] for m in range(M)]) for f in range(3)]
    lines.append(packed([weight[m:m + 1] for m in range(M)]))
    for k in range(8):
        pack[3 * F + k:3 * F + k + 1] = lines[min(k, 3)]


def kernel_wide(geo, n, trace, _, *refs):
    got, (trace_pack, own_pack, lines, sx, sy) = take(refs, n[2:], 5)
    F, EX, EY, EZ = geo.F, geo.EX, geo.EY, geo.EZ
    parity, _ = place()
    lane = lane_iota((F, EZ))

    def mixed(rows_at):
        if not got[0]:
            return jnp.zeros((F, EZ), f32)[:rows_at.stop - rows_at.start]
        below = chosen(got[0], parity[2], lambda r: r[rows_at], True)
        above = chosen(got[0], parity[2], lambda r: r[rows_at])
        return jnp.where(lane[:below.shape[0]] % STRIDE < 2, below, above)

    lines[...] = mixed(slice(3 * F, 3 * F + 8))
    for f in range(3):
        v = mixed(slice(f * F, (f + 1) * F))
        old = jnp.where(lane < EZ // 2, v, 0.0)
        load = jnp.where(lane < EZ // 2, moved(v, EZ // 2, 0), 0.0)
        trace_pack[f] = old
        own_pack[f] = load - lines[f:f + 1] * old
        if f == 0:
            for j in range(EY):
                sx[j] = rows(trace, geo, 0, j)
            sx[EY] = old
        if f == 1:
            for i in range(EX):
                sy[i] = rows(trace, geo, 1, i * EY)
            sy[EX] = old


def take(refs, *sizes):
    refs = list(refs)
    out = []
    for s in sizes:
        if isinstance(s, (list, tuple)):
            group = []
            for n in s:
                group.append([refs.pop(0) for _ in range(n)])
            out.append(group)
        else:
            out.append([refs.pop(0) for _ in range(s)])
    assert not refs
    return out


def fetch(pairs, sems):
    copies = [pltpu.make_async_copy(src, dst, sems.at[k]) for k, (src, dst) in enumerate(pairs)]
    for c in copies:
        c.start()
    return copies


def kernel_prepare(geo, trace, load, diag_in, fine, coeff, schur, own, diag, weight, matrix, vload, vfine, vcoeff, vschur, sems):
    copies = fetch([(load, vload), (diag_in, diag), (fine, vfine), (coeff, vcoeff), (schur, vschur)], sems)
    for c in copies:
        c.wait()
    weight[...] = vfine[...].astype(f32) * vcoeff[...]
    n = 6 * geo.F
    matrix[:n], matrix[n:] = split(vschur[...])
    for f in range(3):
        for m in range(geo.M):
            own[f, m] = rows(vload, geo, f, m) - diag[f * geo.M + m:f * geo.M + m + 1] * rows(trace, geo, f, m)


def kernel_start(geo, n, trace, own, weight, schur, trace_pack, own_pack, lines, *refs):
    got, halos, (partial, partial_pack), sends, (ghi, glo) = take(refs, n[:2], 2, 2, n[:2], 2)
    F, EX, EY, EZ = geo.F, geo.EX, geo.EY, geo.EZ
    parity, _ = place()

    def above(a, k):
        return chosen(got[a], parity[a], lambda r: r[k]) if got[a] else jnp.zeros((F, EZ), f32)

    for a, count in ((0, EY), (1, EX)):
        for k in range(count):
            halos[a][k] = above(a, k)
    halo = (lambda j: halos[0][j], lambda i: halos[1][i], trace_pack[2])
    wide = (trace_pack[0], trace_pack[1], above(0, EY), above(1, EX))
    y = gather_and_apply(geo, lambda f, m: rows(trace, geo, f, m), halo, schur, ghi, glo, wide)
    spread(geo, y, weight[...], lambda f, m: own[f, m], -1.0, partial, sends, parity,
           lines[3:4], lambda f: own_pack[f], {f: partial_pack.at[f] for f in range(3)})


def accumulate(total, value):
    return value if total is None else total + value


def kernel_middle(geo, n, partial, partial_pack, diag, weight, schur, lines, *refs):
    sent, got, (full, full_z), halos, (image, image_z), sends, (dots,), (ghi, glo) = take(refs, n[:2], n[:2], 2, 2, 2, n[:2], 1, 2)
    F, EX, EY, EZ, M = geo.F, geo.EX, geo.EY, geo.EZ, geo.M
    parity, below_top = place()
    completed(geo, partial, sent, got, parity, below_top, full, halos)
    lane, column, at_i, at_j = lanes_of(geo)
    packs = []
    for a, edge, count in ((0, at_i == 0, EY), (1, at_j == 0, EX)):
        v = partial_pack[a]
        if got[a]:
            v = v + jnp.where(edge, chosen(got[a], parity[a], lambda r: r[count], True), 0.0)
        packs.append(v)
    wide = (*packs, both_sides(geo, sent[0], got[0], parity[0], below_top[0], EY), both_sides(geo, sent[1], got[1], parity[1], below_top[1], EX))
    full_z[...] = jnp.where(column < 2, partial_pack[2], partial_pack[2] * below_top[2])
    halo = (lambda j: halos[0][j], lambda i: halos[1][i], full_z[...])
    y = gather_and_apply(geo, lambda f, m: full[f, m], halo, schur, ghi, glo, wide)
    squares = energy = None
    for f in range(3):
        for m in range(M):
            vv = folded(None, full[f, m] * full[f, m])
            squares = accumulate(squares, vv)
            energy = accumulate(energy, vv * diag[f * M + m:f * M + m + 1])
    for m in range(M):
        part = None
        for s in range(6):
            at = at_rows(geo, s, m)
            part = folded(part, (ghi[at].astype(f32) + glo[at].astype(f32)) * y[at])
        energy = energy + part * weight[m:m + 1]
    dots[0], dots[1] = squares, energy
    spread(geo, y, weight[...], lambda f, m: diag[f * M + m:f * M + m + 1] * full[f, m], 1.0, image, sends, parity,
           lines[3:4], lambda f: lines[f:f + 1] * full_z[...], {2: image_z})
    image_z[...] = image_z[...] * below_top[2]


def kernel_last(geo, n, partial, image_z, diag, weight, schur, dots, r, hxr, hyr, hzr, *refs):
    sent, got, (full,), halos, (message,), (ghi, glo) = take(refs, n[:2], n[:2], 1, 2, 1, 2)
    F, EX, EY, EZ, M = geo.F, geo.EX, geo.EY, geo.EZ, geo.M
    parity, below_top = place()
    completed(geo, partial, sent, got, parity, below_top, full, halos)
    along = None
    for f in range(3):
        for m in range(M):
            along = folded(along, r[f, m] * full[f, m])
    squares = jnp.sum(dots[0], keepdims=True)
    along = jnp.sum(along, keepdims=True)
    shift = jnp.where(squares > 0, jnp.clip(along / squares, -SHIFT_LIMIT, SHIFT_LIMIT), 0.0)
    halo = (lambda j: halos[0][j] - shift * hxr[j], lambda i: halos[1][i] - shift * hyr[i], image_z[...] - shift * hzr[...])
    y = gather_and_apply(geo, lambda f, m: full[f, m] - shift * r[f, m], halo, schur, ghi, glo)
    rp = pp = erp = epp = None
    for f in range(3):
        for m in range(M):
            v = r[f, m]
            p = full[f, m] - shift * v
            d = diag[f * M + m:f * M + m + 1]
            a, b = folded(None, v * p), folded(None, p * p)
            rp, pp = accumulate(rp, a), accumulate(pp, b)
            erp, epp = accumulate(erp, a * d), accumulate(epp, b * d)
    for m in range(M):
        i, j = divmod(m, EY)
        blocks = [
            r[0, m], r[0, m + EY] if i + 1 < EX else hxr[j],
            r[1, m], r[1, m + 1] if j + 1 < EY else hyr[i],
            r[2, m], z_above(geo, r[2, m], hzr[...], m),
        ]
        one = two = None
        for s, block in enumerate(blocks):
            at = at_rows(geo, s, m)
            one = folded(one, block * y[at])
            two = folded(two, (ghi[at].astype(f32) + glo[at].astype(f32)) * y[at])
        erp = erp + one * weight[m:m + 1]
        epp = epp + two * weight[m:m + 1]
    lane = lane_iota((1, EZ))
    line = jnp.where(lane == 0, shift, jnp.where(lane == 1, squares, 0.0))
    for k, v in enumerate((rp, pp, dots[1], erp, epp)):
        line = jnp.where(lane == k + 2, jnp.sum(v, keepdims=True), line)
    message[...] = jnp.broadcast_to(line, message.shape)


def step_sizes(rows_of_devices):
    lanes = lane_iota(rows_of_devices.shape)
    theta, rr, rp, pp, err, erp, epp = [jnp.sum(jnp.where(lanes == k, rows_of_devices, 0.0), 1, keepdims=True) for k in range(7)]

    def total(v):
        return jnp.sum(v, 0, keepdims=True)

    old = total(rr)
    alpha = old / total(err)
    u = 1.0 - alpha * theta
    new = total(u * u * rr - 2.0 * u * alpha * rp + alpha * alpha * pp)
    beta = new / old
    c = u + beta
    energy = total(c * c * err - 2.0 * c * alpha * erp + alpha * alpha * epp)
    second = jnp.where(energy > 0, new / energy, 0.0)
    return alpha + second * (1.0 + beta), -alpha * second


def kernel_volume(geo, fields, fine, operator, base, plain, vfields, vfine, voperator, sems):
    M, EZ = geo.M, geo.EZ
    dofs = operator.shape[0]
    for c in fetch([(fields, vfields), (fine, vfine), (operator, voperator)], sems):
        c.wait()
    plain[...] = vfields[...].astype(f32)
    nodal = [plain[pl.ds(m, dofs, stride=M), :] for m in range(M)]
    volume = jnp.dot(voperator[...], jnp.concatenate([v.astype(bf16) for v in nodal], 1), preferred_element_type=f32)
    coarse = 1.0 - vfine[...].astype(f32)
    for m in range(M):
        base[m] = nodal[m] + (TIME_STEP * coarse[m:m + 1]) * volume[:, m * EZ:(m + 1) * EZ]


def kernel_finish(geo, message, trace, base, fine, lift, r, q, *refs):
    (hx, hy, hz), (hxr, hyr, hzr), (hxq, hyq, hzq), (fields_out, trace_out), (g, plain, fields_new, trace_new, sems) = take(refs, 3, 3, 3, 2, 5)
    F, EX, EY, EZ, M = geo.F, geo.EX, geo.EY, geo.EZ, geo.M
    cr, cq = step_sizes(message[...])
    flag = fine[...].astype(f32)
    z_step = cr * hzr[...] + cq * hzq[...]
    for m in range(M):
        i, j = divmod(m, EY)
        mark = flag[m:m + 1]

        def old_step(f, k):
            return rows(trace, geo, f, k), cr * r[f, k] + cq * q[f, k]

        ox, sx = old_step(0, m)
        oy, sy = old_step(1, m)
        oz, sz = old_step(2, m)
        for f, (o, s) in enumerate(((ox, sx), (oy, sy), (oz, sz))):
            trace_new[pl.ds(f * F * M + m, F, stride=M), :] = o + s
        up_x = old_step(0, m + EY) if i + 1 < EX else (hx[j], cr * hxr[j] + cq * hxq[j])
        up_y = old_step(1, m + 1) if j + 1 < EY else (hy[i], cr * hyr[i] + cq * hyq[i])
        up_z = (z_above(geo, oz, hz[2], m), z_above(geo, sz, z_step, m))
        for s, (o, step) in enumerate(((ox, sx), up_x, (oy, sy), up_y, (oz, sz), up_z)):
            g[s * F:(s + 1) * F, m * EZ:(m + 1) * EZ] = (o + mark * step).astype(bf16)
    copies = [pltpu.make_async_copy(trace_new, trace_out, sems.at[0])]
    copies[0].start()
    dofs = lift.shape[0]
    part = dofs // PARTS
    for k in range(PARTS):
        lifted = jnp.dot(lift[k * part:(k + 1) * part], g[...], preferred_element_type=f32)
        for m in range(M):
            plain[pl.ds(k * part * M + m, part, stride=M), :] = base[m, k * part:(k + 1) * part] + TIME_STEP * lifted[:, m * EZ:(m + 1) * EZ]
        some = pl.ds(k * part * M, part * M)
        fields_new[some] = plain[some].astype(bf16)
        copies.append(pltpu.make_async_copy(fields_new.at[some], fields_out.at[some], sems.at[k + 1]))
        copies[-1].start()
    for c in copies:
        c.wait()


VMEM, HBM = pltpu.MemorySpace.VMEM, pltpu.MemorySpace.HBM


def call(kernel, outs, args, scratch, flops, hbm_args=(), hbm_outs=()):
    def specs(count, in_hbm):
        return [pl.BlockSpec(memory_space=HBM if k in in_hbm else VMEM) for k in range(count)]

    args = [pltpu.with_memory_space_constraint(v, HBM) if k in hbm_args else v for k, v in enumerate(args)]
    return pl.pallas_call(
        kernel,
        out_shape=[(HBM if k in hbm_outs else jax.ShapeDtypeStruct)(s, d) for k, (s, d) in enumerate(outs)],
        in_specs=specs(len(args), hbm_args),
        out_specs=specs(len(outs), hbm_outs),
        scratch_shapes=scratch,
        cost_estimate=pl.CostEstimate(flops=flops, bytes_accessed=1 << 20, transcendentals=0),
        compiler_params=pltpu.CompilerParams(vmem_limit_bytes=VMEM_GRANT),
    )(*args)


def flat(groups):
    return [v for group in groups for v in group if v is not None]


def like(array):
    return pltpu.VMEM(array.shape, array.dtype)


def body(fields, trace_old, face_load, face_diag, fine_flag, coeff, volume_op, lift_op, schur_op):
    _, F, EX, EY, EZ = trace_old.shape
    geo = Geometry(F, EX, EY, EZ)
    M, dofs, N = geo.M, fields.shape[0], 6 * F
    devices = 1
    for a in AXES:
        devices *= lax.axis_size(a)
    n = counts()
    trace = trace_old.reshape(3 * F * M, EZ)
    load = face_load.reshape(3 * F * M, EZ)
    diag_in = face_diag.reshape(3 * M, EZ)
    fine = fine_flag.reshape(M, EZ)
    scale = coeff.reshape(M, EZ)
    nodal = fields.reshape(dofs * M, EZ)
    slab = [(EY, F, EZ), (EX, F, EZ)]
    slab_wide = [(EY + 1, F, EZ), (EX + 1, F, EZ)]
    full, pack, line = (3, M, F, EZ), (3, F, EZ), (8, EZ)
    halo_outs = [(s, f32) for s in slab]
    flops = 2 * 3 * N * N * M * EZ
    dma = pltpu.SemaphoreType.DMA

    def halves(blocks):
        return [pltpu.VMEM((N, blocks * EZ), bf16)] * 2

    def send_outs(shapes):
        return [(s, f32) for s, k in zip(shapes, n) for _ in range(k)]

    def grouped(values):
        values = list(values)
        return [[values.pop(0) for _ in range(k)] for k in n[:2]]

    packed, held = call(functools.partial(kernel_pack, geo), [((3 * F + 8, EZ), f32), (trace.shape, f32)], [trace, load, diag_in, fine, scale],
                        [like(load), like(diag_in), like(fine), like(scale), dma((5,))], 1 << 20, hbm_args=range(5))
    got = exchange(AXES[2:], [[packed, packed]])
    own, diag, weight, schur = call(
        functools.partial(kernel_prepare, geo), [(full, f32), ((3 * M, EZ), f32), ((M, EZ), f32), ((2 * N, N), bf16)],
        [held, load, diag_in, fine, scale, schur_op], [like(load), like(fine), like(scale), like(schur_op), dma((5,))],
        flops, hbm_args=(1, 2, 3, 4, 5))
    trace_pack, own_pack, lines, sx, sy = call(
        functools.partial(kernel_wide, geo, n), [(pack, f32), (pack, f32), (line, f32)] + [(s, f32) for s in slab_wide],
        [held, weight] + flat(got), [], 1 << 20)
    got = exchange(AXES[:2], [[sx, sx], [sy, sy]])
    out = call(functools.partial(kernel_start, geo, n), halo_outs + [(full, f32), (pack, f32)] + send_outs(slab_wide),
               [held, own, weight, schur, trace_pack, own_pack, lines] + flat(got), halves(M + 1), flops)
    halo_old, partial, partial_pack, sent = [*out[:2], trace_pack], out[2], out[3], grouped(out[4:])
    got = exchange(AXES[:2], sent)
    out = call(functools.partial(kernel_middle, geo, n),
               [(full, f32), ((F, EZ), f32)] + halo_outs + [(full, f32), ((F, EZ), f32)] + send_outs(slab) + [((2, 8, EZ), f32)],
               [partial, partial_pack, diag, weight, schur, lines] + flat(sent) + flat(got), halves(M + 1), flops)
    r, r_z, partial, image_z, sent, dots = out[0], out[1], out[4], out[5], grouped(out[6:-1]), out[-1]
    halo_r = [*out[2:4], r_z]
    got = exchange(AXES[:2], sent)
    out = call(functools.partial(kernel_last, geo, n), [(full, f32)] + halo_outs + [((devices, EZ), f32)],
               [partial, image_z, diag, weight, schur, dots, r, *halo_r] + flat(sent) + flat(got), halves(M), flops)
    q, halo_q, message = out[0], [*out[1:3], image_z], out[3]
    message = lax.all_to_all(message, AXES, 0, 0, tiled=True)
    base = call(functools.partial(kernel_volume, geo), [((M, dofs, EZ), f32)], [nodal, fine, volume_op],
                [pltpu.VMEM((dofs * M, EZ), f32), like(nodal), like(fine), like(volume_op), dma((3,))],
                2 * dofs * dofs * M * EZ, hbm_args=(0, 1, 2))[0]
    fields_new, trace_new = call(
        functools.partial(kernel_finish, geo), [((dofs * M, EZ), bf16), ((3 * F * M, EZ), f32)],
        [message, trace, base, fine, lift_op, r, q, *halo_old, *halo_r, *halo_q],
        [pltpu.VMEM((N, M * EZ), bf16), pltpu.VMEM((dofs * M, EZ), f32), like(nodal), like(trace), dma((PARTS + 1,))],
        2 * dofs * N * M * EZ, hbm_outs=(0, 1))
    return fields_new.reshape(fields.shape), trace_new.reshape(trace_old.shape)


def solution(mesh):
    placed = (
        P(None, *AXES), P(None, None, *AXES), P(None, None, *AXES), P(None, *AXES), P(*AXES), P(*AXES), P(), P(), P(),
    )
    return jax.shard_map(body, mesh=mesh, in_specs=placed, out_specs=(P(None, *AXES), P(None, None, *AXES)), check_vma=False)
```

time: 60.2 us -> 47.5 us (0.79)
  local copies, waits for them, and re-layouts: 14.1 us -> 0.15 us
  starting transfers between devices: 29.5 us -> 26.9 us
  Pallas kernels: 7.27 us -> 9.71 us
  waiting for transfers between devices: 7.7 us -> 9.67 us
    unnamed x47 -> x7, local copies, waits for them, and re-layouts: 14.1 us -> 0.15 us
    pallas_call x7 -> x8, Pallas kernels: 7.27 us -> 9.71 us  [call(): pl.pallas_call(kernel, out_shape=[(HBM if k in hbm_outs else jax.ShapeDty...]
    ppermute x15 -> x11, waiting for transfers between devices: 2.69 us -> 4.73 us  [exchange(): lax.ppermute(v, axis, pairs(axis, odd))]
    all_to_all x1, starting transfers between devices: 7.32 us -> 5.74 us  [body(): message = lax.all_to_all(message, AXES, 0, 0, tiled=True)]
    ppermute x15 -> x11, starting transfers between devices: 22.2 us -> 21.1 us  [exchange(): lax.ppermute(v, axis, pairs(axis, odd))]
  transfers between devices with their start and end apart: 16 -> 12, of which waited for: 4 -> 4; matrix products, arithmetic and copies ran while one was open for 0% -> 0% of each run, Pallas kernels for 3% -> 7%
where the time goes in v2:
time: 47.5 us; the launch traced here: 47.2 us
  starting transfers between devices  26.9 us (57%)
  Pallas kernels  9.71 us (20%)
  waiting for transfers between devices  9.67 us (20%)
  between operations  0.75 us (2%)
    ppermute x11, starting transfers between devices, exchange(): lax.ppermute(v, axis, pairs(axis, odd))  21.1 us
    pallas_call x8, Pallas kernels, call(): pl.pallas_call(kernel, out_shape=[(HBM if k in hbm_outs else jax.ShapeDty...  9.71 us
    all_to_all x1, starting transfers between devices, body(): message = lax.all_to_all(message, AXES, 0, 0, tiled=True)  5.74 us
    all_to_all x1, waiting for transfers between devices, body(): message = lax.all_to_all(message, AXES, 0, 0, tiled=True)  4.94 us
    ppermute x11, waiting for transfers between devices, exchange(): lax.ppermute(v, axis, pairs(axis, odd))  4.73 us
  transfers between devices with their start and end apart: 12, of which 4 were waited for; matrix products, arithmetic and copies ran while one was open for 0% of the time, Pallas kernels for 7%

profile of v2, /device:TPU:0, one launch (start us, length us, event | category | flops | bytes accessed | tf_op | source)
XLA Modules:
  0.0 47.2 jit_solution(15882844777409188655)
XLA Ops:
  0.6 1.5 %shard_map.104 = (f32[104,128]{1,0:T(8,128)S(1)}, f32[768,128]{1,0:T(8,128)S(1)}) custom-call(f32[768,128]{1,0:T(8,128)} %bitcast.12, f32[768,128]{1,0:T(8,128)} %bitcast.19, f32[24,128]{1,0:T(8,128)} %bitcast.22, s32[8,128]{1,0:T(8,128)} %bitcast.14, f32[8,128]{1,0:T(8,128)} %bitcast.24), custom_call_target="tpu_custom_call" | custom-call | flops 1048576 | bytes 1048576 | tf_op jit(solution)/shard_map/pallas_call | solution.py:466
  2.1 0.7 %collective-permute-start.1 = (f32[104,128]{1,0:T(8,128)S(1)}, f32[104,128]{1,0:T(8,128)S(1)}, u32[]{:S(2)}, u32[]{:S(2)}) collective-permute-start(f32[104,128]{1,0:T(8,128)S(1)} %get-tuple-element.40), channel_id=1, source_target_pairs={{1,2},{2,1},{5,6},{6,5},{9,10},{10,9},{13,14},{14,13},{17,18},{18,... | collective-permute-start | bytes 159752 | tf_op jit(solution)/shard_map/ppermute | solution.py:28
  2.8 4.4 %collective-permute-start = (f32[104,128]{1,0:T(8,128)S(1)}, f32[104,128]{1,0:T(8,128)S(1)}, u32[]{:S(2)}, u32[]{:S(2)}) collective-permute-start(f32[104,128]{1,0:T(8,128)S(1)} %get-tuple-element.40), channel_id=1, source_target_pairs={{0,1},{1,0},{2,3},{3,2},{4,5},{5,4},{6,7},{7,6},{8,9},{9,8},{10,11... | collective-permute-start | bytes 159752 | tf_op jit(solution)/shard_map/ppermute | solution.py:28
  7.2 1.3 %shard_map.105 = (f32[3,8,32,128]{3,2,1,0:T(8,128)S(1)}, f32[24,128]{1,0:T(8,128)S(1)}, f32[8,128]{1,0:T(8,128)S(1)}, bf16[384,192]{1,0:T(8,128)(2,1)S(1)}) custom-call(f32[768,128]{1,0:T(8,128)S(1)} %get-tuple-element.36.trace, f32[768,128]{1,0:T(8,128)} %bitcast.20, f32[24,128]{1,0:T(8,128)} %bitcast.23, s32[8,128]{1,0:T(8,128)} %bitcast.15, ...), custom_call_target="tpu_custom_call" | custom-call | flops 226492416 | bytes 1048576 | tf_op jit(solution)/shard_map/pallas_call | solution.py:466
  8.6 1.6 %collective-permute-start.2 = (f32[5,32,128]{2,1,0:T(8,128)S(1)}, f32[5,32,128]{2,1,0:T(8,128)S(1)}, u32[]{:S(2)}, u32[]{:S(2)}) collective-permute-start(f32[5,32,128]{2,1,0:T(8,128)S(1)} %get-tuple-element.44), channel_id=1, source_target_pairs={{0,16},{16,0},{1,17},{17,1},{2,18},{18,2},{3,19},{19,3},{4,20},{20... | collective-permute-start | bytes 245768 | tf_op jit(solution)/shard_map/ppermute | solution.py:28
  10.2 0.7 %collective-permute-start.4 = (f32[3,32,128]{2,1,0:T(8,128)S(1)}, f32[3,32,128]{2,1,0:T(8,128)S(1)}, u32[]{:S(2)}, u32[]{:S(2)}) collective-permute-start(f32[3,32,128]{2,1,0:T(8,128)S(1)} %get-tuple-element.45), channel_id=1, source_target_pairs={{4,8},{8,4},{5,9},{9,5},{6,10},{10,6},{7,11},{11,7},{20,24},{24,20... | collective-permute-start | bytes 147464 | tf_op jit(solution)/shard_map/ppermute | solution.py:28
  10.8 4.5 %collective-permute-start.3 = (f32[3,32,128]{2,1,0:T(8,128)S(1)}, f32[3,32,128]{2,1,0:T(8,128)S(1)}, u32[]{:S(2)}, u32[]{:S(2)}) collective-permute-start(f32[3,32,128]{2,1,0:T(8,128)S(1)} %get-tuple-element.45), channel_id=1, source_target_pairs={{0,4},{4,0},{8,12},{12,8},{1,5},{5,1},{9,13},{13,9},{2,6},{6,2},{1... | collective-permute-start | bytes 147464 | tf_op jit(solution)/shard_map/ppermute | solution.py:28
  15.3 2.1 %collective-permute-done.3.refs_1_ = f32[3,32,128]{2,1,0:T(8,128)S(1)} collective-permute-done((f32[3,32,128]{2,1,0:T(8,128)S(1)}, f32[3,32,128]{2,1,0:T(8,128)S(1)}, u32[]{:S(2)}, u32[]{:S(2)}) %collective-permute-start.3) | collective-permute-done | bytes 49184 | tf_op jit(solution)/shard_map/ppermute | solution.py:28
  17.4 0.8 %shard_map.107 = (f32[4,32,128]{2,1,0:T(8,128)S(1)}, f32[2,32,128]{2,1,0:T(8,128)S(1)}, f32[3,8,32,128]{3,2,1,0:T(8,128)S(1)}, f32[3,32,128]{2,1,0:T(8,128)S(1)}...) custom-call(f32[768,128]{1,0:T(8,128)S(1)} %get-tuple-element.36.trace, ...), custom_call_target="tpu_custom_call" | custom-call | flops 226492416 | bytes 1048576 | tf_op jit(solution)/shard_map/pallas_call | solution.py:466
  18.2 0.6 %collective-permute-start.5 = (f32[5,32,128]{2,1,0:T(8,128)S(1)}, f32[5,32,128]{2,1,0:T(8,128)S(1)}, u32[]{:S(2)}, u32[]{:S(2)}) collective-permute-start(f32[5,32,128]{2,1,0:T(8,128)S(1)} %get-tuple-element.49.refs_0_), channel_id=1, source_target_pairs={{0,16},{16,0},{1,17},{17,1},{2,18},{18,2},{3,19},{19,3},{4,20},{20... | collective-permute-start | bytes 245768 | tf_op jit(solution)/shard_map/ppermute | solution.py:28
  18.8 2.0 %collective-permute-start.6 = (f32[3,32,128]{2,1,0:T(8,128)S(1)}, f32[3,32,128]{2,1,0:T(8,128)S(1)}, u32[]{:S(2)}, u32[]{:S(2)}) collective-permute-start(f32[3,32,128]{2,1,0:T(8,128)S(1)} %get-tuple-element.50.refs_1_), channel_id=1, source_target_pairs={{0,4},{4,0},{8,12},{12,8},{1,5},{5,1},{9,13},{13,9},{2,6},{6,2},{1... | collective-permute-start | bytes 147464 | tf_op jit(solution)/shard_map/ppermute | solution.py:28
  20.8 0.7 %collective-permute-start.7 = (f32[3,32,128]{2,1,0:T(8,128)S(1)}, f32[3,32,128]{2,1,0:T(8,128)S(1)}, u32[]{:S(2)}, u32[]{:S(2)}) collective-permute-start(f32[3,32,128]{2,1,0:T(8,128)S(1)} %get-tuple-element.51.refs_2_), channel_id=1, source_target_pairs={{4,8},{8,4},{5,9},{9,5},{6,10},{10,6},{7,11},{11,7},{20,24},{24,20... | collective-permute-start | bytes 147464 | tf_op jit(solution)/shard_map/ppermute | solution.py:28
  21.4 1.4 %collective-permute-done.6.refs_4_ = f32[3,32,128]{2,1,0:T(8,128)S(1)} collective-permute-done((f32[3,32,128]{2,1,0:T(8,128)S(1)}, f32[3,32,128]{2,1,0:T(8,128)S(1)}, u32[]{:S(2)}, u32[]{:S(2)}) %collective-permute-start.6) | collective-permute-done | bytes 49184 | tf_op jit(solution)/shard_map/ppermute | solution.py:28
  22.8 0.8 %shard_map.108 = (f32[3,8,32,128]{3,2,1,0:T(8,128)S(1)}, f32[32,128]{1,0:T(8,128)S(1)}, f32[4,32,128]{2,1,0:T(8,128)S(1)}, f32[2,32,128]{2,1,0:T(8,128)S(1)}, f3...) custom-call(f32[3,8,32,128]{3,2,1,0:T(8,128)S(1)} %get-tuple-element, ...), custom_call_target="tpu_custom_call" | custom-call | flops 226492416 | bytes 1048576 | tf_op jit(solution)/shard_map/pallas_call | solution.py:466
  23.7 1.6 %collective-permute-start.8 = (f32[4,32,128]{2,1,0:T(8,128)S(1)}, f32[4,32,128]{2,1,0:T(8,128)S(1)}, u32[]{:S(2)}, u32[]{:S(2)}) collective-permute-start(f32[4,32,128]{2,1,0:T(8,128)S(1)} %get-tuple-element.59.refs_0_), channel_id=1, source_target_pairs={{0,16},{16,0},{1,17},{17,1},{2,18},{18,2},{3,19},{19,3},{4,20},{20... | collective-permute-start | bytes 196616 | tf_op jit(solution)/shard_map/ppermute | solution.py:28
  25.3 3.9 %collective-permute-start.9 = (f32[2,32,128]{2,1,0:T(8,128)S(1)}, f32[2,32,128]{2,1,0:T(8,128)S(1)}, u32[]{:S(2)}, u32[]{:S(2)}) collective-permute-start(f32[2,32,128]{2,1,0:T(8,128)S(1)} %get-tuple-element.60.refs_1_), channel_id=1, source_target_pairs={{0,4},{4,0},{8,12},{12,8},{1,5},{5,1},{9,13},{13,9},{2,6},{6,2},{1... | collective-permute-start | bytes 98312 | tf_op jit(solution)/shard_map/ppermute | solution.py:28
  29.2 0.7 %collective-permute-start.10 = (f32[2,32,128]{2,1,0:T(8,128)S(1)}, f32[2,32,128]{2,1,0:T(8,128)S(1)}, u32[]{:S(2)}, u32[]{:S(2)}) collective-permute-start(f32[2,32,128]{2,1,0:T(8,128)S(1)} %get-tuple-element.61.refs_2_), channel_id=1, source_target_pairs={{4,8},{8,4},{5,9},{9,5},{6,10},{10,6},{7,11},{11,7},{20,24},{24,20... | collective-permute-start | bytes 98312 | tf_op jit(solution)/shard_map/ppermute | solution.py:28
  29.8 1.2 %collective-permute-done.9.refs_4_ = f32[2,32,128]{2,1,0:T(8,128)S(1)} collective-permute-done((f32[2,32,128]{2,1,0:T(8,128)S(1)}, f32[2,32,128]{2,1,0:T(8,128)S(1)}, u32[]{:S(2)}, u32[]{:S(2)}) %collective-permute-start.9) | collective-permute-done | bytes 32800 | tf_op jit(solution)/shard_map/ppermute | solution.py:28
  31.1 1.6 %shard_map.109 = (f32[3,8,32,128]{3,2,1,0:T(8,128)S(1)}, f32[4,32,128]{2,1,0:T(8,128)S(1)}, f32[2,32,128]{2,1,0:T(8,128)S(1)}, f32[32,128]{1,0:T(8,128)}) custom-call(f32[3,8,32,128]{3,2,1,0:T(8,128)S(1)} %get-tuple-element.52.partial, f32[32,128]{1,0:T(8,128)S(1)} %get-tuple-element.53.image_z.refs_8_, f32[24,128]{1,0:T(8,128)S(1)} %get-tuple-element.48.diag, ...), custom_call_target="tpu_custom_call" | custom-call | flops 226492416 | bytes 1048576 | tf_op jit(solution)/shard_map/pallas_call | solution.py:466
  32.7 5.7 %all-to-all-start = ((f32[32,1,128]{2,1,0:T(1,128)}), f32[32,1,128]{2,1,0:T(1,128)S(1)}, u32[]{:S(2)}, u32[]{:S(2)}) async-start(f32[32,1,128]{2,1,0:T(1,128)} %bitcast.6), calls=%async_computation | async-start | bytes 32768 | tf_op jit(solution)/shard_map/all_to_all | solution.py:540
  38.4 0.1 copy.13.lift
  38.6 2.0 %shard_map.110.base = f32[8,384,128]{2,1,0:T(8,128)S(1)} custom-call(bf16[3072,128]{1,0:T(8,128)(2,1)} %bitcast.21, s32[8,128]{1,0:T(8,128)} %bitcast.16, bf16[384,384]{1,0:T(8,128)(2,1)} %operator.1), custom_call_target="tpu_custom_call" | custom-call | flops 301989888 | bytes 1048576 | tf_op jit(solution)/shard_map/pallas_call | solution.py:466
  40.6 4.9 %all-to-all-done = f32[32,1,128]{2,1,0:T(1,128)S(1)} async-done(((f32[32,1,128]{2,1,0:T(1,128)}), f32[32,1,128]{2,1,0:T(1,128)S(1)}, u32[]{:S(2)}, u32[]{:S(2)}) %all-to-all-start) | async-done | bytes 16416 | tf_op jit(solution)/shard_map/all_to_all | solution.py:540
  45.5 1.6 %shard_map.111 = (bf16[3072,128]{1,0:T(8,128)(2,1)}, f32[768,128]{1,0:T(8,128)}) custom-call(f32[32,128]{1,0:T(8,128)S(1)} %bitcast.18, f32[768,128]{1,0:T(8,128)S(1)} %bitcast.13, f32[8,384,128]{2,1,0:T(8,128)S(1)} %shard_map.110.base, s32[8,128]{1,0:T(8,128)S(1)} %bitcast.17, bf16[384,192]{1,0:T(8,128)(2,1)S(1)} %copy.13.lift, ...), custom_call_target="tpu_custom_call" | custom-call | flops 150994944 | bytes 1048576 | tf_op jit(solution)/shard_map/pallas_call | solution.py:466
  (15 shorter events, 0.1 us)
Async XLA Ops:
  2.1 6.4 %collective-permute-start.1 = (f32[104,128]{1,0:T(8,128)S(1)}, f32[104,128]{1,0:T(8,128)S(1)}, u32[]{:S(2)}, u32[]{:S(2)}) collective-permute-start(f32[104,128]{1,0:T(8,128)S(1)} %get-tuple-element.40), channel_id=1, source_target_pairs={{1,2},{2,1},{5,6},{6,5},{9,10},{10,9},{13,14},{14,13},{17,18},{18,... | collective-permute-start | bytes 159752 | tf_op jit(solution)/shard_map/ppermute | solution.py:28
  2.8 5.7 %collective-permute-start = (f32[104,128]{1,0:T(8,128)S(1)}, f32[104,128]{1,0:T(8,128)S(1)}, u32[]{:S(2)}, u32[]{:S(2)}) collective-permute-start(f32[104,128]{1,0:T(8,128)S(1)} %get-tuple-element.40), channel_id=1, source_target_pairs={{0,1},{1,0},{2,3},{3,2},{4,5},{5,4},{6,7},{7,6},{8,9},{9,8},{10,11... | collective-permute-start | bytes 159752 | tf_op jit(solution)/shard_map/ppermute | solution.py:28
  8.6 8.8 %collective-permute-start.2 = (f32[5,32,128]{2,1,0:T(8,128)S(1)}, f32[5,32,128]{2,1,0:T(8,128)S(1)}, u32[]{:S(2)}, u32[]{:S(2)}) collective-permute-start(f32[5,32,128]{2,1,0:T(8,128)S(1)} %get-tuple-element.44), channel_id=1, source_target_pairs={{0,16},{16,0},{1,17},{17,1},{2,18},{18,2},{3,19},{19,3},{4,20},{20... | collective-permute-start | bytes 245768 | tf_op jit(solution)/shard_map/ppermute | solution.py:28
  10.2 5.1 %collective-permute-start.4 = (f32[3,32,128]{2,1,0:T(8,128)S(1)}, f32[3,32,128]{2,1,0:T(8,128)S(1)}, u32[]{:S(2)}, u32[]{:S(2)}) collective-permute-start(f32[3,32,128]{2,1,0:T(8,128)S(1)} %get-tuple-element.45), channel_id=1, source_target_pairs={{4,8},{8,4},{5,9},{9,5},{6,10},{10,6},{7,11},{11,7},{20,24},{24,20... | collective-permute-start | bytes 147464 | tf_op jit(solution)/shard_map/ppermute | solution.py:28
  10.8 6.5 %collective-permute-start.3 = (f32[3,32,128]{2,1,0:T(8,128)S(1)}, f32[3,32,128]{2,1,0:T(8,128)S(1)}, u32[]{:S(2)}, u32[]{:S(2)}) collective-permute-start(f32[3,32,128]{2,1,0:T(8,128)S(1)} %get-tuple-element.45), channel_id=1, source_target_pairs={{0,4},{4,0},{8,12},{12,8},{1,5},{5,1},{9,13},{13,9},{2,6},{6,2},{1... | collective-permute-start | bytes 147464 | tf_op jit(solution)/shard_map/ppermute | solution.py:28
  17.4 21.1 %copy-start.2 = (bf16[384,192]{0,1:T(8,128)(2,1)S(1)}, bf16[384,192]{0,1:T(8,128)(2,1)}, u32[]{:S(2)}) copy-start(bf16[384,192]{0,1:T(8,128)(2,1)} %param.16) | copy-start | bytes 442372
  18.2 4.7 %collective-permute-start.5 = (f32[5,32,128]{2,1,0:T(8,128)S(1)}, f32[5,32,128]{2,1,0:T(8,128)S(1)}, u32[]{:S(2)}, u32[]{:S(2)}) collective-permute-start(f32[5,32,128]{2,1,0:T(8,128)S(1)} %get-tuple-element.49.refs_0_), channel_id=1, source_target_pairs={{0,16},{16,0},{1,17},{17,1},{2,18},{18,2},{3,19},{19,3},{4,20},{20... | collective-permute-start | bytes 245768 | tf_op jit(solution)/shard_map/ppermute | solution.py:28
  18.8 4.1 %collective-permute-start.6 = (f32[3,32,128]{2,1,0:T(8,128)S(1)}, f32[3,32,128]{2,1,0:T(8,128)S(1)}, u32[]{:S(2)}, u32[]{:S(2)}) collective-permute-start(f32[3,32,128]{2,1,0:T(8,128)S(1)} %get-tuple-element.50.refs_1_), channel_id=1, source_target_pairs={{0,4},{4,0},{8,12},{12,8},{1,5},{5,1},{9,13},{13,9},{2,6},{6,2},{1... | collective-permute-start | bytes 147464 | tf_op jit(solution)/shard_map/ppermute | solution.py:28
  20.8 2.1 %collective-permute-start.7 = (f32[3,32,128]{2,1,0:T(8,128)S(1)}, f32[3,32,128]{2,1,0:T(8,128)S(1)}, u32[]{:S(2)}, u32[]{:S(2)}) collective-permute-start(f32[3,32,128]{2,1,0:T(8,128)S(1)} %get-tuple-element.51.refs_2_), channel_id=1, source_target_pairs={{4,8},{8,4},{5,9},{9,5},{6,10},{10,6},{7,11},{11,7},{20,24},{24,20... | collective-permute-start | bytes 147464 | tf_op jit(solution)/shard_map/ppermute | solution.py:28
  23.7 7.4 %collective-permute-start.8 = (f32[4,32,128]{2,1,0:T(8,128)S(1)}, f32[4,32,128]{2,1,0:T(8,128)S(1)}, u32[]{:S(2)}, u32[]{:S(2)}) collective-permute-start(f32[4,32,128]{2,1,0:T(8,128)S(1)} %get-tuple-element.59.refs_0_), channel_id=1, source_target_pairs={{0,16},{16,0},{1,17},{17,1},{2,18},{18,2},{3,19},{19,3},{4,20},{20... | collective-permute-start | bytes 196616 | tf_op jit(solution)/shard_map/ppermute | solution.py:28
  25.3 5.8 %collective-permute-start.9 = (f32[2,32,128]{2,1,0:T(8,128)S(1)}, f32[2,32,128]{2,1,0:T(8,128)S(1)}, u32[]{:S(2)}, u32[]{:S(2)}) collective-permute-start(f32[2,32,128]{2,1,0:T(8,128)S(1)} %get-tuple-element.60.refs_1_), channel_id=1, source_target_pairs={{0,4},{4,0},{8,12},{12,8},{1,5},{5,1},{9,13},{13,9},{2,6},{6,2},{1... | collective-permute-start | bytes 98312 | tf_op jit(solution)/shard_map/ppermute | solution.py:28
  29.2 1.9 %collective-permute-start.10 = (f32[2,32,128]{2,1,0:T(8,128)S(1)}, f32[2,32,128]{2,1,0:T(8,128)S(1)}, u32[]{:S(2)}, u32[]{:S(2)}) collective-permute-start(f32[2,32,128]{2,1,0:T(8,128)S(1)} %get-tuple-element.61.refs_2_), channel_id=1, source_target_pairs={{4,8},{8,4},{5,9},{9,5},{6,10},{10,6},{7,11},{11,7},{20,24},{24,20... | collective-permute-start | bytes 98312 | tf_op jit(solution)/shard_map/ppermute | solution.py:28
  32.7 12.9 %copy-start = (f32[3,32,2,4,128]{4,3,2,1,0:T(4,128)S(1)}, f32[3,32,2,4,128]{4,3,2,1,0:T(4,128)}, u32[]{:S(2)}) copy-start(f32[3,32,2,4,128]{4,3,2,1,0:T(4,128)} %param.10) | copy-start | bytes 1179652
  32.7 12.9 %copy-start.1 = (s32[2,4,128]{2,1,0:T(4,128)S(1)}, s32[2,4,128]{2,1,0:T(4,128)}, u32[]{:S(2)}) copy-start(s32[2,4,128]{2,1,0:T(4,128)} %param.13) | copy-start | bytes 12292
  32.7 12.9 %all-to-all-start = ((f32[32,1,128]{2,1,0:T(1,128)}), f32[32,1,128]{2,1,0:T(1,128)S(1)}, u32[]{:S(2)}, u32[]{:S(2)}) async-start(f32[32,1,128]{2,1,0:T(1,128)} %bitcast.6), calls=%async_computation | async-start | bytes 32768 | tf_op jit(solution)/shard_map/all_to_all | solution.py:540

commit v3 on v2

--- a/solution.py
+++ b/solution.py
@@ -67,6 +67,25 @@
 def lanes_of(geo):
     lane = lane_iota((geo.F, geo.EZ))
     return lane, lane % STRIDE, lane // (STRIDE * geo.EY), (lane // STRIDE) % geo.EY
+
+
+def part_of(geo, k, count):
+    return slice(k * geo.F, k * geo.F + (geo.F if k < count else 8))
+
+
+def fold(geo, a, value):
+    lane = lane_iota((8, geo.EZ))
+    unit = geo.EY * STRIDE if a == 0 else STRIDE
+    slot = lane // unit if a == 0 else (lane % (geo.EY * STRIDE)) // unit
+    out = jnp.zeros((8, geo.EZ), f32)
+    for q in range(geo.F // 8):
+        out = jnp.where(slot == q, moved(value[8 * q:8 * q + 8], 0, q * unit), out)
+    return out
+
+
+def unfold(geo, a, value):
+    unit = geo.EY * STRIDE if a == 0 else STRIDE
+    return jnp.concatenate([moved(value, q * unit, 0) for q in range(geo.F // 8)], 0)
 
 
 def z_above(geo, z_own, z_pack, m):
@@ -145,15 +164,15 @@
         up = block(1, M)
         v = own_pack(0) + block(0, M)
         pack_out[0][...] = v + jnp.where(at_i > 0, moved(up, 0, EY * STRIDE), 0.0)
-        shared[0].append((v, moved(up, (EX - 1) * EY * STRIDE, 0)))
+        shared[0].append((fold(geo, 0, v), fold(geo, 0, moved(up, (EX - 1) * EY * STRIDE, 0))))
         up = block(3, M)
         v = own_pack(1) + block(2, M)
         pack_out[1][...] = v + jnp.where(at_j > 0, moved(up, 0, STRIDE), 0.0)
-        shared[1].append((v, moved(up, (EY - 1) * STRIDE, 0)))
+        shared[1].append((fold(geo, 1, v), fold(geo, 1, moved(up, (EY - 1) * STRIDE, 0))))
     for a in (0, 1):
         for odd, ref in enumerate(sends[a]):
             for k, (bottom, high) in enumerate(shared[a]):
-                ref[k] = jnp.where(parity[a] == odd, high, bottom)
+                ref[part_of(geo, k, (EY, EX)[a])] = jnp.where(parity[a] == odd, high, bottom)
 
 
 def chosen(refs, parity, read, flip=False):
@@ -173,18 +192,18 @@
             i, j = divmod(m, EY)
             v = partial[f, m]
             if f == 0 and i == 0 and got[0]:
-                v = v + chosen(got[0], parity[0], lambda r: r[j], True)
+                v = v + chosen(got[0], parity[0], lambda r: r[part_of(geo, j, EY)], True)
             if f == 1 and j == 0 and got[1]:
-                v = v + chosen(got[1], parity[1], lambda r: r[i], True)
+                v = v + chosen(got[1], parity[1], lambda r: r[part_of(geo, i, EX)], True)
             full[f, m] = v
     for a, n in ((0, EY), (1, EX)):
         for k in range(n):
-            halos[a][k] = both_sides(geo, sent[a], got[a], parity[a], below_top[a], k)
+            halos[a][k] = both_sides(geo, sent[a], got[a], parity[a], below_top[a], part_of(geo, k, n))
 
 
 def both_sides(geo, sent, got, parity, below_top, k):
     if not got:
-        return jnp.zeros((geo.F, geo.EZ), f32)
+        return jnp.zeros((k.stop - k.start, geo.EZ), f32)
     return (chosen(sent, parity, lambda r: r[k]) + chosen(got, parity, lambda r: r[k])) * below_top
 
 
@@ -241,14 +260,11 @@
         load = jnp.where(lane < EZ // 2, moved(v, EZ // 2, 0), 0.0)
         trace_pack[f] = old
         own_pack[f] = load - lines[f:f + 1] * old
-        if f == 0:
-            for j in range(EY):
-                sx[j] = rows(trace, geo, 0, j)
-            sx[EY] = old
-        if f == 1:
-            for i in range(EX):
-                sy[i] = rows(trace, geo, 1, i * EY)
-            sy[EX] = old
+        if f < 2:
+            ref, count, step = ((sx, EY, 1), (sy, EX, EY))[f]
+            for k in range(count):
+                ref[part_of(geo, k, count)] = rows(trace, geo, f, k * step)
+            ref[part_of(geo, count, count)] = fold(geo, f, old)
 
 
 def take(refs, *sizes):
@@ -285,19 +301,20 @@
             own[f, m] = rows(vload, geo, f, m) - diag[f * geo.M + m:f * geo.M + m + 1] * rows(trace, geo, f, m)
 
 
-def kernel_start(geo, n, trace, own, weight, schur, trace_pack, own_pack, lines, *refs):
+def kernel_start(geo, n, trace, own, weight, schur, _, trace_pack, own_pack, lines, *refs):
     got, halos, (partial, partial_pack), sends, (ghi, glo) = take(refs, n[:2], 2, 2, n[:2], 2)
     F, EX, EY, EZ = geo.F, geo.EX, geo.EY, geo.EZ
     parity, _ = place()
 
     def above(a, k):
-        return chosen(got[a], parity[a], lambda r: r[k]) if got[a] else jnp.zeros((F, EZ), f32)
+        at = part_of(geo, k, (EY, EX)[a])
+        return chosen(got[a], parity[a], lambda r: r[at]) if got[a] else jnp.zeros((at.stop - at.start, EZ), f32)
 
     for a, count in ((0, EY), (1, EX)):
         for k in range(count):
             halos[a][k] = above(a, k)
     halo = (lambda j: halos[0][j], lambda i: halos[1][i], trace_pack[2])
-    wide = (trace_pack[0], trace_pack[1], above(0, EY), above(1, EX))
+    wide = (trace_pack[0], trace_pack[1], unfold(geo, 0, above(0, EY)), unfold(geo, 1, above(1, EX)))
     y = gather_and_apply(geo, lambda f, m: rows(trace, geo, f, m), halo, schur, ghi, glo, wide)
     spread(geo, y, weight[...], lambda f, m: own[f, m], -1.0, partial, sends, parity,
            lines[3:4], lambda f: own_pack[f], {f: partial_pack.at[f] for f in range(3)})
@@ -317,9 +334,10 @@
     for a, edge, count in ((0, at_i == 0, EY), (1, at_j == 0, EX)):
         v = partial_pack[a]
         if got[a]:
-            v = v + jnp.where(edge, chosen(got[a], parity[a], lambda r: r[count], True), 0.0)
+            v = v + jnp.where(edge, unfold(geo, a, chosen(got[a], parity[a], lambda r: r[part_of(geo, count, count)], True)), 0.0)
         packs.append(v)
-    wide = (*packs, both_sides(geo, sent[0], got[0], parity[0], below_top[0], EY), both_sides(geo, sent[1], got[1], parity[1], below_top[1], EX))
+    beside = [unfold(geo, a, both_sides(geo, sent[a], got[a], parity[a], below_top[a], part_of(geo, k, k))) for a, k in ((0, EY), (1, EX))]
+    wide = (*packs, *beside)
     full_z[...] = jnp.where(column < 2, partial_pack[2], partial_pack[2] * below_top[2])
     halo = (lambda j: halos[0][j], lambda i: halos[1][i], full_z[...])
     y = gather_and_apply(geo, lambda f, m: full[f, m], halo, schur, ghi, glo, wide)
@@ -403,12 +421,13 @@
     return alpha + second * (1.0 + beta), -alpha * second
 
 
-def kernel_volume(geo, fields, fine, operator, base, plain, vfields, vfine, voperator, sems):
+def kernel_volume(geo, fields, fine, operator, lift_in, base, lift, plain, vfields, vfine, voperator, vlift, sems):
     M, EZ = geo.M, geo.EZ
     dofs = operator.shape[0]
-    for c in fetch([(fields, vfields), (fine, vfine), (operator, voperator)], sems):
+    for c in fetch([(fields, vfields), (fine, vfine), (operator, voperator), (lift_in, vlift)], sems):
         c.wait()
     plain[...] = vfields[...].astype(f32)
+    lift[...] = vlift[...].T
     nodal = [plain[pl.ds(m, dofs, stride=M), :] for m in range(M)]
     volume = jnp.dot(voperator[...], jnp.concatenate([v.astype(bf16) for v in nodal], 1), preferred_element_type=f32)
     coarse = 1.0 - vfine[...].astype(f32)
@@ -497,7 +516,8 @@
     scale = coeff.reshape(M, EZ)
     nodal = fields.reshape(dofs * M, EZ)
     slab = [(EY, F, EZ), (EX, F, EZ)]
-    slab_wide = [(EY + 1, F, EZ), (EX + 1, F, EZ)]
+    slab_sent = [(EY * F, EZ), (EX * F, EZ)]
+    slab_wide = [(EY * F + 8, EZ), (EX * F + 8, EZ)]
     full, pack, line = (3, M, F, EZ), (3, F, EZ), (8, EZ)
     halo_outs = [(s, f32) for s in slab]
     flops = 2 * 3 * N * N * M * EZ
@@ -520,16 +540,20 @@
         functools.partial(kernel_prepare, geo), [(full, f32), ((3 * M, EZ), f32), ((M, EZ), f32), ((2 * N, N), bf16)],
         [held, load, diag_in, fine, scale, schur_op], [like(load), like(fine), like(scale), like(schur_op), dma((5,))],
         flops, hbm_args=(1, 2, 3, 4, 5))
+    base, lift = call(
+        functools.partial(kernel_volume, geo), [((M, dofs, EZ), f32), (lift_op.shape, bf16)], [nodal, fine, volume_op, lift_op.T],
+        [pltpu.VMEM((dofs * M, EZ), f32), like(nodal), like(fine), like(volume_op), like(lift_op.T), dma((4,))],
+        2 * dofs * dofs * M * EZ, hbm_args=(0, 1, 2, 3))
     trace_pack, own_pack, lines, sx, sy = call(
         functools.partial(kernel_wide, geo, n), [(pack, f32), (pack, f32), (line, f32)] + [(s, f32) for s in slab_wide],
         [held, weight] + flat(got), [], 1 << 20)
     got = exchange(AXES[:2], [[sx, sx], [sy, sy]])
     out = call(functools.partial(kernel_start, geo, n), halo_outs + [(full, f32), (pack, f32)] + send_outs(slab_wide),
-               [held, own, weight, schur, trace_pack, own_pack, lines] + flat(got), halves(M + 1), flops)
+               [held, own, weight, schur, base, trace_pack, own_pack, lines] + flat(got), halves(M + 1), flops)
     halo_old, partial, partial_pack, sent = [*out[:2], trace_pack], out[2], out[3], grouped(out[4:])
     got = exchange(AXES[:2], sent)
     out = call(functools.partial(kernel_middle, geo, n),
-               [(full, f32), ((F, EZ), f32)] + halo_outs + [(full, f32), ((F, EZ), f32)] + send_outs(slab) + [((2, 8, EZ), f32)],
+               [(full, f32), ((F, EZ), f32)] + halo_outs + [(full, f32), ((F, EZ), f32)] + send_outs(slab_sent) + [((2, 8, EZ), f32)],
                [partial, partial_pack, diag, weight, schur, lines] + flat(sent) + flat(got), halves(M + 1), flops)
     r, r_z, partial, image_z, sent, dots = out[0], out[1], out[4], out[5], grouped(out[6:-1]), out[-1]
     halo_r = [*out[2:4], r_z]
@@ -538,12 +562,9 @@
                [partial, image_z, diag, weight, schur, dots, r, *halo_r] + flat(sent) + flat(got), halves(M), flops)
     q, halo_q, message = out[0], [*out[1:3], image_z], out[3]
     message = lax.all_to_all(message, AXES, 0, 0, tiled=True)
-    base = call(functools.partial(kernel_volume, geo), [((M, dofs, EZ), f32)], [nodal, fine, volume_op],
-                [pltpu.VMEM((dofs * M, EZ), f32), like(nodal), like(fine), like(volume_op), dma((3,))],
-                2 * dofs * dofs * M * EZ, hbm_args=(0, 1, 2))[0]
     fields_new, trace_new = call(
         functools.partial(kernel_finish, geo), [((dofs * M, EZ), bf16), ((3 * F * M, EZ), f32)],
-        [message, trace, base, fine, lift_op, r, q, *halo_old, *halo_r, *halo_q],
+        [message, trace, base, fine, lift, r, q, *halo_old, *halo_r, *halo_q],
         [pltpu.VMEM((N, M * EZ), bf16), pltpu.VMEM((dofs * M, EZ), f32), like(nodal), like(trace), dma((PARTS + 1,))],
         2 * dofs * N * M * EZ, hbm_outs=(0, 1))
     return fields_new.reshape(fields.shape), trace_new.reshape(trace_old.shape)

time: 47.5 us -> 46.7 us (0.983)
  blocking collectives: 0 us -> 12.7 us
  waiting for transfers between devices: 9.67 us -> 2.68 us
  starting transfers between devices: 26.9 us -> 21 us
    all_to_all x0 -> x1, blocking collectives: none -> 12.7 us  [body(): message = lax.all_to_all(message, AXES, 0, 0, tiled=True)]
    all_to_all x1 -> x0, starting transfers between devices: 5.74 us -> none  [body(): message = lax.all_to_all(message, AXES, 0, 0, tiled=True)]
    all_to_all x1 -> x0, waiting for transfers between devices: 4.94 us -> none  [body(): message = lax.all_to_all(message, AXES, 0, 0, tiled=True)]
    ppermute x11, waiting for transfers between devices: 4.73 us -> 2.68 us  [exchange(): lax.ppermute(v, axis, pairs(axis, odd))]
  transfers between devices with their start and end apart: 12 -> 11, of which waited for: 4 -> 2; matrix products, arithmetic and copies ran while one was open for 0% -> 0% of each run, Pallas kernels for 7% -> 7%
where the time goes in v3:
time: 46.7 us; the launch traced here: 46.4 us
  starting transfers between devices  21 us (45%)
  blocking collectives  12.7 us (27%)
  Pallas kernels  9.24 us (20%)
  waiting for transfers between devices  2.68 us (6%)
  between operations  0.77 us (2%)
    ppermute x11, starting transfers between devices, exchange(): lax.ppermute(v, axis, pairs(axis, odd))  21 us
    all_to_all x1, blocking collectives, body(): message = lax.all_to_all(message, AXES, 0, 0, tiled=True)  12.7 us
    pallas_call x8, Pallas kernels, call(): pl.pallas_call(kernel, out_shape=[(HBM if k in hbm_outs else jax.ShapeDty...  9.24 us
    ppermute x11, waiting for transfers between devices, exchange(): lax.ppermute(v, axis, pairs(axis, odd))  2.68 us
  transfers between devices with their start and end apart: 11, of which 2 were waited for; matrix products, arithmetic and copies ran while one was open for 0% of the time, Pallas kernels for 7%

profile of v3, /device:TPU:0, one launch (start us, length us, event | category | flops | bytes accessed | tf_op | source)
XLA Modules:
  0.0 46.4 jit_solution(11271048289077511992)
XLA Ops:
  0.6 1.5 %shard_map.104 = (f32[104,128]{1,0:T(8,128)S(1)}, f32[768,128]{1,0:T(8,128)S(1)}) custom-call(f32[768,128]{1,0:T(8,128)} %bitcast.13, f32[768,128]{1,0:T(8,128)} %bitcast.21, f32[24,128]{1,0:T(8,128)} %bitcast.25, s32[8,128]{1,0:T(8,128)} %bitcast.15, f32[8,128]{1,0:T(8,128)} %bitcast.27), custom_call_target="tpu_custom_call" | custom-call | flops 1048576 | bytes 1048576 | tf_op jit(solution)/shard_map/pallas_call | solution.py:485
  2.1 0.7 %collective-permute-start.1 = (f32[104,128]{1,0:T(8,128)S(1)}, f32[104,128]{1,0:T(8,128)S(1)}, u32[]{:S(2)}, u32[]{:S(2)}) collective-permute-start(f32[104,128]{1,0:T(8,128)S(1)} %get-tuple-element.43), channel_id=1, source_target_pairs={{1,2},{2,1},{5,6},{6,5},{9,10},{10,9},{13,14},{14,13},{17,18},{18,... | collective-permute-start | bytes 159752 | tf_op jit(solution)/shard_map/ppermute | solution.py:28
  2.8 4.4 %collective-permute-start = (f32[104,128]{1,0:T(8,128)S(1)}, f32[104,128]{1,0:T(8,128)S(1)}, u32[]{:S(2)}, u32[]{:S(2)}) collective-permute-start(f32[104,128]{1,0:T(8,128)S(1)} %get-tuple-element.43), channel_id=1, source_target_pairs={{0,1},{1,0},{2,3},{3,2},{4,5},{5,4},{6,7},{7,6},{8,9},{9,8},{10,11... | collective-permute-start | bytes 159752 | tf_op jit(solution)/shard_map/ppermute | solution.py:28
  7.2 1.3 %shard_map.105 = (f32[3,8,32,128]{3,2,1,0:T(8,128)S(1)}, f32[24,128]{1,0:T(8,128)S(1)}, f32[8,128]{1,0:T(8,128)S(1)}, bf16[384,192]{1,0:T(8,128)(2,1)S(1)}) custom-call(f32[768,128]{1,0:T(8,128)S(1)} %get-tuple-element.38.trace, f32[768,128]{1,0:T(8,128)} %bitcast.22, f32[24,128]{1,0:T(8,128)} %bitcast.26, s32[8,128]{1,0:T(8,128)} %bitcast.16, ...), custom_call_target="tpu_custom_call" | custom-call | flops 226492416 | bytes 1048576 | tf_op jit(solution)/shard_map/pallas_call | solution.py:485
  8.5 0.1 shard_map.107
  8.6 1.6 %collective-permute-start.2 = (f32[136,128]{1,0:T(8,128)S(1)}, f32[136,128]{1,0:T(8,128)S(1)}, u32[]{:S(2)}, u32[]{:S(2)}) collective-permute-start(f32[136,128]{1,0:T(8,128)S(1)} %get-tuple-element.47), channel_id=1, source_target_pairs={{0,16},{16,0},{1,17},{17,1},{2,18},{18,2},{3,19},{19,3},{4,20},{20... | collective-permute-start | bytes 208904 | tf_op jit(solution)/shard_map/ppermute | solution.py:28
  10.2 0.7 %collective-permute-start.4 = (f32[72,128]{1,0:T(8,128)S(1)}, f32[72,128]{1,0:T(8,128)S(1)}, u32[]{:S(2)}, u32[]{:S(2)}) collective-permute-start(f32[72,128]{1,0:T(8,128)S(1)} %get-tuple-element.48), channel_id=1, source_target_pairs={{4,8},{8,4},{5,9},{9,5},{6,10},{10,6},{7,11},{11,7},{20,24},{24,20... | collective-permute-start | bytes 110600 | tf_op jit(solution)/shard_map/ppermute | solution.py:28
  10.8 4.5 %collective-permute-start.3 = (f32[72,128]{1,0:T(8,128)S(1)}, f32[72,128]{1,0:T(8,128)S(1)}, u32[]{:S(2)}, u32[]{:S(2)}) collective-permute-start(f32[72,128]{1,0:T(8,128)S(1)} %get-tuple-element.48), channel_id=1, source_target_pairs={{0,4},{4,0},{8,12},{12,8},{1,5},{5,1},{9,13},{13,9},{2,6},{6,2},{1... | collective-permute-start | bytes 110600 | tf_op jit(solution)/shard_map/ppermute | solution.py:28
  15.3 2.0 %shard_map.106 = (f32[8,384,128]{2,1,0:T(8,128)S(1)}, bf16[384,192]{1,0:T(8,128)(2,1)S(1)}) custom-call(bf16[3072,128]{1,0:T(8,128)(2,1)} %bitcast.23, s32[8,128]{1,0:T(8,128)} %bitcast.17, bf16[384,384]{1,0:T(8,128)(2,1)} %operator.1, bf16[192,384]{1,0:T(8,128)(2,1)} %bitcast.24), custom_call_target="tpu_custom_call" | custom-call | flops 301989888 | bytes 1048576 | tf_op jit(solution)/shard_map/pallas_call | solution.py:485
  17.4 0.8 %shard_map.108 = (f32[4,32,128]{2,1,0:T(8,128)S(1)}, f32[2,32,128]{2,1,0:T(8,128)S(1)}, f32[3,8,32,128]{3,2,1,0:T(8,128)S(1)}, f32[3,32,128]{2,1,0:T(8,128)S(1)}...) custom-call(f32[768,128]{1,0:T(8,128)S(1)} %get-tuple-element.38.trace, ...), custom_call_target="tpu_custom_call" | custom-call | flops 226492416 | bytes 1048576 | tf_op jit(solution)/shard_map/pallas_call | solution.py:485
  18.2 0.0 copy-start
  18.2 0.0 copy-start.1
  18.2 0.6 %collective-permute-start.5 = (f32[136,128]{1,0:T(8,128)S(1)}, f32[136,128]{1,0:T(8,128)S(1)}, u32[]{:S(2)}, u32[]{:S(2)}) collective-permute-start(f32[136,128]{1,0:T(8,128)S(1)} %get-tuple-element.52.refs_0_), channel_id=1, source_target_pairs={{0,16},{16,0},{1,17},{17,1},{2,18},{18,2},{3,19},{19,3},{4,20},{20... | collective-permute-start | bytes 208904 | tf_op jit(solution)/shard_map/ppermute | solution.py:28
  18.8 1.9 %collective-permute-start.6 = (f32[72,128]{1,0:T(8,128)S(1)}, f32[72,128]{1,0:T(8,128)S(1)}, u32[]{:S(2)}, u32[]{:S(2)}) collective-permute-start(f32[72,128]{1,0:T(8,128)S(1)} %get-tuple-element.53.refs_1_), channel_id=1, source_target_pairs={{0,4},{4,0},{8,12},{12,8},{1,5},{5,1},{9,13},{13,9},{2,6},{6,2},{1... | collective-permute-start | bytes 110600 | tf_op jit(solution)/shard_map/ppermute | solution.py:28
  20.7 0.7 %collective-permute-start.7 = (f32[72,128]{1,0:T(8,128)S(1)}, f32[72,128]{1,0:T(8,128)S(1)}, u32[]{:S(2)}, u32[]{:S(2)}) collective-permute-start(f32[72,128]{1,0:T(8,128)S(1)} %get-tuple-element.54.refs_2_), channel_id=1, source_target_pairs={{4,8},{8,4},{5,9},{9,5},{6,10},{10,6},{7,11},{11,7},{20,24},{24,20... | collective-permute-start | bytes 110600 | tf_op jit(solution)/shard_map/ppermute | solution.py:28
  21.3 1.4 %collective-permute-done.6.refs_4_ = f32[72,128]{1,0:T(8,128)S(1)} collective-permute-done((f32[72,128]{1,0:T(8,128)S(1)}, f32[72,128]{1,0:T(8,128)S(1)}, u32[]{:S(2)}, u32[]{:S(2)}) %collective-permute-start.6) | collective-permute-done | bytes 36896 | tf_op jit(solution)/shard_map/ppermute | solution.py:28
  22.8 0.9 %shard_map.109 = (f32[3,8,32,128]{3,2,1,0:T(8,128)S(1)}, f32[32,128]{1,0:T(8,128)S(1)}, f32[4,32,128]{2,1,0:T(8,128)S(1)}, f32[2,32,128]{2,1,0:T(8,128)S(1)}, f3...) custom-call(f32[3,8,32,128]{3,2,1,0:T(8,128)S(1)} %get-tuple-element, ...), custom_call_target="tpu_custom_call" | custom-call | flops 226492416 | bytes 1048576 | tf_op jit(solution)/shard_map/pallas_call | solution.py:485
  23.6 1.6 %collective-permute-start.8 = (f32[128,128]{1,0:T(8,128)S(1)}, f32[128,128]{1,0:T(8,128)S(1)}, u32[]{:S(2)}, u32[]{:S(2)}) collective-permute-start(f32[128,128]{1,0:T(8,128)S(1)} %get-tuple-element.62.refs_0_), channel_id=1, source_target_pairs={{0,16},{16,0},{1,17},{17,1},{2,18},{18,2},{3,19},{19,3},{4,20},{20... | collective-permute-start | bytes 196616 | tf_op jit(solution)/shard_map/ppermute | solution.py:28
  25.2 3.9 %collective-permute-start.9 = (f32[64,128]{1,0:T(8,128)S(1)}, f32[64,128]{1,0:T(8,128)S(1)}, u32[]{:S(2)}, u32[]{:S(2)}) collective-permute-start(f32[64,128]{1,0:T(8,128)S(1)} %get-tuple-element.63.refs_1_), channel_id=1, source_target_pairs={{0,4},{4,0},{8,12},{12,8},{1,5},{5,1},{9,13},{13,9},{2,6},{6,2},{1... | collective-permute-start | bytes 98312 | tf_op jit(solution)/shard_map/ppermute | solution.py:28
  29.1 0.7 %collective-permute-start.10 = (f32[64,128]{1,0:T(8,128)S(1)}, f32[64,128]{1,0:T(8,128)S(1)}, u32[]{:S(2)}, u32[]{:S(2)}) collective-permute-start(f32[64,128]{1,0:T(8,128)S(1)} %get-tuple-element.64.refs_2_), channel_id=1, source_target_pairs={{4,8},{8,4},{5,9},{9,5},{6,10},{10,6},{7,11},{11,7},{20,24},{24,20... | collective-permute-start | bytes 98312 | tf_op jit(solution)/shard_map/ppermute | solution.py:28
  29.8 1.2 %collective-permute-done.9.refs_4_ = f32[64,128]{1,0:T(8,128)S(1)} collective-permute-done((f32[64,128]{1,0:T(8,128)S(1)}, f32[64,128]{1,0:T(8,128)S(1)}, u32[]{:S(2)}, u32[]{:S(2)}) %collective-permute-start.9) | collective-permute-done | bytes 32800 | tf_op jit(solution)/shard_map/ppermute | solution.py:28
  31.0 1.0 %shard_map.110 = (f32[3,8,32,128]{3,2,1,0:T(8,128)S(1)}, f32[4,32,128]{2,1,0:T(8,128)S(1)}, f32[2,32,128]{2,1,0:T(8,128)S(1)}, f32[32,128]{1,0:T(8,128)S(1)}) custom-call(f32[3,8,32,128]{3,2,1,0:T(8,128)S(1)} %get-tuple-element.55.partial, f32[32,128]{1,0:T(8,128)S(1)} %get-tuple-element.56.image_z.refs_8_, f32[24,128]{1,0:T(8,128)S(1)} %get-tuple-element.51.diag, ...), custom_call_target="tpu_custom_call" | custom-call | flops 226492416 | bytes 1048576 | tf_op jit(solution)/shard_map/pallas_call | solution.py:485
  32.0 12.7 %all_to_all.11 = f32[32,1,128]{2,1,0:T(1,128)S(1)} all-to-all(f32[32,1,128]{2,1,0:T(1,128)S(1)} %bitcast.20), channel_id=1, replica_groups=mesh['gx'=2,'gy'=4,'gz'=4] {'gx','gy','gz'}, dimensions={0} | all-to-all | bytes 32768 | tf_op jit(solution)/shard_map/all_to_all | solution.py:564
  44.8 1.7 %shard_map.111 = (bf16[3072,128]{1,0:T(8,128)(2,1)}, f32[768,128]{1,0:T(8,128)}) custom-call(f32[32,128]{1,0:T(8,128)S(1)} %bitcast.19, f32[768,128]{1,0:T(8,128)S(1)} %bitcast.14, f32[8,384,128]{2,1,0:T(8,128)S(1)} %get-tuple-element.42._.base, s32[8,128]{1,0:T(8,128)S(1)} %bitcast.18, bf16[384,192]{1,0:T(8,128)(2,1)S(1)} %get-tuple-element.66.lift, ...), custom_call_target="tpu_custom_call" | custom-call | flops 150994944 | bytes 1048576 | tf_op jit(solution)/shard_map/pallas_call | solution.py:485
  (11 shorter events, 0.0 us)
Async XLA Ops:
  2.1 6.4 %collective-permute-start.1 = (f32[104,128]{1,0:T(8,128)S(1)}, f32[104,128]{1,0:T(8,128)S(1)}, u32[]{:S(2)}, u32[]{:S(2)}) collective-permute-start(f32[104,128]{1,0:T(8,128)S(1)} %get-tuple-element.43), channel_id=1, source_target_pairs={{1,2},{2,1},{5,6},{6,5},{9,10},{10,9},{13,14},{14,13},{17,18},{18,... | collective-permute-start | bytes 159752 | tf_op jit(solution)/shard_map/ppermute | solution.py:28
  2.8 5.7 %collective-permute-start = (f32[104,128]{1,0:T(8,128)S(1)}, f32[104,128]{1,0:T(8,128)S(1)}, u32[]{:S(2)}, u32[]{:S(2)}) collective-permute-start(f32[104,128]{1,0:T(8,128)S(1)} %get-tuple-element.43), channel_id=1, source_target_pairs={{0,1},{1,0},{2,3},{3,2},{4,5},{5,4},{6,7},{7,6},{8,9},{9,8},{10,11... | collective-permute-start | bytes 159752 | tf_op jit(solution)/shard_map/ppermute | solution.py:28
  8.6 8.8 %collective-permute-start.2 = (f32[136,128]{1,0:T(8,128)S(1)}, f32[136,128]{1,0:T(8,128)S(1)}, u32[]{:S(2)}, u32[]{:S(2)}) collective-permute-start(f32[136,128]{1,0:T(8,128)S(1)} %get-tuple-element.47), channel_id=1, source_target_pairs={{0,16},{16,0},{1,17},{17,1},{2,18},{18,2},{3,19},{19,3},{4,20},{20... | collective-permute-start | bytes 208904 | tf_op jit(solution)/shard_map/ppermute | solution.py:28
  10.2 7.2 %collective-permute-start.4 = (f32[72,128]{1,0:T(8,128)S(1)}, f32[72,128]{1,0:T(8,128)S(1)}, u32[]{:S(2)}, u32[]{:S(2)}) collective-permute-start(f32[72,128]{1,0:T(8,128)S(1)} %get-tuple-element.48), channel_id=1, source_target_pairs={{4,8},{8,4},{5,9},{9,5},{6,10},{10,6},{7,11},{11,7},{20,24},{24,20... | collective-permute-start | bytes 110600 | tf_op jit(solution)/shard_map/ppermute | solution.py:28
  10.8 6.5 %collective-permute-start.3 = (f32[72,128]{1,0:T(8,128)S(1)}, f32[72,128]{1,0:T(8,128)S(1)}, u32[]{:S(2)}, u32[]{:S(2)}) collective-permute-start(f32[72,128]{1,0:T(8,128)S(1)} %get-tuple-element.48), channel_id=1, source_target_pairs={{0,4},{4,0},{8,12},{12,8},{1,5},{5,1},{9,13},{13,9},{2,6},{6,2},{1... | collective-permute-start | bytes 110600 | tf_op jit(solution)/shard_map/ppermute | solution.py:28
  18.2 26.6 %copy-start = (f32[3,32,2,4,128]{4,3,2,1,0:T(4,128)S(1)}, f32[3,32,2,4,128]{4,3,2,1,0:T(4,128)}, u32[]{:S(2)}) copy-start(f32[3,32,2,4,128]{4,3,2,1,0:T(4,128)} %param.10) | copy-start | bytes 1179652
  18.2 26.6 %copy-start.1 = (s32[2,4,128]{2,1,0:T(4,128)S(1)}, s32[2,4,128]{2,1,0:T(4,128)}, u32[]{:S(2)}) copy-start(s32[2,4,128]{2,1,0:T(4,128)} %param.13) | copy-start | bytes 12292
  18.2 4.5 %collective-permute-start.5 = (f32[136,128]{1,0:T(8,128)S(1)}, f32[136,128]{1,0:T(8,128)S(1)}, u32[]{:S(2)}, u32[]{:S(2)}) collective-permute-start(f32[136,128]{1,0:T(8,128)S(1)} %get-tuple-element.52.refs_0_), channel_id=1, source_target_pairs={{0,16},{16,0},{1,17},{17,1},{2,18},{18,2},{3,19},{19,3},{4,20},{20... | collective-permute-start | bytes 208904 | tf_op jit(solution)/shard_map/ppermute | solution.py:28
  18.8 4.0 %collective-permute-start.6 = (f32[72,128]{1,0:T(8,128)S(1)}, f32[72,128]{1,0:T(8,128)S(1)}, u32[]{:S(2)}, u32[]{:S(2)}) collective-permute-start(f32[72,128]{1,0:T(8,128)S(1)} %get-tuple-element.53.refs_1_), channel_id=1, source_target_pairs={{0,4},{4,0},{8,12},{12,8},{1,5},{5,1},{9,13},{13,9},{2,6},{6,2},{1... | collective-permute-start | bytes 110600 | tf_op jit(solution)/shard_map/ppermute | solution.py:28
  20.7 2.1 %collective-permute-start.7 = (f32[72,128]{1,0:T(8,128)S(1)}, f32[72,128]{1,0:T(8,128)S(1)}, u32[]{:S(2)}, u32[]{:S(2)}) collective-permute-start(f32[72,128]{1,0:T(8,128)S(1)} %get-tuple-element.54.refs_2_), channel_id=1, source_target_pairs={{4,8},{8,4},{5,9},{9,5},{6,10},{10,6},{7,11},{11,7},{20,24},{24,20... | collective-permute-start | bytes 110600 | tf_op jit(solution)/shard_map/ppermute | solution.py:28
  23.6 7.4 %collective-permute-start.8 = (f32[128,128]{1,0:T(8,128)S(1)}, f32[128,128]{1,0:T(8,128)S(1)}, u32[]{:S(2)}, u32[]{:S(2)}) collective-permute-start(f32[128,128]{1,0:T(8,128)S(1)} %get-tuple-element.62.refs_0_), channel_id=1, source_target_pairs={{0,16},{16,0},{1,17},{17,1},{2,18},{18,2},{3,19},{19,3},{4,20},{20... | collective-permute-start | bytes 196616 | tf_op jit(solution)/shard_map/ppermute | solution.py:28
  25.2 5.8 %collective-permute-start.9 = (f32[64,128]{1,0:T(8,128)S(1)}, f32[64,128]{1,0:T(8,128)S(1)}, u32[]{:S(2)}, u32[]{:S(2)}) collective-permute-start(f32[64,128]{1,0:T(8,128)S(1)} %get-tuple-element.63.refs_1_), channel_id=1, source_target_pairs={{0,4},{4,0},{8,12},{12,8},{1,5},{5,1},{9,13},{13,9},{2,6},{6,2},{1... | collective-permute-start | bytes 98312 | tf_op jit(solution)/shard_map/ppermute | solution.py:28
  29.1 1.9 %collective-permute-start.10 = (f32[64,128]{1,0:T(8,128)S(1)}, f32[64,128]{1,0:T(8,128)S(1)}, u32[]{:S(2)}, u32[]{:S(2)}) collective-permute-start(f32[64,128]{1,0:T(8,128)S(1)} %get-tuple-element.64.refs_2_), channel_id=1, source_target_pairs={{4,8},{8,4},{5,9},{9,5},{6,10},{10,6},{7,11},{11,7},{20,24},{24,20... | collective-permute-start | bytes 98312 | tf_op jit(solution)/shard_map/ppermute | solution.py:28

commit v4 on v3

--- a/solution.py
+++ b/solution.py
@@ -216,55 +216,34 @@
     return ref[pl.ds(f * geo.F * geo.M + m, geo.F, stride=geo.M), :]
 
 
-def kernel_pack(geo, trace, load, diag, fine, coeff, pack, vtrace, vload, vdiag, vfine, vcoeff, sems):
-    F, EZ, M = geo.F, geo.EZ, geo.M
-    for c in fetch([(trace, vtrace), (load, vload), (diag, vdiag), (fine, vfine), (coeff, vcoeff)], sems):
+def kernel_slabs(geo, trace, held, sx, sy, sems):
+    for c in fetch([(trace, held)], sems):
         c.wait()
-    half = EZ // 2
-
-    def packed(parts):
-        shape = parts[0].shape
-        lane = lane_iota(shape)
-        out = jnp.zeros(shape, f32)
-        for m, part in enumerate(parts):
-            start = (m // M) * half + (m % M) * STRIDE
-            out = jnp.where((lane >= start) & (lane < start + 5), moved(part, 0, start + 2), out)
-        return out
-
-    for f in range(3):
-        pack[f * F:(f + 1) * F] = packed([rows(v, geo, f, m) for v in (vtrace, vload) for m in range(M)])
-    weight = vfine[...].astype(f32) * vcoeff[...]
-    lines = [packed([vdiag[f * M + m:f * M + m + 1] for m in range(M)]) for f in range(3)]
-    lines.append(packed([weight[m:m + 1] for m in range(M)]))
-    for k in range(8):
-        pack[3 * F + k:3 * F + k + 1] = lines[min(k, 3)]
-
-
-def kernel_wide(geo, n, trace, _, *refs):
-    got, (trace_pack, own_pack, lines, sx, sy) = take(refs, n[2:], 5)
-    F, EX, EY, EZ = geo.F, geo.EX, geo.EY, geo.EZ
+    for f, (ref, count, step) in enumerate(((sx, geo.EY, 1), (sy, geo.EX, geo.EY))):
+        for k in range(count):
+            ref[part_of(geo, k, count)] = rows(held, geo, f, k * step)
+
+
+def packed(geo, parts, start=0, out=None, spread=1):
+    slot = lane_iota(parts[0].shape) // STRIDE
+    out = jnp.zeros(parts[0].shape, f32) if out is None else out
+    for k, part in enumerate(parts):
+        at = start + k * spread * STRIDE
+        out = jnp.where(slot == at // STRIDE, moved(part, 0, at + 2), out)
+    return out
+
+
+def kernel_pack(geo, n, columns, *refs):
+    got, (out,) = take(refs, n[:2], 1)
     parity, _ = place()
-    lane = lane_iota((F, EZ))
-
-    def mixed(rows_at):
-        if not got[0]:
-            return jnp.zeros((F, EZ), f32)[:rows_at.stop - rows_at.start]
-        below = chosen(got[0], parity[2], lambda r: r[rows_at], True)
-        above = chosen(got[0], parity[2], lambda r: r[rows_at])
-        return jnp.where(lane[:below.shape[0]] % STRIDE < 2, below, above)
-
-    lines[...] = mixed(slice(3 * F, 3 * F + 8))
-    for f in range(3):
-        v = mixed(slice(f * F, (f + 1) * F))
-        old = jnp.where(lane < EZ // 2, v, 0.0)
-        load = jnp.where(lane < EZ // 2, moved(v, EZ // 2, 0), 0.0)
-        trace_pack[f] = old
-        own_pack[f] = load - lines[f:f + 1] * old
-        if f < 2:
-            ref, count, step = ((sx, EY, 1), (sy, EX, EY))[f]
-            for k in range(count):
-                ref[part_of(geo, k, count)] = rows(trace, geo, f, k * step)
-            ref[part_of(geo, count, count)] = fold(geo, f, old)
+    rows_in = columns.shape[0]
+    out[:rows_in] = columns[...]
+    block = jnp.zeros((geo.F, geo.EZ), f32)
+    for a, count, spread in ((0, geo.EY, 1), (1, geo.EX, geo.EY)):
+        if got[a]:
+            parts = [chosen(got[a], parity[a], lambda r: r[part_of(geo, k, count)]) for k in range(count)]
+            block = packed(geo, parts, a * geo.EZ // 2, block, spread)
+    out[rows_in:] = block
 
 
 def take(refs, *sizes):
@@ -289,32 +268,51 @@
     return copies
 
 
-def kernel_prepare(geo, trace, load, diag_in, fine, coeff, schur, own, diag, weight, matrix, vload, vfine, vcoeff, vschur, sems):
+def kernel_prepare(geo, trace, load, diag_in, fine, coeff, schur, own, diag, weight, matrix, columns, vload, vfine, vcoeff, vschur, sems):
+    F, M = geo.F, geo.M
     copies = fetch([(load, vload), (diag_in, diag), (fine, vfine), (coeff, vcoeff), (schur, vschur)], sems)
     for c in copies:
         c.wait()
-    weight[...] = vfine[...].astype(f32) * vcoeff[...]
-    n = 6 * geo.F
+    scale = vfine[...].astype(f32) * vcoeff[...]
+    weight[...] = scale
+    n = 6 * F
     matrix[:n], matrix[n:] = split(vschur[...])
     for f in range(3):
-        for m in range(geo.M):
-            own[f, m] = rows(vload, geo, f, m) - diag[f * geo.M + m:f * geo.M + m + 1] * rows(trace, geo, f, m)
-
-
-def kernel_start(geo, n, trace, own, weight, schur, _, trace_pack, own_pack, lines, *refs):
-    got, halos, (partial, partial_pack), sends, (ghi, glo) = take(refs, n[:2], 2, 2, n[:2], 2)
+        for m in range(M):
+            own[f, m] = rows(vload, geo, f, m) - diag[f * M + m:f * M + m + 1] * rows(trace, geo, f, m)
+        old = packed(geo, [rows(trace, geo, f, m) for m in range(M)])
+        columns[f * F:(f + 1) * F] = packed(geo, [own[f, m] for m in range(M)], geo.EZ // 2, old)
+    lines = [packed(geo, [diag[f * M + m:f * M + m + 1] for m in range(M)]) for f in range(3)]
+    lines.append(packed(geo, [scale[m:m + 1] for m in range(M)]))
+    for k in range(8):
+        columns[3 * F + k:3 * F + k + 1] = lines[min(k, 3)]
+
+
+def kernel_start(geo, n, trace, own, weight, schur, _, *refs):
+    got, halos, (trace_pack, lines, partial, partial_pack), sends, (ghi, glo) = take(refs, n, 2, 4, n[:2], 2)
     F, EX, EY, EZ = geo.F, geo.EX, geo.EY, geo.EZ
     parity, _ = place()
-
-    def above(a, k):
-        at = part_of(geo, k, (EY, EX)[a])
-        return chosen(got[a], parity[a], lambda r: r[at]) if got[a] else jnp.zeros((at.stop - at.start, EZ), f32)
-
+    lane = lane_iota((F, EZ))
+
+    def mixed(rows_at):
+        if not got[2]:
+            return jnp.zeros((rows_at.stop - rows_at.start, EZ), f32)
+        below = chosen(got[2], parity[2], lambda r: r[rows_at], True)
+        above = chosen(got[2], parity[2], lambda r: r[rows_at])
+        return jnp.where(lane[:below.shape[0]] % STRIDE < 2, below, above)
+
+    lines[...] = mixed(slice(3 * F, 3 * F + 8))
+    own_pack = []
+    for f in range(3):
+        v = mixed(slice(f * F, (f + 1) * F))
+        trace_pack[f] = jnp.where(lane < EZ // 2, v, 0.0)
+        own_pack.append(jnp.where(lane < EZ // 2, moved(v, EZ // 2, 0), 0.0))
+    beside = mixed(slice(3 * F + 8, 4 * F + 8))
     for a, count in ((0, EY), (1, EX)):
         for k in range(count):
-            halos[a][k] = above(a, k)
+            halos[a][k] = chosen(got[a], parity[a], lambda r: r[part_of(geo, k, count)]) if got[a] else jnp.zeros((F, EZ), f32)
     halo = (lambda j: halos[0][j], lambda i: halos[1][i], trace_pack[2])
-    wide = (trace_pack[0], trace_pack[1], unfold(geo, 0, above(0, EY)), unfold(geo, 1, above(1, EX)))
+    wide = (trace_pack[0], trace_pack[1], beside, moved(beside, EZ // 2, 0))
     y = gather_and_apply(geo, lambda f, m: rows(trace, geo, f, m), halo, schur, ghi, glo, wide)
     spread(geo, y, weight[...], lambda f, m: own[f, m], -1.0, partial, sends, parity,
            lines[3:4], lambda f: own_pack[f], {f: partial_pack.at[f] for f in range(3)})
@@ -533,24 +531,25 @@
         values = list(values)
         return [[values.pop(0) for _ in range(k)] for k in n[:2]]
 
-    packed, held = call(functools.partial(kernel_pack, geo), [((3 * F + 8, EZ), f32), (trace.shape, f32)], [trace, load, diag_in, fine, scale],
-                        [like(load), like(diag_in), like(fine), like(scale), dma((5,))], 1 << 20, hbm_args=range(5))
-    got = exchange(AXES[2:], [[packed, packed]])
-    own, diag, weight, schur = call(
-        functools.partial(kernel_prepare, geo), [(full, f32), ((3 * M, EZ), f32), ((M, EZ), f32), ((2 * N, N), bf16)],
+    held, sx, sy = call(functools.partial(kernel_slabs, geo), [(trace.shape, f32)] + [(s, f32) for s in slab_sent], [trace], [dma((1,))],
+                        1 << 20, hbm_args=(0,))
+    old = exchange(AXES[:2], [[sx, sx], [sy, sy]])
+    own, diag, weight, schur, columns = call(
+        functools.partial(kernel_prepare, geo),
+        [(full, f32), ((3 * M, EZ), f32), ((M, EZ), f32), ((2 * N, N), bf16), ((3 * F + 8, EZ), f32)],
         [held, load, diag_in, fine, scale, schur_op], [like(load), like(fine), like(scale), like(schur_op), dma((5,))],
         flops, hbm_args=(1, 2, 3, 4, 5))
     base, lift = call(
         functools.partial(kernel_volume, geo), [((M, dofs, EZ), f32), (lift_op.shape, bf16)], [nodal, fine, volume_op, lift_op.T],
         [pltpu.VMEM((dofs * M, EZ), f32), like(nodal), like(fine), like(volume_op), like(lift_op.T), dma((4,))],
         2 * dofs * dofs * M * EZ, hbm_args=(0, 1, 2, 3))
-    trace_pack, own_pack, lines, sx, sy = call(
-        functools.partial(kernel_wide, geo, n), [(pack, f32), (pack, f32), (line, f32)] + [(s, f32) for s in slab_wide],
-        [held, weight] + flat(got), [], 1 << 20)
-    got = exchange(AXES[:2], [[sx, sx], [sy, sy]])
-    out = call(functools.partial(kernel_start, geo, n), halo_outs + [(full, f32), (pack, f32)] + send_outs(slab_wide),
-               [held, own, weight, schur, base, trace_pack, own_pack, lines] + flat(got), halves(M + 1), flops)
-    halo_old, partial, partial_pack, sent = [*out[:2], trace_pack], out[2], out[3], grouped(out[4:])
+    wide = call(functools.partial(kernel_pack, geo, n), [((4 * F + 8, EZ), f32)], [columns] + flat(old), [], 1 << 20)[0]
+    got = exchange(AXES[2:], [[wide, wide]])
+    out = call(functools.partial(kernel_start, geo, n),
+               halo_outs + [(pack, f32), (line, f32), (full, f32), (pack, f32)] + send_outs(slab_wide),
+               [held, own, weight, schur, base] + flat(old) + flat(got), halves(M + 1), flops)
+    trace_pack, lines, partial, partial_pack, sent = out[2], out[3], out[4], out[5], grouped(out[6:])
+    halo_old = [*out[:2], trace_pack]
     got = exchange(AXES[:2], sent)
     out = call(functools.partial(kernel_middle, geo, n),
                [(full, f32), ((F, EZ), f32)] + halo_outs + [(full, f32), ((F, EZ), f32)] + send_outs(slab_sent) + [((2, 8, EZ), f32)],

time: 46.7 us -> 46.4 us (level)
  blocking collectives: 12.7 us -> 12.2 us
    all_to_all x1, blocking collectives: 12.7 us -> 12.2 us  [body(): message = lax.all_to_all(message, AXES, 0, 0, tiled=True)]
  transfers between devices with their start and end apart: 11 -> 11, of which waited for: 2 -> 3; matrix products, arithmetic and copies ran while one was open for 0% -> 0% of each run, Pallas kernels for 7% -> 8%
where the time goes in v4:
time: 46.4 us; the launch traced here: 46.1 us
  starting transfers between devices  21.1 us (45%)
  blocking collectives  12.2 us (26%)
  Pallas kernels  9.11 us (20%)
  waiting for transfers between devices  2.91 us (6%)
  between operations  0.76 us (2%)
    ppermute x11, starting transfers between devices, exchange(): lax.ppermute(v, axis, pairs(axis, odd))  21.1 us
    all_to_all x1, blocking collectives, body(): message = lax.all_to_all(message, AXES, 0, 0, tiled=True)  12.2 us
    pallas_call x8, Pallas kernels, call(): pl.pallas_call(kernel, out_shape=[(HBM if k in hbm_outs else jax.ShapeDty...  9.11 us
    ppermute x11, waiting for transfers between devices, exchange(): lax.ppermute(v, axis, pairs(axis, odd))  2.91 us
  transfers between devices with their start and end apart: 11, of which 3 were waited for; matrix products, arithmetic and copies ran while one was open for 0% of the time, Pallas kernels for 8%

profile of v4, /device:TPU:0, one launch (start us, length us, event | category | flops | bytes accessed | tf_op | source)
XLA Modules:
  0.0 46.1 jit_solution(6073795240316769026)
XLA Ops:
  0.6 1.0 %shard_map.104 = (f32[768,128]{1,0:T(8,128)S(1)}, f32[128,128]{1,0:T(8,128)S(1)}, f32[64,128]{1,0:T(8,128)S(1)}) custom-call(f32[768,128]{1,0:T(8,128)} %bitcast.13), custom_call_target="tpu_custom_call" | custom-call | flops 1048576 | bytes 1048576 | tf_op jit(solution)/shard_map/pallas_call | solution.py:483
  1.7 3.1 %collective-permute-start = (f32[128,128]{1,0:T(8,128)S(1)}, f32[128,128]{1,0:T(8,128)S(1)}, u32[]{:S(2)}, u32[]{:S(2)}) collective-permute-start(f32[128,128]{1,0:T(8,128)S(1)} %get-tuple-element.42), channel_id=1, source_target_pairs={{0,16},{16,0},{1,17},{17,1},{2,18},{18,2},{3,19},{19,3},{4,20},{20... | collective-permute-start | bytes 196616 | tf_op jit(solution)/shard_map/ppermute | solution.py:28
  4.7 0.7 %collective-permute-start.2 = (f32[64,128]{1,0:T(8,128)S(1)}, f32[64,128]{1,0:T(8,128)S(1)}, u32[]{:S(2)}, u32[]{:S(2)}) collective-permute-start(f32[64,128]{1,0:T(8,128)S(1)} %get-tuple-element.43), channel_id=1, source_target_pairs={{4,8},{8,4},{5,9},{9,5},{6,10},{10,6},{7,11},{11,7},{20,24},{24,20... | collective-permute-start | bytes 98312 | tf_op jit(solution)/shard_map/ppermute | solution.py:28
  5.4 4.5 %collective-permute-start.1 = (f32[64,128]{1,0:T(8,128)S(1)}, f32[64,128]{1,0:T(8,128)S(1)}, u32[]{:S(2)}, u32[]{:S(2)}) collective-permute-start(f32[64,128]{1,0:T(8,128)S(1)} %get-tuple-element.43), channel_id=1, source_target_pairs={{0,4},{4,0},{8,12},{12,8},{1,5},{5,1},{9,13},{13,9},{2,6},{6,2},{1... | collective-permute-start | bytes 98312 | tf_op jit(solution)/shard_map/ppermute | solution.py:28
  9.8 1.5 %shard_map.105 = (f32[3,8,32,128]{3,2,1,0:T(8,128)S(1)}, f32[24,128]{1,0:T(8,128)S(1)}, f32[8,128]{1,0:T(8,128)S(1)}, bf16[384,192]{1,0:T(8,128)(2,1)S(1)}, f32[104,128]{1,0:T(8,128)S(1)}) custom-call(f32[768,128]{1,0:T(8,128)S(1)} %get-tuple-element.37.trace, f32[768,128]{1,0:T(8,128)} %bitcast.21, f32[24,128]{1,0:T(8,128)} %bitcast.23, s32[8,128]{1,0:T(8,128)} %bitcast.16, ...), custom_call_target="tpu_custom_call" | custom-call | flops 226492416 | bytes 1048576 | tf_op jit(solution)/shard_map/pallas_call | solution.py:483
  11.4 0.4 collective-permute-done.1.refs_1_
  11.7 0.1 shard_map.107
  11.8 0.7 %collective-permute-start.4 = (f32[136,128]{1,0:T(8,128)S(1)}, f32[136,128]{1,0:T(8,128)S(1)}, u32[]{:S(2)}, u32[]{:S(2)}) collective-permute-start(f32[136,128]{1,0:T(8,128)S(1)} %shard_map.107), channel_id=1, source_target_pairs={{1,2},{2,1},{5,6},{6,5},{9,10},{10,9},{13,14},{14,13},{17,18},{18,... | collective-permute-start | bytes 208904 | tf_op jit(solution)/shard_map/ppermute | solution.py:28
  12.5 2.9 %collective-permute-start.3 = (f32[136,128]{1,0:T(8,128)S(1)}, f32[136,128]{1,0:T(8,128)S(1)}, u32[]{:S(2)}, u32[]{:S(2)}) collective-permute-start(f32[136,128]{1,0:T(8,128)S(1)} %shard_map.107), channel_id=1, source_target_pairs={{0,1},{1,0},{2,3},{3,2},{4,5},{5,4},{6,7},{7,6},{8,9},{9,8},{10,11... | collective-permute-start | bytes 208904 | tf_op jit(solution)/shard_map/ppermute | solution.py:28
  15.4 2.0 %shard_map.106 = (f32[8,384,128]{2,1,0:T(8,128)S(1)}, bf16[384,192]{1,0:T(8,128)(2,1)S(1)}) custom-call(bf16[3072,128]{1,0:T(8,128)(2,1)} %bitcast.20, s32[8,128]{1,0:T(8,128)} %bitcast.17, bf16[384,384]{1,0:T(8,128)(2,1)} %operator.1, bf16[192,384]{1,0:T(8,128)(2,1)} %bitcast.22), custom_call_target="tpu_custom_call" | custom-call | flops 301989888 | bytes 1048576 | tf_op jit(solution)/shard_map/pallas_call | solution.py:483
  17.5 0.8 %shard_map.108 = (f32[4,32,128]{2,1,0:T(8,128)S(1)}, f32[2,32,128]{2,1,0:T(8,128)S(1)}, f32[3,32,128]{2,1,0:T(8,128)S(1)}, f32[8,128]{1,0:T(8,128)S(1)}, f32[3,8...) custom-call(f32[768,128]{1,0:T(8,128)S(1)} %get-tuple-element.37.tra, ...), custom_call_target="tpu_custom_call" | custom-call | flops 226492416 | bytes 1048576 | tf_op jit(solution)/shard_map/pallas_call | solution.py:483
  18.3 0.0 copy-start
  18.4 0.6 %collective-permute-start.5 = (f32[136,128]{1,0:T(8,128)S(1)}, f32[136,128]{1,0:T(8,128)S(1)}, u32[]{:S(2)}, u32[]{:S(2)}) collective-permute-start(f32[136,128]{1,0:T(8,128)S(1)} %get-tuple-element.49.refs_0_), channel_id=1, source_target_pairs={{0,16},{16,0},{1,17},{17,1},{2,18},{18,2},{3,19},{19,3},{4,20},{20... | collective-permute-start | bytes 208904 | tf_op jit(solution)/shard_map/ppermute | solution.py:28
  18.9 2.0 %collective-permute-start.6 = (f32[72,128]{1,0:T(8,128)S(1)}, f32[72,128]{1,0:T(8,128)S(1)}, u32[]{:S(2)}, u32[]{:S(2)}) collective-permute-start(f32[72,128]{1,0:T(8,128)S(1)} %get-tuple-element.50.refs_1_), channel_id=1, source_target_pairs={{0,4},{4,0},{8,12},{12,8},{1,5},{5,1},{9,13},{13,9},{2,6},{6,2},{1... | collective-permute-start | bytes 110600 | tf_op jit(solution)/shard_map/ppermute | solution.py:28
  20.9 0.7 %collective-permute-start.7 = (f32[72,128]{1,0:T(8,128)S(1)}, f32[72,128]{1,0:T(8,128)S(1)}, u32[]{:S(2)}, u32[]{:S(2)}) collective-permute-start(f32[72,128]{1,0:T(8,128)S(1)} %get-tuple-element.51.refs_2_), channel_id=1, source_target_pairs={{4,8},{8,4},{5,9},{9,5},{6,10},{10,6},{7,11},{11,7},{20,24},{24,20... | collective-permute-start | bytes 110600 | tf_op jit(solution)/shard_map/ppermute | solution.py:28
  21.6 1.3 %collective-permute-done.6.refs_4_ = f32[72,128]{1,0:T(8,128)S(1)} collective-permute-done((f32[72,128]{1,0:T(8,128)S(1)}, f32[72,128]{1,0:T(8,128)S(1)}, u32[]{:S(2)}, u32[]{:S(2)}) %collective-permute-start.6) | collective-permute-done | bytes 36896 | tf_op jit(solution)/shard_map/ppermute | solution.py:28
  22.9 0.9 %shard_map.109 = (f32[3,8,32,128]{3,2,1,0:T(8,128)S(1)}, f32[32,128]{1,0:T(8,128)S(1)}, f32[4,32,128]{2,1,0:T(8,128)S(1)}, f32[2,32,128]{2,1,0:T(8,128)S(1)}, f3...) custom-call(f32[3,8,32,128]{3,2,1,0:T(8,128)S(1)} %get-tuple-element, ...), custom_call_target="tpu_custom_call" | custom-call | flops 226492416 | bytes 1048576 | tf_op jit(solution)/shard_map/pallas_call | solution.py:483
  23.8 1.6 %collective-permute-start.8 = (f32[128,128]{1,0:T(8,128)S(1)}, f32[128,128]{1,0:T(8,128)S(1)}, u32[]{:S(2)}, u32[]{:S(2)}) collective-permute-start(f32[128,128]{1,0:T(8,128)S(1)} %get-tuple-element.59.refs_0_), channel_id=1, source_target_pairs={{0,16},{16,0},{1,17},{17,1},{2,18},{18,2},{3,19},{19,3},{4,20},{20... | collective-permute-start | bytes 196616 | tf_op jit(solution)/shard_map/ppermute | solution.py:28
  25.4 3.9 %collective-permute-start.9 = (f32[64,128]{1,0:T(8,128)S(1)}, f32[64,128]{1,0:T(8,128)S(1)}, u32[]{:S(2)}, u32[]{:S(2)}) collective-permute-start(f32[64,128]{1,0:T(8,128)S(1)} %get-tuple-element.60.refs_1_), channel_id=1, source_target_pairs={{0,4},{4,0},{8,12},{12,8},{1,5},{5,1},{9,13},{13,9},{2,6},{6,2},{1... | collective-permute-start | bytes 98312 | tf_op jit(solution)/shard_map/ppermute | solution.py:28
  29.3 0.7 %collective-permute-start.10 = (f32[64,128]{1,0:T(8,128)S(1)}, f32[64,128]{1,0:T(8,128)S(1)}, u32[]{:S(2)}, u32[]{:S(2)}) collective-permute-start(f32[64,128]{1,0:T(8,128)S(1)} %get-tuple-element.61.refs_2_), channel_id=1, source_target_pairs={{4,8},{8,4},{5,9},{9,5},{6,10},{10,6},{7,11},{11,7},{20,24},{24,20... | collective-permute-start | bytes 98312 | tf_op jit(solution)/shard_map/ppermute | solution.py:28
  29.9 1.2 %collective-permute-done.9.refs_4_ = f32[64,128]{1,0:T(8,128)S(1)} collective-permute-done((f32[64,128]{1,0:T(8,128)S(1)}, f32[64,128]{1,0:T(8,128)S(1)}, u32[]{:S(2)}, u32[]{:S(2)}) %collective-permute-start.9) | collective-permute-done | bytes 32800 | tf_op jit(solution)/shard_map/ppermute | solution.py:28
  31.2 1.0 %shard_map.110 = (f32[3,8,32,128]{3,2,1,0:T(8,128)S(1)}, f32[4,32,128]{2,1,0:T(8,128)S(1)}, f32[2,32,128]{2,1,0:T(8,128)S(1)}, f32[32,128]{1,0:T(8,128)S(1)}) custom-call(f32[3,8,32,128]{3,2,1,0:T(8,128)S(1)} %get-tuple-element.52.partial, f32[32,128]{1,0:T(8,128)S(1)} %get-tuple-element.53.image_z.refs_8_, f32[24,128]{1,0:T(8,128)S(1)} %get-tuple-element.47.diag, ...), custom_call_target="tpu_custom_call" | custom-call | flops 226492416 | bytes 1048576 | tf_op jit(solution)/shard_map/pallas_call | solution.py:483
  32.2 12.2 %all_to_all.11 = f32[32,1,128]{2,1,0:T(1,128)S(1)} all-to-all(f32[32,1,128]{2,1,0:T(1,128)S(1)} %bitcast.19), channel_id=1, replica_groups=mesh['gx'=2,'gy'=4,'gz'=4] {'gx','gy','gz'}, dimensions={0} | all-to-all | bytes 32768 | tf_op jit(solution)/shard_map/all_to_all | solution.py:563
  44.4 1.7 %shard_map.111 = (bf16[3072,128]{1,0:T(8,128)(2,1)}, f32[768,128]{1,0:T(8,128)}) custom-call(f32[32,128]{1,0:T(8,128)S(1)} %bitcast.15, f32[768,128]{1,0:T(8,128)S(1)} %bitcast.14, f32[8,384,128]{2,1,0:T(8,128)S(1)} %get-tuple-element.41._.base, s32[8,128]{1,0:T(8,128)S(1)} %bitcast.18, bf16[384,192]{1,0:T(8,128)(2,1)S(1)} %get-tuple-element.63.lift, ...), custom_call_target="tpu_custom_call" | custom-call | flops 150994944 | bytes 1048576 | tf_op jit(solution)/shard_map/pallas_call | solution.py:483
  (11 shorter events, 0.0 us)
Async XLA Ops:
  1.7 10.1 %collective-permute-start = (f32[128,128]{1,0:T(8,128)S(1)}, f32[128,128]{1,0:T(8,128)S(1)}, u32[]{:S(2)}, u32[]{:S(2)}) collective-permute-start(f32[128,128]{1,0:T(8,128)S(1)} %get-tuple-element.42), channel_id=1, source_target_pairs={{0,16},{16,0},{1,17},{17,1},{2,18},{18,2},{3,19},{19,3},{4,20},{20... | collective-permute-start | bytes 196616 | tf_op jit(solution)/shard_map/ppermute | solution.py:28
  4.7 6.6 %collective-permute-start.2 = (f32[64,128]{1,0:T(8,128)S(1)}, f32[64,128]{1,0:T(8,128)S(1)}, u32[]{:S(2)}, u32[]{:S(2)}) collective-permute-start(f32[64,128]{1,0:T(8,128)S(1)} %get-tuple-element.43), channel_id=1, source_target_pairs={{4,8},{8,4},{5,9},{9,5},{6,10},{10,6},{7,11},{11,7},{20,24},{24,20... | collective-permute-start | bytes 98312 | tf_op jit(solution)/shard_map/ppermute | solution.py:28
  5.4 6.4 %collective-permute-start.1 = (f32[64,128]{1,0:T(8,128)S(1)}, f32[64,128]{1,0:T(8,128)S(1)}, u32[]{:S(2)}, u32[]{:S(2)}) collective-permute-start(f32[64,128]{1,0:T(8,128)S(1)} %get-tuple-element.43), channel_id=1, source_target_pairs={{0,4},{4,0},{8,12},{12,8},{1,5},{5,1},{9,13},{13,9},{2,6},{6,2},{1... | collective-permute-start | bytes 98312 | tf_op jit(solution)/shard_map/ppermute | solution.py:28
  11.8 5.6 %collective-permute-start.4 = (f32[136,128]{1,0:T(8,128)S(1)}, f32[136,128]{1,0:T(8,128)S(1)}, u32[]{:S(2)}, u32[]{:S(2)}) collective-permute-start(f32[136,128]{1,0:T(8,128)S(1)} %shard_map.107), channel_id=1, source_target_pairs={{1,2},{2,1},{5,6},{6,5},{9,10},{10,9},{13,14},{14,13},{17,18},{18,... | collective-permute-start | bytes 208904 | tf_op jit(solution)/shard_map/ppermute | solution.py:28
  12.5 5.0 %collective-permute-start.3 = (f32[136,128]{1,0:T(8,128)S(1)}, f32[136,128]{1,0:T(8,128)S(1)}, u32[]{:S(2)}, u32[]{:S(2)}) collective-permute-start(f32[136,128]{1,0:T(8,128)S(1)} %shard_map.107), channel_id=1, source_target_pairs={{0,1},{1,0},{2,3},{3,2},{4,5},{5,4},{6,7},{7,6},{8,9},{9,8},{10,11... | collective-permute-start | bytes 208904 | tf_op jit(solution)/shard_map/ppermute | solution.py:28
  18.3 26.0 %copy-start = (f32[3,32,2,4,128]{4,3,2,1,0:T(4,128)S(1)}, f32[3,32,2,4,128]{4,3,2,1,0:T(4,128)}, u32[]{:S(2)}) copy-start(f32[3,32,2,4,128]{4,3,2,1,0:T(4,128)} %param.10) | copy-start | bytes 1179652
  18.3 26.0 %copy-start.1 = (s32[2,4,128]{2,1,0:T(4,128)S(1)}, s32[2,4,128]{2,1,0:T(4,128)}, u32[]{:S(2)}) copy-start(s32[2,4,128]{2,1,0:T(4,128)} %param.13) | copy-start | bytes 12292
  18.4 4.5 %collective-permute-start.5 = (f32[136,128]{1,0:T(8,128)S(1)}, f32[136,128]{1,0:T(8,128)S(1)}, u32[]{:S(2)}, u32[]{:S(2)}) collective-permute-start(f32[136,128]{1,0:T(8,128)S(1)} %get-tuple-element.49.refs_0_), channel_id=1, source_target_pairs={{0,16},{16,0},{1,17},{17,1},{2,18},{18,2},{3,19},{19,3},{4,20},{20... | collective-permute-start | bytes 208904 | tf_op jit(solution)/shard_map/ppermute | solution.py:28
  18.9 4.0 %collective-permute-start.6 = (f32[72,128]{1,0:T(8,128)S(1)}, f32[72,128]{1,0:T(8,128)S(1)}, u32[]{:S(2)}, u32[]{:S(2)}) collective-permute-start(f32[72,128]{1,0:T(8,128)S(1)} %get-tuple-element.50.refs_1_), channel_id=1, source_target_pairs={{0,4},{4,0},{8,12},{12,8},{1,5},{5,1},{9,13},{13,9},{2,6},{6,2},{1... | collective-permute-start | bytes 110600 | tf_op jit(solution)/shard_map/ppermute | solution.py:28
  20.9 1.9 %collective-permute-start.7 = (f32[72,128]{1,0:T(8,128)S(1)}, f32[72,128]{1,0:T(8,128)S(1)}, u32[]{:S(2)}, u32[]{:S(2)}) collective-permute-start(f32[72,128]{1,0:T(8,128)S(1)} %get-tuple-element.51.refs_2_), channel_id=1, source_target_pairs={{4,8},{8,4},{5,9},{9,5},{6,10},{10,6},{7,11},{11,7},{20,24},{24,20... | collective-permute-start | bytes 110600 | tf_op jit(solution)/shard_map/ppermute | solution.py:28
  23.8 7.4 %collective-permute-start.8 = (f32[128,128]{1,0:T(8,128)S(1)}, f32[128,128]{1,0:T(8,128)S(1)}, u32[]{:S(2)}, u32[]{:S(2)}) collective-permute-start(f32[128,128]{1,0:T(8,128)S(1)} %get-tuple-element.59.refs_0_), channel_id=1, source_target_pairs={{0,16},{16,0},{1,17},{17,1},{2,18},{18,2},{3,19},{19,3},{4,20},{20... | collective-permute-start | bytes 196616 | tf_op jit(solution)/shard_map/ppermute | solution.py:28
  25.4 5.8 %collective-permute-start.9 = (f32[64,128]{1,0:T(8,128)S(1)}, f32[64,128]{1,0:T(8,128)S(1)}, u32[]{:S(2)}, u32[]{:S(2)}) collective-permute-start(f32[64,128]{1,0:T(8,128)S(1)} %get-tuple-element.60.refs_1_), channel_id=1, source_target_pairs={{0,4},{4,0},{8,12},{12,8},{1,5},{5,1},{9,13},{13,9},{2,6},{6,2},{1... | collective-permute-start | bytes 98312 | tf_op jit(solution)/shard_map/ppermute | solution.py:28
  29.3 1.9 %collective-permute-start.10 = (f32[64,128]{1,0:T(8,128)S(1)}, f32[64,128]{1,0:T(8,128)S(1)}, u32[]{:S(2)}, u32[]{:S(2)}) collective-permute-start(f32[64,128]{1,0:T(8,128)S(1)} %get-tuple-element.61.refs_2_), channel_id=1, source_target_pairs={{4,8},{8,4},{5,9},{9,5},{6,10},{10,6},{7,11},{11,7},{20,24},{24,20... | collective-permute-start | bytes 98312 | tf_op jit(solution)/shard_map/ppermute | solution.py:28

commit v5 on v4

--- a/solution.py
+++ b/solution.py
@@ -238,12 +238,12 @@
     parity, _ = place()
     rows_in = columns.shape[0]
     out[:rows_in] = columns[...]
-    block = jnp.zeros((geo.F, geo.EZ), f32)
     for a, count, spread in ((0, geo.EY, 1), (1, geo.EX, geo.EY)):
+        block = jnp.zeros((geo.F, geo.EZ), f32)
         if got[a]:
             parts = [chosen(got[a], parity[a], lambda r: r[part_of(geo, k, count)]) for k in range(count)]
-            block = packed(geo, parts, a * geo.EZ // 2, block, spread)
-    out[rows_in:] = block
+            block = packed(geo, parts, 0, block, spread)
+        out[rows_in + 8 * a:rows_in + 8 * a + 8] = fold(geo, a, block)
 
 
 def take(refs, *sizes):
@@ -307,12 +307,12 @@
         v = mixed(slice(f * F, (f + 1) * F))
         trace_pack[f] = jnp.where(lane < EZ // 2, v, 0.0)
         own_pack.append(jnp.where(lane < EZ // 2, moved(v, EZ // 2, 0), 0.0))
-    beside = mixed(slice(3 * F + 8, 4 * F + 8))
+    beside = [unfold(geo, a, mixed(slice(3 * F + 8 + 8 * a, 3 * F + 16 + 8 * a))) for a in (0, 1)]
     for a, count in ((0, EY), (1, EX)):
         for k in range(count):
             halos[a][k] = chosen(got[a], parity[a], lambda r: r[part_of(geo, k, count)]) if got[a] else jnp.zeros((F, EZ), f32)
     halo = (lambda j: halos[0][j], lambda i: halos[1][i], trace_pack[2])
-    wide = (trace_pack[0], trace_pack[1], beside, moved(beside, EZ // 2, 0))
+    wide = (trace_pack[0], trace_pack[1], *beside)
     y = gather_and_apply(geo, lambda f, m: rows(trace, geo, f, m), halo, schur, ghi, glo, wide)
     spread(geo, y, weight[...], lambda f, m: own[f, m], -1.0, partial, sends, parity,
            lines[3:4], lambda f: own_pack[f], {f: partial_pack.at[f] for f in range(3)})
@@ -543,7 +543,7 @@
         functools.partial(kernel_volume, geo), [((M, dofs, EZ), f32), (lift_op.shape, bf16)], [nodal, fine, volume_op, lift_op.T],
         [pltpu.VMEM((dofs * M, EZ), f32), like(nodal), like(fine), like(volume_op), like(lift_op.T), dma((4,))],
         2 * dofs * dofs * M * EZ, hbm_args=(0, 1, 2, 3))
-    wide = call(functools.partial(kernel_pack, geo, n), [((4 * F + 8, EZ), f32)], [columns] + flat(old), [], 1 << 20)[0]
+    wide = call(functools.partial(kernel_pack, geo, n), [((3 * F + 24, EZ), f32)], [columns] + flat(old), [], 1 << 20)[0]
     got = exchange(AXES[2:], [[wide, wide]])
     out = call(functools.partial(kernel_start, geo, n),
                halo_outs + [(pack, f32), (line, f32), (full, f32), (pack, f32)] + send_outs(slab_wide),

time: 46.4 us -> 46.3 us (level)
  no operation moved by 1% of the time
where the time goes in v5:
time: 46.3 us; the launch traced here: 46 us
  starting transfers between devices  21.1 us (46%)
  blocking collectives  12.1 us (26%)
  Pallas kernels  9.16 us (20%)
  waiting for transfers between devices  2.91 us (6%)
  between operations  0.75 us (2%)
    ppermute x11, starting transfers between devices, exchange(): lax.ppermute(v, axis, pairs(axis, odd))  21.1 us
    all_to_all x1, blocking collectives, body(): message = lax.all_to_all(message, AXES, 0, 0, tiled=True)  12.1 us
    pallas_call x8, Pallas kernels, call(): pl.pallas_call(kernel, out_shape=[(HBM if k in hbm_outs else jax.ShapeDty...  9.16 us
    ppermute x11, waiting for transfers between devices, exchange(): lax.ppermute(v, axis, pairs(axis, odd))  2.91 us
  transfers between devices with their start and end apart: 11, of which 3 were waited for; matrix products, arithmetic and copies ran while one was open for 0% of the time, Pallas kernels for 8%

profile of v5, /device:TPU:0, one launch (start us, length us, event | category | flops | bytes accessed | tf_op | source)
XLA Modules:
  0.0 46.0 jit_solution(11671527000166019235)
XLA Ops:
  0.6 1.0 %shard_map.104 = (f32[768,128]{1,0:T(8,128)S(1)}, f32[128,128]{1,0:T(8,128)S(1)}, f32[64,128]{1,0:T(8,128)S(1)}) custom-call(f32[768,128]{1,0:T(8,128)} %bitcast.13), custom_call_target="tpu_custom_call" | custom-call | flops 1048576 | bytes 1048576 | tf_op jit(solution)/shard_map/pallas_call | solution.py:483
  1.7 3.1 %collective-permute-start = (f32[128,128]{1,0:T(8,128)S(1)}, f32[128,128]{1,0:T(8,128)S(1)}, u32[]{:S(2)}, u32[]{:S(2)}) collective-permute-start(f32[128,128]{1,0:T(8,128)S(1)} %get-tuple-element.42), channel_id=1, source_target_pairs={{0,16},{16,0},{1,17},{17,1},{2,18},{18,2},{3,19},{19,3},{4,20},{20... | collective-permute-start | bytes 196616 | tf_op jit(solution)/shard_map/ppermute | solution.py:28
  4.7 0.7 %collective-permute-start.2 = (f32[64,128]{1,0:T(8,128)S(1)}, f32[64,128]{1,0:T(8,128)S(1)}, u32[]{:S(2)}, u32[]{:S(2)}) collective-permute-start(f32[64,128]{1,0:T(8,128)S(1)} %get-tuple-element.43), channel_id=1, source_target_pairs={{4,8},{8,4},{5,9},{9,5},{6,10},{10,6},{7,11},{11,7},{20,24},{24,20... | collective-permute-start | bytes 98312 | tf_op jit(solution)/shard_map/ppermute | solution.py:28
  5.4 4.5 %collective-permute-start.1 = (f32[64,128]{1,0:T(8,128)S(1)}, f32[64,128]{1,0:T(8,128)S(1)}, u32[]{:S(2)}, u32[]{:S(2)}) collective-permute-start(f32[64,128]{1,0:T(8,128)S(1)} %get-tuple-element.43), channel_id=1, source_target_pairs={{0,4},{4,0},{8,12},{12,8},{1,5},{5,1},{9,13},{13,9},{2,6},{6,2},{1... | collective-permute-start | bytes 98312 | tf_op jit(solution)/shard_map/ppermute | solution.py:28
  9.8 1.5 %shard_map.105 = (f32[3,8,32,128]{3,2,1,0:T(8,128)S(1)}, f32[24,128]{1,0:T(8,128)S(1)}, f32[8,128]{1,0:T(8,128)S(1)}, bf16[384,192]{1,0:T(8,128)(2,1)S(1)}, f32[104,128]{1,0:T(8,128)S(1)}) custom-call(f32[768,128]{1,0:T(8,128)S(1)} %get-tuple-element.37.trace, f32[768,128]{1,0:T(8,128)} %bitcast.21, f32[24,128]{1,0:T(8,128)} %bitcast.23, s32[8,128]{1,0:T(8,128)} %bitcast.16, ...), custom_call_target="tpu_custom_call" | custom-call | flops 226492416 | bytes 1048576 | tf_op jit(solution)/shard_map/pallas_call | solution.py:483
  11.4 0.4 collective-permute-done.1.refs_1_
  11.7 0.2 shard_map.107
  11.9 0.7 %collective-permute-start.4 = (f32[120,128]{1,0:T(8,128)S(1)}, f32[120,128]{1,0:T(8,128)S(1)}, u32[]{:S(2)}, u32[]{:S(2)}) collective-permute-start(f32[120,128]{1,0:T(8,128)S(1)} %shard_map.107), channel_id=1, source_target_pairs={{1,2},{2,1},{5,6},{6,5},{9,10},{10,9},{13,14},{14,13},{17,18},{18,... | collective-permute-start | bytes 184328 | tf_op jit(solution)/shard_map/ppermute | solution.py:28
  12.6 2.9 %collective-permute-start.3 = (f32[120,128]{1,0:T(8,128)S(1)}, f32[120,128]{1,0:T(8,128)S(1)}, u32[]{:S(2)}, u32[]{:S(2)}) collective-permute-start(f32[120,128]{1,0:T(8,128)S(1)} %shard_map.107), channel_id=1, source_target_pairs={{0,1},{1,0},{2,3},{3,2},{4,5},{5,4},{6,7},{7,6},{8,9},{9,8},{10,11... | collective-permute-start | bytes 184328 | tf_op jit(solution)/shard_map/ppermute | solution.py:28
  15.5 2.0 %shard_map.106 = (f32[8,384,128]{2,1,0:T(8,128)S(1)}, bf16[384,192]{1,0:T(8,128)(2,1)S(1)}) custom-call(bf16[3072,128]{1,0:T(8,128)(2,1)} %bitcast.20, s32[8,128]{1,0:T(8,128)} %bitcast.17, bf16[384,384]{1,0:T(8,128)(2,1)} %operator.1, bf16[192,384]{1,0:T(8,128)(2,1)} %bitcast.22), custom_call_target="tpu_custom_call" | custom-call | flops 301989888 | bytes 1048576 | tf_op jit(solution)/shard_map/pallas_call | solution.py:483
  17.6 0.8 %shard_map.108 = (f32[4,32,128]{2,1,0:T(8,128)S(1)}, f32[2,32,128]{2,1,0:T(8,128)S(1)}, f32[3,32,128]{2,1,0:T(8,128)S(1)}, f32[8,128]{1,0:T(8,128)S(1)}, f32[3,8...) custom-call(f32[768,128]{1,0:T(8,128)S(1)} %get-tuple-element.37.tra, ...), custom_call_target="tpu_custom_call" | custom-call | flops 226492416 | bytes 1048576 | tf_op jit(solution)/shard_map/pallas_call | solution.py:483
  18.4 0.0 copy-start.1
  18.4 0.6 %collective-permute-start.5 = (f32[136,128]{1,0:T(8,128)S(1)}, f32[136,128]{1,0:T(8,128)S(1)}, u32[]{:S(2)}, u32[]{:S(2)}) collective-permute-start(f32[136,128]{1,0:T(8,128)S(1)} %get-tuple-element.49.refs_0_), channel_id=1, source_target_pairs={{0,16},{16,0},{1,17},{17,1},{2,18},{18,2},{3,19},{19,3},{4,20},{20... | collective-permute-start | bytes 208904 | tf_op jit(solution)/shard_map/ppermute | solution.py:28
  19.0 2.0 %collective-permute-start.6 = (f32[72,128]{1,0:T(8,128)S(1)}, f32[72,128]{1,0:T(8,128)S(1)}, u32[]{:S(2)}, u32[]{:S(2)}) collective-permute-start(f32[72,128]{1,0:T(8,128)S(1)} %get-tuple-element.50.refs_1_), channel_id=1, source_target_pairs={{0,4},{4,0},{8,12},{12,8},{1,5},{5,1},{9,13},{13,9},{2,6},{6,2},{1... | collective-permute-start | bytes 110600 | tf_op jit(solution)/shard_map/ppermute | solution.py:28
  21.0 0.7 %collective-permute-start.7 = (f32[72,128]{1,0:T(8,128)S(1)}, f32[72,128]{1,0:T(8,128)S(1)}, u32[]{:S(2)}, u32[]{:S(2)}) collective-permute-start(f32[72,128]{1,0:T(8,128)S(1)} %get-tuple-element.51.refs_2_), channel_id=1, source_target_pairs={{4,8},{8,4},{5,9},{9,5},{6,10},{10,6},{7,11},{11,7},{20,24},{24,20... | collective-permute-start | bytes 110600 | tf_op jit(solution)/shard_map/ppermute | solution.py:28
  21.7 1.3 %collective-permute-done.6.refs_4_ = f32[72,128]{1,0:T(8,128)S(1)} collective-permute-done((f32[72,128]{1,0:T(8,128)S(1)}, f32[72,128]{1,0:T(8,128)S(1)}, u32[]{:S(2)}, u32[]{:S(2)}) %collective-permute-start.6) | collective-permute-done | bytes 36896 | tf_op jit(solution)/shard_map/ppermute | solution.py:28
  22.9 0.9 %shard_map.109 = (f32[3,8,32,128]{3,2,1,0:T(8,128)S(1)}, f32[32,128]{1,0:T(8,128)S(1)}, f32[4,32,128]{2,1,0:T(8,128)S(1)}, f32[2,32,128]{2,1,0:T(8,128)S(1)}, f3...) custom-call(f32[3,8,32,128]{3,2,1,0:T(8,128)S(1)} %get-tuple-element, ...), custom_call_target="tpu_custom_call" | custom-call | flops 226492416 | bytes 1048576 | tf_op jit(solution)/shard_map/pallas_call | solution.py:483
  23.8 1.6 %collective-permute-start.8 = (f32[128,128]{1,0:T(8,128)S(1)}, f32[128,128]{1,0:T(8,128)S(1)}, u32[]{:S(2)}, u32[]{:S(2)}) collective-permute-start(f32[128,128]{1,0:T(8,128)S(1)} %get-tuple-element.59.refs_0_), channel_id=1, source_target_pairs={{0,16},{16,0},{1,17},{17,1},{2,18},{18,2},{3,19},{19,3},{4,20},{20... | collective-permute-start | bytes 196616 | tf_op jit(solution)/shard_map/ppermute | solution.py:28
  25.4 3.9 %collective-permute-start.9 = (f32[64,128]{1,0:T(8,128)S(1)}, f32[64,128]{1,0:T(8,128)S(1)}, u32[]{:S(2)}, u32[]{:S(2)}) collective-permute-start(f32[64,128]{1,0:T(8,128)S(1)} %get-tuple-element.60.refs_1_), channel_id=1, source_target_pairs={{0,4},{4,0},{8,12},{12,8},{1,5},{5,1},{9,13},{13,9},{2,6},{6,2},{1... | collective-permute-start | bytes 98312 | tf_op jit(solution)/shard_map/ppermute | solution.py:28
  29.3 0.7 %collective-permute-start.10 = (f32[64,128]{1,0:T(8,128)S(1)}, f32[64,128]{1,0:T(8,128)S(1)}, u32[]{:S(2)}, u32[]{:S(2)}) collective-permute-start(f32[64,128]{1,0:T(8,128)S(1)} %get-tuple-element.61.refs_2_), channel_id=1, source_target_pairs={{4,8},{8,4},{5,9},{9,5},{6,10},{10,6},{7,11},{11,7},{20,24},{24,20... | collective-permute-start | bytes 98312 | tf_op jit(solution)/shard_map/ppermute | solution.py:28
  30.0 1.2 %collective-permute-done.9.refs_4_ = f32[64,128]{1,0:T(8,128)S(1)} collective-permute-done((f32[64,128]{1,0:T(8,128)S(1)}, f32[64,128]{1,0:T(8,128)S(1)}, u32[]{:S(2)}, u32[]{:S(2)}) %collective-permute-start.9) | collective-permute-done | bytes 32800 | tf_op jit(solution)/shard_map/ppermute | solution.py:28
  31.2 1.0 %shard_map.110 = (f32[3,8,32,128]{3,2,1,0:T(8,128)S(1)}, f32[4,32,128]{2,1,0:T(8,128)S(1)}, f32[2,32,128]{2,1,0:T(8,128)S(1)}, f32[32,128]{1,0:T(8,128)S(1)}) custom-call(f32[3,8,32,128]{3,2,1,0:T(8,128)S(1)} %get-tuple-element.52.partial, f32[32,128]{1,0:T(8,128)S(1)} %get-tuple-element.53.image_z.refs_8_, f32[24,128]{1,0:T(8,128)S(1)} %get-tuple-element.47.diag, ...), custom_call_target="tpu_custom_call" | custom-call | flops 226492416 | bytes 1048576 | tf_op jit(solution)/shard_map/pallas_call | solution.py:483
  32.3 12.1 %all_to_all.11 = f32[32,1,128]{2,1,0:T(1,128)S(1)} all-to-all(f32[32,1,128]{2,1,0:T(1,128)S(1)} %bitcast.19), channel_id=1, replica_groups=mesh['gx'=2,'gy'=4,'gz'=4] {'gx','gy','gz'}, dimensions={0} | all-to-all | bytes 32768 | tf_op jit(solution)/shard_map/all_to_all | solution.py:563
  44.3 1.7 %shard_map.111 = (bf16[3072,128]{1,0:T(8,128)(2,1)}, f32[768,128]{1,0:T(8,128)}) custom-call(f32[32,128]{1,0:T(8,128)S(1)} %bitcast.15, f32[768,128]{1,0:T(8,128)S(1)} %bitcast.14, f32[8,384,128]{2,1,0:T(8,128)S(1)} %get-tuple-element.41._.base, s32[8,128]{1,0:T(8,128)S(1)} %bitcast.18, bf16[384,192]{1,0:T(8,128)(2,1)S(1)} %get-tuple-element.63.lift, ...), custom_call_target="tpu_custom_call" | custom-call | flops 150994944 | bytes 1048576 | tf_op jit(solution)/shard_map/pallas_call | solution.py:483
  (11 shorter events, 0.0 us)
Async XLA Ops:
  1.7 10.1 %collective-permute-start = (f32[128,128]{1,0:T(8,128)S(1)}, f32[128,128]{1,0:T(8,128)S(1)}, u32[]{:S(2)}, u32[]{:S(2)}) collective-permute-start(f32[128,128]{1,0:T(8,128)S(1)} %get-tuple-element.42), channel_id=1, source_target_pairs={{0,16},{16,0},{1,17},{17,1},{2,18},{18,2},{3,19},{19,3},{4,20},{20... | collective-permute-start | bytes 196616 | tf_op jit(solution)/shard_map/ppermute | solution.py:28
  4.7 6.6 %collective-permute-start.2 = (f32[64,128]{1,0:T(8,128)S(1)}, f32[64,128]{1,0:T(8,128)S(1)}, u32[]{:S(2)}, u32[]{:S(2)}) collective-permute-start(f32[64,128]{1,0:T(8,128)S(1)} %get-tuple-element.43), channel_id=1, source_target_pairs={{4,8},{8,4},{5,9},{9,5},{6,10},{10,6},{7,11},{11,7},{20,24},{24,20... | collective-permute-start | bytes 98312 | tf_op jit(solution)/shard_map/ppermute | solution.py:28
  5.4 6.4 %collective-permute-start.1 = (f32[64,128]{1,0:T(8,128)S(1)}, f32[64,128]{1,0:T(8,128)S(1)}, u32[]{:S(2)}, u32[]{:S(2)}) collective-permute-start(f32[64,128]{1,0:T(8,128)S(1)} %get-tuple-element.43), channel_id=1, source_target_pairs={{0,4},{4,0},{8,12},{12,8},{1,5},{5,1},{9,13},{13,9},{2,6},{6,2},{1... | collective-permute-start | bytes 98312 | tf_op jit(solution)/shard_map/ppermute | solution.py:28
  11.9 5.6 %collective-permute-start.4 = (f32[120,128]{1,0:T(8,128)S(1)}, f32[120,128]{1,0:T(8,128)S(1)}, u32[]{:S(2)}, u32[]{:S(2)}) collective-permute-start(f32[120,128]{1,0:T(8,128)S(1)} %shard_map.107), channel_id=1, source_target_pairs={{1,2},{2,1},{5,6},{6,5},{9,10},{10,9},{13,14},{14,13},{17,18},{18,... | collective-permute-start | bytes 184328 | tf_op jit(solution)/shard_map/ppermute | solution.py:28
  12.6 5.0 %collective-permute-start.3 = (f32[120,128]{1,0:T(8,128)S(1)}, f32[120,128]{1,0:T(8,128)S(1)}, u32[]{:S(2)}, u32[]{:S(2)}) collective-permute-start(f32[120,128]{1,0:T(8,128)S(1)} %shard_map.107), channel_id=1, source_target_pairs={{0,1},{1,0},{2,3},{3,2},{4,5},{5,4},{6,7},{7,6},{8,9},{9,8},{10,11... | collective-permute-start | bytes 184328 | tf_op jit(solution)/shard_map/ppermute | solution.py:28
  18.4 26.0 %copy-start = (f32[3,32,2,4,128]{4,3,2,1,0:T(4,128)S(1)}, f32[3,32,2,4,128]{4,3,2,1,0:T(4,128)}, u32[]{:S(2)}) copy-start(f32[3,32,2,4,128]{4,3,2,1,0:T(4,128)} %param.10) | copy-start | bytes 1179652
  18.4 25.9 %copy-start.1 = (s32[2,4,128]{2,1,0:T(4,128)S(1)}, s32[2,4,128]{2,1,0:T(4,128)}, u32[]{:S(2)}) copy-start(s32[2,4,128]{2,1,0:T(4,128)} %param.13) | copy-start | bytes 12292
  18.4 4.5 %collective-permute-start.5 = (f32[136,128]{1,0:T(8,128)S(1)}, f32[136,128]{1,0:T(8,128)S(1)}, u32[]{:S(2)}, u32[]{:S(2)}) collective-permute-start(f32[136,128]{1,0:T(8,128)S(1)} %get-tuple-element.49.refs_0_), channel_id=1, source_target_pairs={{0,16},{16,0},{1,17},{17,1},{2,18},{18,2},{3,19},{19,3},{4,20},{20... | collective-permute-start | bytes 208904 | tf_op jit(solution)/shard_map/ppermute | solution.py:28
  19.0 4.0 %collective-permute-start.6 = (f32[72,128]{1,0:T(8,128)S(1)}, f32[72,128]{1,0:T(8,128)S(1)}, u32[]{:S(2)}, u32[]{:S(2)}) collective-permute-start(f32[72,128]{1,0:T(8,128)S(1)} %get-tuple-element.50.refs_1_), channel_id=1, source_target_pairs={{0,4},{4,0},{8,12},{12,8},{1,5},{5,1},{9,13},{13,9},{2,6},{6,2},{1... | collective-permute-start | bytes 110600 | tf_op jit(solution)/shard_map/ppermute | solution.py:28
  21.0 1.9 %collective-permute-start.7 = (f32[72,128]{1,0:T(8,128)S(1)}, f32[72,128]{1,0:T(8,128)S(1)}, u32[]{:S(2)}, u32[]{:S(2)}) collective-permute-start(f32[72,128]{1,0:T(8,128)S(1)} %get-tuple-element.51.refs_2_), channel_id=1, source_target_pairs={{4,8},{8,4},{5,9},{9,5},{6,10},{10,6},{7,11},{11,7},{20,24},{24,20... | collective-permute-start | bytes 110600 | tf_op jit(solution)/shard_map/ppermute | solution.py:28
  23.8 7.4 %collective-permute-start.8 = (f32[128,128]{1,0:T(8,128)S(1)}, f32[128,128]{1,0:T(8,128)S(1)}, u32[]{:S(2)}, u32[]{:S(2)}) collective-permute-start(f32[128,128]{1,0:T(8,128)S(1)} %get-tuple-element.59.refs_0_), channel_id=1, source_target_pairs={{0,16},{16,0},{1,17},{17,1},{2,18},{18,2},{3,19},{19,3},{4,20},{20... | collective-permute-start | bytes 196616 | tf_op jit(solution)/shard_map/ppermute | solution.py:28
  25.4 5.8 %collective-permute-start.9 = (f32[64,128]{1,0:T(8,128)S(1)}, f32[64,128]{1,0:T(8,128)S(1)}, u32[]{:S(2)}, u32[]{:S(2)}) collective-permute-start(f32[64,128]{1,0:T(8,128)S(1)} %get-tuple-element.60.refs_1_), channel_id=1, source_target_pairs={{0,4},{4,0},{8,12},{12,8},{1,5},{5,1},{9,13},{13,9},{2,6},{6,2},{1... | collective-permute-start | bytes 98312 | tf_op jit(solution)/shard_map/ppermute | solution.py:28
  29.3 1.9 %collective-permute-start.10 = (f32[64,128]{1,0:T(8,128)S(1)}, f32[64,128]{1,0:T(8,128)S(1)}, u32[]{:S(2)}, u32[]{:S(2)}) collective-permute-start(f32[64,128]{1,0:T(8,128)S(1)} %get-tuple-element.61.refs_2_), channel_id=1, source_target_pairs={{4,8},{8,4},{5,9},{9,5},{6,10},{10,6},{7,11},{11,7},{20,24},{24,20... | collective-permute-start | bytes 98312 | tf_op jit(solution)/shard_map/ppermute | solution.py:28
